TPU v7x, 32 devices: a whole 2x2x4 slice. The times are simulated.
32 devices in a mesh: mpo: 4 (over y, x), sec: 8 (over z, core).
Axes of the slice: x: 2, y: 2, z: 4, core: 2. Of those that a mesh axis runs over, the one named last changes fastest.
Arguments:
- wavefunction: bfloat16 [8, 256, 256], P('sec'), may hold values from -6 to 6
- left_dims: int32 [8], P('sec'), may hold values from 64 to 256
- right_dims: int32 [8], P('sec'), may hold values from 64 to 256
- left_environment_block: bfloat16 [1280, 256, 256], P(('mpo', 'sec')), may hold values from -0.375 to 0.375
- right_env: bfloat16 [1280, 256, 256], P(('mpo', 'sec')), may hold values from -0.03125 to 0.03125
- task_out: int32 [1280], P(('mpo', 'sec')), may hold values from 0 to 7
- task_in: int32 [1280], P(('mpo', 'sec')), may hold values from 0 to 7
Outputs:
- applied: bfloat16 [8, 256, 256], P('sec', 'mpo')
All inputs are finite; a program needn't handle non-finite values.
Results may differ from a plain program's by a relative error of at most 0.0078.
Values may be sent and summed in bfloat16 or wider, within the bound.
No kernel may reach another device: no remote copies, remote signals or barrier semaphores. Data moves between devices by JAX's collectives and lax.ppermute only.
A program may use at most 128 MiB of HBM per device.

v0:
```python
import jax
import jax.numpy as jnp
from jax import lax
from jax.sharding import PartitionSpec as P


def on_device(
    wavefunction, left_dims, right_dims, left_environment_block, right_env, task_out, task_in
):
    block_rows = wavefunction.shape[1]
    block_cols = wavefunction.shape[2]
    groups = lax.axis_size("mpo")
    quarter = block_rows // groups
    row_ids = lax.broadcasted_iota(jnp.int32, wavefunction.shape, 1)
    col_ids = lax.broadcasted_iota(jnp.int32, wavefunction.shape, 2)
    live_cells = (row_ids < left_dims[:, None, None]) & (col_ids < right_dims[:, None, None])
    masked = jnp.where(live_cells, wavefunction, jnp.zeros_like(wavefunction))
    blocks = lax.all_gather(masked, "sec", axis=0, tiled=True)
    sectors = blocks.shape[0]
    number_of_tasks = task_out.shape[0]
    picked_tasks = jnp.take(blocks, task_in, axis=0)
    middle_tensor = jnp.einsum(
        "xvz,xzy->xvy", left_environment_block, picked_tasks, preferred_element_type=jnp.float32
    ).astype(jnp.bfloat16)
    middle_split = middle_tensor.reshape(number_of_tasks, groups, quarter, block_cols)
    task_product = jnp.einsum(
        "tmrc,tdc->mtrd", middle_split, right_env, preferred_element_type=jnp.float32
    )

    def sector_sums(terms):
        return jax.ops.segment_sum(terms, task_out, num_segments=sectors)

    summed = jax.vmap(sector_sums)(task_product)
    row_sums = lax.psum_scatter(summed, "mpo", scatter_dimension=0, tiled=True)
    own_sum = lax.psum_scatter(row_sums[0], "sec", scatter_dimension=0, tiled=True)
    out_rows = (
        lax.broadcasted_iota(jnp.int32, (1, quarter, block_cols), 1)
        + lax.axis_index("mpo") * quarter
    )
    out_cols = lax.broadcasted_iota(jnp.int32, (1, quarter, block_cols), 2)
    kept_cells = (out_rows < left_dims[:, None, None]) & (out_cols < right_dims[:, None, None])
    return jnp.where(kept_cells, own_sum, jnp.zeros_like(own_sum)).astype(jnp.bfloat16)


def solution(mesh):
    return jax.shard_map(
        on_device,
        mesh=mesh,
        in_specs=(
            P("sec", None, None),
            P("sec"),
            P("sec"),
            P(("mpo", "sec"), None, None),
            P(("mpo", "sec"), None, None),
            P(("mpo", "sec")),
            P(("mpo", "sec")),
        ),
        out_specs=P("sec", "mpo", None),
        check_vma=False,
    )
```

profile of v0, /device:TPU:0, one launch (start us, length us, event | category | flops | bytes accessed | tf_op | source)
XLA Modules:
  0.0 144.9 jit_solution(14078317793506280598)
XLA Ops:
  6.5 0.0 all-gather.2.cloned.1.call-start
  7.8 1.6 %fusion.10 = bf16[1,256,256]{2,1,0:T(8,128)(2,1)} fusion(bf16[1,256,256]{2,1,0:T(8,128)(2,1)} %param.7, s32[]{:T(128)} %bitcast.17, s32[]{:T(128)} %bitcast.15), kind=kLoop, calls=%fused_computation.12 | loop fusion | flops 262144 | bytes 262152 | tf_op jit(solution)/shard_map/jit(_where)/select_n | solution.py:17
  9.4 0.0 all-gather.2.cloned.1.call-update
  9.5 0.0 reduce-scatter.7.cloned.1.call-start
  9.5 0.7 compare_select_fusion
  10.2 0.7 compare_and_fusion
  10.8 23.7 %all-gather.2.cloned.1.call-done = bf16[8,256,256]{2,1,0:T(8,128)(2,1)} async-done(((bf16[1,256,256]{2,1,0:T(8,128)(2,1)}), bf16[8,256,256]{2,1,0:T(8,128)(2,1)}) %all-gather.2.cloned.1.call-update) | async-done | bytes 1048592 | tf_op jit(solution)/shard_map/all_gather | solution.py:18
  34.6 5.9 %gather_fusion = bf16[40,256,256]{2,1,0:T(8,128)(2,1)} fusion(bf16[8,256,256]{2,1,0:T(8,128)(2,1)} %all-gather.2.cloned.1.call-done, s32[1024]{0:T(1024)S(1)} %pad_clamp_fusion), kind=kCustom, calls=%fused_computation | custom fusion | bytes 10485920 | tf_op jit(solution)/shard_map/jit(_take)/gather | solution.py:21
  40.5 5.8 %fusion.5 = bf16[40,256,256]{1,2,0:T(8,128)(2,1)S(1)} fusion(bf16[40,256,256]{2,1,0:T(8,128)(2,1)} %param.10, bf16[40,256,256]{2,1,0:T(8,128)(2,1)} %gather_fusion, pred[40]{0:T(512)(128)(4,1)S(1)} %compare_and_fusion), kind=kOutput, calls=%fused_computation.7 | convolution fusion | flops 1347420160 | bytes 15728680 | tf_op jit(solution)/shard_map/xvz,xzy->xvy/dot_general | solution.py:22
  46.3 0.0 slice-done
  46.3 0.0 slice-done.1
  46.4 0.0 copy-start.1
  46.4 5.6 %fusion = f32[40,4,64,256]{3,2,1,0:T(8,128)} fusion(bf16[40,4,64,256]{3,2,1,0:T(8,128)(2,1)S(1)} %bitcast.20, bf16[40,256,256]{2,1,0:T(8,128)(2,1)S(1)} %bitcast.19), kind=kOutput, calls=%fused_computation.2 | convolution fusion | flops 1342177280 | bytes 20971520 | tf_op jit(solution)/shard_map/tmrc,tdc->mtrd/dot_general | solution.py:26
  51.9 0.2 broadcast_in_dim.28
  52.2 0.0 copy-done.1
  52.2 14.8 %scatter_fusion = f32[4,8,64,256]{3,2,1,0:T(8,128)S(1)} fusion(f32[4,8,64,256]{3,2,1,0:T(8,128)S(1)} %broadcast_in_dim.28, s32[40]{0:T(128)S(1)} %copy-done.1, f32[40,4,64,256]{3,2,1,0:T(8,128)} %fusion), kind=kCustom, calls=%fused_computation.1 | custom fusion | flops 2621440 | bytes 31457440 | tf_op jit(solution)/shard_map/vmap()/scatter-add | solution.py:31
  67.0 0.0 copy-start
  67.0 1.3 copy-done
  68.4 0.0 reduce-scatter.7.cloned.1.call-update
  68.4 0.0 reduce-scatter.5.cloned.1.call-start
  68.4 34.8 %reduce-scatter.7.cloned.1.call-done = f32[1,8,64,256]{3,2,1,0:T(8,128)} async-done(((f32[4,8,64,256]{3,2,1,0:T(8,128)}), f32[1,8,64,256]{3,2,1,0:T(8,128)}) %reduce-scatter.7.cloned.1.call-update) | async-done | bytes 524304
  103.2 0.0 reduce-scatter.5.cloned.1.call-update
  103.3 33.6 %reduce-scatter.5.cloned.1.call-done = f32[1,64,256]{2,1,0:T(8,128)} async-done(((f32[8,64,256]{2,1,0:T(8,128)}), f32[1,64,256]{2,1,0:T(8,128)}) %reduce-scatter.5.cloned.1.call-update) | async-done | bytes 65552 | tf_op jit(solution)/shard_map/reduce_scatter | solution.py:35
  136.8 1.5 %select_convert_fusion = bf16[1,64,256]{2,1,0:T(8,128)(2,1)} fusion(f32[1,64,256]{2,1,0:T(8,128)} %reduce-scatter.5.cloned.1.call-done, s32[]{:T(128)} %bitcast.16, pred[64]{0:T(512)(128)(4,1)S(1)} %add_compare_fusion), kind=kLoop, calls=%fused_computation.13 | loop fusion | flops 49152 | bytes 98372 | tf_op jit(solution)/shard_map/convert_element_type | solution.py:42
  (5 shorter events, 0.0 us)
Async XLA Ops:
  6.5 28.0 %all-gather.2.cloned.1.call-start = ((), (), s32[]{:S(2)}) async-start(), calls=%async_computation.2 | async-start | bytes 1179648 | tf_op jit(solution)/shard_map/all_gather | solution.py:18
  9.5 93.8 %reduce-scatter.7.cloned.1.call-start = ((), (), s32[]{:S(2)}) async-start(), calls=%async_computation.4 | async-start | bytes 2621440
  34.6 11.8 %slice-start = ((s8[5242880]{0:T(1024)(128)(4,1)}), s8[1048576]{0:T(1024)(128)(4,1)S(1)}, s32[]{:S(2)}) async-start(s8[5242880]{0:T(1024)(128)(4,1)} %bitcast.18), calls=%async_computation.5 | async-start | bytes 2097152
  40.5 5.9 %slice-start.1 = ((s8[5242880]{0:T(1024)(128)(4,1)}), s8[4194304]{0:T(1024)(128)(4,1)S(1)}, s32[]{:S(2)}) async-start(s8[5242880]{0:T(1024)(128)(4,1)} %bitcast.18), calls=%async_computation.6 | async-start | bytes 8388608
  46.4 5.8 %copy-start.1 = (s32[40]{0:T(128)S(1)}, s32[40]{0:T(128)}, u32[]{:S(2)}) copy-start(s32[40]{0:T(128)} %param.12) | copy-start | bytes 484
  67.0 1.4 copy-start
  68.4 68.4 %reduce-scatter.5.cloned.1.call-start = ((), (), s32[]{:S(2)}) async-start(), calls=%async_computation.3 | async-start | bytes 589824 | tf_op jit(solution)/shard_map/reduce_scatter | solution.py:35
Sparse Core Ops, SparseCore 0:
  9.6 24.9 all-gather.1
  68.5 34.6 reduce-scatter.6
  105.5 31.2 reduce-scatter.4
where the time goes:
time: 145 us
  waiting for transfers between devices  92.1 us (64%)
  other arithmetic  19.3 us (13%)
  between operations  14.5 us (10%)
  matrix products  11.4 us (8%)
  local copies, waits for them, and re-layouts  7.49 us (5%)
    unnamed x4, waiting for transfers between devices  34.8 us
    reduce_scatter x1, waiting for transfers between devices, on_device(): lax.psum_scatter(row_sums[0], 'sec', scatter_dimension=0, tiled=True)  33.6 us
    all_gather x1, waiting for transfers between devices, on_device(): blocks = lax.all_gather(masked, 'sec', axis=0, tiled=True)  23.7 us
    scatter-add x1, other arithmetic, sector_sums(): return jax.ops.segment_sum(terms, task_out, num_segments=sectors)  14.8 us
    gather x1, local copies, waits for them, and re-layouts, on_device(): picked_tasks = jnp.take(blocks, task_in, axis=0)  5.9 us
    dot_general x1, matrix products, on_device(): jnp.einsum('xvz,xzy->xvy', left_environment_block, picked_tasks, preferre...  5.84 us
    dot_general x1, matrix products, on_device(): jnp.einsum('tmrc,tdc->mtrd', middle_split, right_env, preferred_element_t...  5.56 us
  transfers between devices with their start and end apart: 3, of which 3 were waited for; matrix products, arithmetic and copies ran while one was open for 1% of the time, Pallas kernels for 0%

commit v1 on v0

v1 whole, which is shorter than its diff:
```python
import functools

import jax
import jax.numpy as jnp
from jax import lax
from jax.experimental import pallas as pl
from jax.experimental.pallas import tpu as pltpu
from jax.sharding import PartitionSpec as P

CORES = 2
VMEM = pltpu.VMEM
SMEM = pltpu.SMEM


def shift(value, axis, distance, stride=1):
    size = lax.axis_size(axis)
    ring = size // stride
    pairs = [(i, (i // stride + distance) % ring * stride + i % stride) for i in range(size)]
    return lax.ppermute(value, axis, pairs)


def swap(value):
    return lax.ppermute(value, "sec", [(i, i ^ 1) for i in range(lax.axis_size("sec"))])


def contract(groups, depth, chunk, *refs):
    task_in, task_out, own, near = refs[:4]
    mine, theirs = refs[4 : 4 + groups], refs[4 + groups : 4 + 2 * groups]
    left, right, send, keep, blocks, acc, left_buf, right_buf, sems = refs[4 + 2 * groups :]
    tasks = left.shape[0]
    size = own.shape[1]
    quarter = size // groups
    chunks = tasks // chunk

    def fetch(n, which):
        source, target = ((left, left_buf), (right, right_buf))[which]
        span = pl.ds(n * chunk, chunk)
        return pltpu.make_async_copy(source.at[span], target.at[span], sems.at[which, n])

    for n in range(chunks):
        fetch(n, 0).start()
        fetch(n, 1).start()

    sec = lax.axis_index("sec")
    layer, core = sec // CORES, sec % CORES
    group = lax.axis_index("mpo")
    blocks[sec] = own[0]
    blocks[sec + 1 - 2 * core] = near[0]

    def place(k, _):
        base = lax.rem(layer + depth - 1 - k, depth) * CORES
        for j in range(groups):
            rows = pl.ds(pl.multiple_of(lax.rem(group + groups - j, groups) * quarter, quarter), quarter)
            blocks[base + core, rows] = mine[j][k]
            blocks[base + 1 - core, rows] = theirs[j][k]
        return 0

    lax.fori_loop(0, depth - 1, place, 0)
    acc[...] = jnp.zeros_like(acc)

    def step(n, _):
        fetch(n, 0).wait()
        fetch(n, 1).wait()
        for u in range(chunk):
            t = n * chunk + u
            middle = jnp.dot(
                left_buf[t], blocks[task_in[t]], preferred_element_type=jnp.float32
            ).astype(jnp.bfloat16)
            acc[task_out[t]] += lax.dot_general(
                middle, right_buf[t], (((1,), (1,)), ((), ())), preferred_element_type=jnp.float32
            )
        return 0

    lax.fori_loop(0, chunks, step, 0)

    def put(k, _):
        base = lax.rem(layer + k, depth) * CORES
        for j in range(groups):
            rows = pl.ds(pl.multiple_of(lax.rem(group + j, groups) * quarter, quarter), quarter)
            keep[j, k] = acc[base + core, rows]
            send[j, k] = acc[base + 1 - core, rows].astype(send.dtype)
        return 0

    lax.fori_loop(0, depth, put, 0)


def merge_cores(groups, keep, got, total, *sends):
    total[...] = keep[0] + got[0].astype(jnp.float32)
    for j in range(1, groups):
        sends[j - 1][...] = (keep[j] + got[j].astype(jnp.float32)).astype(jnp.bfloat16)


def merge_groups(groups, depth, *refs):
    keep, gots = refs[0], refs[1:groups]
    total, sends = refs[groups], refs[groups + 1 :]
    for k in range(depth):
        value = keep[k]
        for got in gots:
            value += got[k].astype(jnp.float32)
        if k == 0:
            total[...] = value
        else:
            sends[k - 1][...] = value.astype(jnp.bfloat16)


def whole_in_vmem(count):
    return [pl.BlockSpec(memory_space=VMEM)] * count


def on_device(
    wavefunction, left_dims, right_dims, left_environment_block, right_env, task_out, task_in
):
    rows, cols = wavefunction.shape[1:]
    groups = lax.axis_size("mpo")
    sectors = lax.axis_size("sec")
    depth = sectors // CORES
    quarter = rows // groups
    tasks = task_out.shape[0]
    group = lax.axis_index("mpo")
    bf16, f32 = jnp.bfloat16, jnp.float32

    def live(shape, first_row):
        row_ids = lax.broadcasted_iota(jnp.int32, shape, 1) + first_row
        col_ids = lax.broadcasted_iota(jnp.int32, shape, 2)
        return (row_ids < left_dims[:, None, None]) & (col_ids < right_dims[:, None, None])

    part = lax.dynamic_slice_in_dim(wavefunction, group * quarter, quarter, axis=1)
    part = jnp.where(live(part.shape, group * quarter), part, jnp.zeros_like(part))
    layers = [shift(part, "sec", k, CORES) for k in range(1, depth)]
    own = jnp.where(live(wavefunction.shape, 0), wavefunction, jnp.zeros_like(wavefunction))
    near = swap(own)
    mine = [jnp.concatenate(layers, axis=0)]
    mine += [shift(mine[0], "mpo", j) for j in range(1, groups)]
    theirs = [swap(piece) for piece in mine]

    chunk = 4 if tasks % 4 == 0 else 1
    send, keep = pl.pallas_call(
        functools.partial(contract, groups, depth, chunk),
        out_shape=(
            jax.ShapeDtypeStruct((groups, depth, quarter, cols), bf16),
            jax.ShapeDtypeStruct((groups, depth, quarter, cols), f32),
        ),
        in_specs=[pl.BlockSpec(memory_space=SMEM)] * 2
        + whole_in_vmem(2 + 2 * groups)
        + [pl.BlockSpec(memory_space=pl.ANY)] * 2,
        out_specs=tuple(whole_in_vmem(2)),
        scratch_shapes=[
            VMEM((sectors, rows, cols), bf16),
            VMEM((sectors, rows, cols), f32),
            VMEM(left_environment_block.shape, bf16),
            VMEM(right_env.shape, bf16),
            pltpu.SemaphoreType.DMA((2, tasks // chunk)),
        ],
        cost_estimate=pl.CostEstimate(
            flops=4 * tasks * rows * cols * rows,
            bytes_accessed=4 * tasks * rows * cols,
            transcendentals=0,
        ),
        name="contract",
    )(task_in, task_out, own, near, *mine, *theirs, left_environment_block, right_env)

    got = swap(send)
    total, *sends = pl.pallas_call(
        functools.partial(merge_cores, groups),
        out_shape=(jax.ShapeDtypeStruct((depth, quarter, cols), f32),)
        + (jax.ShapeDtypeStruct((depth, quarter, cols), bf16),) * (groups - 1),
        in_specs=whole_in_vmem(2),
        out_specs=tuple(whole_in_vmem(groups)),
        name="merge_cores",
    )(keep, got)
    gots = [shift(piece, "mpo", j + 1) for j, piece in enumerate(sends)]
    total, *sends = pl.pallas_call(
        functools.partial(merge_groups, groups, depth),
        out_shape=(jax.ShapeDtypeStruct((quarter, cols), f32),)
        + (jax.ShapeDtypeStruct((quarter, cols), bf16),) * (depth - 1),
        in_specs=whole_in_vmem(groups),
        out_specs=tuple(whole_in_vmem(depth)),
        name="merge_groups",
    )(total, *gots)
    for k, piece in enumerate(sends):
        total = total + shift(piece, "sec", k + 1, CORES).astype(f32)
    total = total[None]
    return jnp.where(live(total.shape, group * quarter), total, jnp.zeros_like(total)).astype(bf16)


def solution(mesh):
    return jax.shard_map(
        on_device,
        mesh=mesh,
        in_specs=(
            P("sec", None, None),
            P("sec"),
            P("sec"),
            P(("mpo", "sec"), None, None),
            P(("mpo", "sec"), None, None),
            P(("mpo", "sec")),
            P(("mpo", "sec")),
        ),
        out_specs=P("sec", "mpo", None),
        check_vma=False,
    )
```

time: 145 us -> 58.2 us (0.40)
  waiting for transfers between devices: 92.1 us -> 18.4 us
  starting transfers between devices: 0.09 us -> 19 us
  other arithmetic: 19.3 us -> 3.34 us
  Pallas kernels: 0 us -> 13.5 us
  between operations: 14.5 us -> 1.49 us
  matrix products: 11.4 us -> 0 us
  local copies, waits for them, and re-layouts: 7.49 us -> 2.12 us
    unnamed x4 -> x0, waiting for transfers between devices: 34.8 us -> none
    reduce_scatter x1 -> x0, waiting for transfers between devices: 33.6 us -> none  [on_device(): lax.psum_scatter(row_sums[0], 'sec', scatter_dimension=0, tiled=True)]
    all_gather x1 -> x0, waiting for transfers between devices: 23.7 us -> none  [on_device(): blocks = lax.all_gather(masked, 'sec', axis=0, tiled=True)]
    ppermute x0 -> x18, starting transfers between devices: none -> 19 us  [the longest x12 18.2 us: shift(): return lax.ppermute(value, axis, pairs)]
    ppermute x0 -> x18, waiting for transfers between devices: none -> 18.4 us  [the longest x12 15.2 us: shift(): return lax.ppermute(value, axis, pairs)]
    scatter-add x1 -> x0, other arithmetic: 14.8 us -> none  [sector_sums(): return jax.ops.segment_sum(terms, task_out, num_segments=sectors)]
    pallas_call x0 -> x3, Pallas kernels: none -> 13.5 us  [the longest x1 9.45 us: on_device(): pl.pallas_call(functools.partial(contract, groups, depth, chunk), out_sha...]
    dot_general x2 -> x0, matrix products: 11.4 us -> none  [the longest x1 5.84 us: on_device(): jnp.einsum('xvz,xzy->xvy', left_environment_block, picked_tasks, preferre...]
  transfers between devices with their start and end apart: 3 -> 18, of which waited for: 3 -> 11; matrix products, arithmetic and copies ran while one was open for 1% -> 2% of each run, Pallas kernels for 0% -> 0%
where the time goes in v1:
time: 58.2 us; the launch traced here: 57.8 us
  starting transfers between devices  19 us (33%)
  waiting for transfers between devices  18.4 us (32%)
  Pallas kernels  13.5 us (23%)
  other arithmetic  3.34 us (6%)
  local copies, waits for them, and re-layouts  2.12 us (4%)
  between operations  1.49 us (3%)
    ppermute x12, starting transfers between devices, shift(): return lax.ppermute(value, axis, pairs)  18.2 us
    ppermute x12, waiting for transfers between devices, shift(): return lax.ppermute(value, axis, pairs)  15.2 us
    pallas_call x1, Pallas kernels, on_device(): pl.pallas_call(functools.partial(contract, groups, depth, chunk), out_sha...  9.45 us
    ppermute x6, waiting for transfers between devices, swap(): lax.ppermute(value, 'sec', [(i, i ^ 1) for i in range(lax.axis_size('sec'...  3.21 us
    pallas_call x1, Pallas kernels, on_device(): pl.pallas_call(functools.partial(merge_cores, groups), out_shape=(jax.Sha...  2.21 us
    unnamed x30, local copies, waits for them, and re-layouts  2.11 us
    pallas_call x1, Pallas kernels, on_device(): pl.pallas_call(functools.partial(merge_groups, groups, depth), out_shape=...  1.79 us
    convert_element_type x1, other arithmetic, on_device(): jnp.where(live(total.shape, group * quarter), total, jnp.zeros_like(total))  1.54 us
  transfers between devices with their start and end apart: 18, of which 11 were waited for; matrix products, arithmetic and copies ran while one was open for 2% of the time, Pallas kernels for 0%

profile of v1, /device:TPU:0, one launch (start us, length us, event | category | flops | bytes accessed | tf_op | source)
XLA Modules:
  0.0 57.8 jit_solution(17999687911685010813)
XLA Ops:
  1.3 0.8 %fusion.4 = bf16[1,64,256]{2,1,0:T(8,128)(2,1)S(1)} fusion(bf16[1,256,256]{2,1,0:T(8,128)(2,1)} %param.7, s32[]{:T(128)S(6)} %select_n.17, s32[]{:T(128)} %bitcast.8, pred[64]{0:T(512)(128)(4,1)S(1)} %add_compare_fusion), kind=kLoop, calls=%fused_computation.9 | loop fusion | flops 49152 | bytes 65608 | tf_op jit(solution)/shard_map/jit(_where)/select_n | solution.py:128
  2.2 3.1 %collective-permute-start.1 = (bf16[1,64,256]{2,1,0:T(8,128)(2,1)S(1)}, bf16[1,64,256]{2,1,0:T(8,128)(2,1)S(1)}, u32[]{:S(2)}, u32[]{:S(2)}) collective-permute-start(bf16[1,64,256]{2,1,0:T(8,128)(2,1)S(1)} %fusion.4), channel_id=1, source_target_pairs={{0,2},{1,3},{2,4},{3,5},{4,6},{5,7},{6,0},{7,1},{8,10},{9,11},{10,... | collective-permute-start | bytes 98312 | tf_op jit(solution)/shard_map/ppermute | solution.py:19
  5.3 2.1 %collective-permute-start.3 = (bf16[1,64,256]{2,1,0:T(8,128)(2,1)S(1)}, bf16[1,64,256]{2,1,0:T(8,128)(2,1)S(1)}, u32[]{:S(2)}, u32[]{:S(2)}) collective-permute-start(bf16[1,64,256]{2,1,0:T(8,128)(2,1)S(1)} %fusion.4), channel_id=1, source_target_pairs={{0,6},{1,7},{2,0},{3,1},{4,2},{5,3},{6,4},{7,5},{8,14},{9,15},{10,... | collective-permute-start | bytes 98312 | tf_op jit(solution)/shard_map/ppermute | solution.py:19
  7.4 0.9 %collective-permute-start.2 = (bf16[1,64,256]{2,1,0:T(8,128)(2,1)S(1)}, bf16[1,64,256]{2,1,0:T(8,128)(2,1)S(1)}, u32[]{:S(2)}, u32[]{:S(2)}) collective-permute-start(bf16[1,64,256]{2,1,0:T(8,128)(2,1)S(1)} %fusion.4), channel_id=1, source_target_pairs={{0,4},{1,5},{2,6},{3,7},{4,0},{5,1},{6,2},{7,3},{8,12},{9,13},{10,... | collective-permute-start | bytes 98312 | tf_op jit(solution)/shard_map/ppermute | solution.py:19
  8.3 1.0 %collective-permute-done.1 = bf16[1,64,256]{2,1,0:T(8,128)(2,1)S(1)} collective-permute-done((bf16[1,64,256]{2,1,0:T(8,128)(2,1)S(1)}, bf16[1,64,256]{2,1,0:T(8,128)(2,1)S(1)}, u32[]{:S(2)}, u32[]{:S(2)}) %collective-permute-start.1) | collective-permute-done | bytes 32800 | tf_op jit(solution)/shard_map/ppermute | solution.py:19
  9.3 2.9 %collective-permute-done.2 = bf16[1,64,256]{2,1,0:T(8,128)(2,1)S(1)} collective-permute-done((bf16[1,64,256]{2,1,0:T(8,128)(2,1)S(1)}, bf16[1,64,256]{2,1,0:T(8,128)(2,1)S(1)}, u32[]{:S(2)}, u32[]{:S(2)}) %collective-permute-start.2) | collective-permute-done | bytes 32800 | tf_op jit(solution)/shard_map/ppermute | solution.py:19
  12.2 2.7 %collective-permute-start.6 = (bf16[3,64,256]{2,1,0:T(8,128)(2,1)S(1)}, bf16[3,64,256]{2,1,0:T(8,128)(2,1)S(1)}, u32[]{:S(2)}, u32[]{:S(2)}) collective-permute-start(bf16[3,64,256]{2,1,0:T(8,128)(2,1)S(1)} %constant_dynamic-update-slice_fusion.refs_4_), channel_id=1, source_target_pairs={{0,24},{8,0},{16,8},{24,16},{1,25},{9,1},{17,9},{25,17},{2,26},{10... | collective-permute-start | bytes 294920 | tf_op jit(solution)/shard_map/ppermute | solution.py:19
  15.9 1.0 %fusion.1.refs_2_ = bf16[1,256,256]{2,1,0:T(8,128)(2,1)S(1)} fusion(bf16[1,256,256]{2,1,0:T(8,128)(2,1)} %param.7, s32[]{:T(128)} %bitcast.7, s32[]{:T(128)} %bitcast.5), kind=kLoop, calls=%fused_computation.3 | loop fusion | flops 262144 | bytes 262152 | tf_op jit(solution)/shard_map/jit(_where)/select_n | solution.py:130
  17.6 1.9 %collective-permute-done.5.refs_6_ = bf16[3,64,256]{2,1,0:T(8,128)(2,1)S(1)} collective-permute-done((bf16[3,64,256]{2,1,0:T(8,128)(2,1)S(1)}, bf16[3,64,256]{2,1,0:T(8,128)(2,1)S(1)}, u32[]{:S(2)}, u32[]{:S(2)}) %collective-permute-start.5) | collective-permute-done | bytes 98336 | tf_op jit(solution)/shard_map/ppermute | solution.py:19
  19.5 1.4 %collective-permute-done.4.refs_5_ = bf16[3,64,256]{2,1,0:T(8,128)(2,1)S(1)} collective-permute-done((bf16[3,64,256]{2,1,0:T(8,128)(2,1)S(1)}, bf16[3,64,256]{2,1,0:T(8,128)(2,1)S(1)}, u32[]{:S(2)}, u32[]{:S(2)}) %collective-permute-start.4) | collective-permute-done | bytes 98336 | tf_op jit(solution)/shard_map/ppermute | solution.py:19
  21.0 1.2 %collective-permute-done.8.refs_9_ = bf16[3,64,256]{2,1,0:T(8,128)(2,1)S(1)} collective-permute-done((bf16[3,64,256]{2,1,0:T(8,128)(2,1)S(1)}, bf16[3,64,256]{2,1,0:T(8,128)(2,1)S(1)}, u32[]{:S(2)}, u32[]{:S(2)}) %collective-permute-start.8) | collective-permute-done | bytes 98336 | tf_op jit(solution)/shard_map/ppermute | solution.py:23
  22.9 9.5 %contract.1 = (bf16[4,4,64,256]{3,2,1,0:T(8,128)(2,1)}, f32[4,4,64,256]{3,2,1,0:T(8,128)}) custom-call(s32[40]{0:T(128)} %refs_0_.1, s32[40]{0:T(128)} %refs_1_.1, bf16[1,256,256]{2,1,0:T(8,128)(2,1)} %copy-done, bf16[1,256,256]{2,1,0:T(8,128)(2,1)} %copy-done.3, bf16[3,64,256]{2,1,0:T(8,128)(2,1)} %copy-done.2, bf16[3,64,256]{2,1,0:T(8,128)(2,1)} %copy-done.9, ...), custom_call_target="tpu_custom_call" | custom-call | flops 2684354560 | bytes 10485760 | tf_op jit(solution)/shard_map/contract/pallas_call | solution.py:137
  32.6 2.0 %collective-permute-done.11.got = bf16[4,4,64,256]{3,2,1,0:T(8,128)(2,1)S(1)} collective-permute-done((bf16[4,4,64,256]{3,2,1,0:T(8,128)(2,1)}, bf16[4,4,64,256]{3,2,1,0:T(8,128)(2,1)S(1)}, u32[]{:S(2)}, u32[]{:S(2)}) %collective-permute-start.11) | collective-permute-done | bytes 524320 | tf_op jit(solution)/shard_map/ppermute | solution.py:23
  35.3 2.2 %merge_cores.1 = (f32[4,64,256]{2,1,0:T(8,128)}, bf16[4,64,256]{2,1,0:T(8,128)(2,1)}, bf16[4,64,256]{2,1,0:T(8,128)(2,1)}, bf16[4,64,256]{2,1,0:T(8,128)(2,1)}) custom-call(f32[4,4,64,256]{3,2,1,0:T(8,128)} %get-tuple-element.15.keep, bf16[4,4,64,256]{3,2,1,0:T(8,128)(2,1)} %copy-done.1), custom_call_target="tpu_custom_call" | custom-call | tf_op jit(solution)/shard_map/merge_cores/pallas_call | solution.py:163
  37.5 1.5 %collective-permute-start.13 = (bf16[4,64,256]{2,1,0:T(8,128)(2,1)}, bf16[4,64,256]{2,1,0:T(8,128)(2,1)S(1)}, u32[]{:S(2)}, u32[]{:S(2)}) collective-permute-start(bf16[4,64,256]{2,1,0:T(8,128)(2,1)} %get-tuple-element.19), channel_id=1, source_target_pairs={{0,16},{8,24},{16,0},{24,8},{1,17},{9,25},{17,1},{25,9},{2,18},{10... | collective-permute-start | bytes 393224 | tf_op jit(solution)/shard_map/ppermute | solution.py:19
  39.1 2.9 %collective-permute-start.14 = (bf16[4,64,256]{2,1,0:T(8,128)(2,1)}, bf16[4,64,256]{2,1,0:T(8,128)(2,1)S(1)}, u32[]{:S(2)}, u32[]{:S(2)}) collective-permute-start(bf16[4,64,256]{2,1,0:T(8,128)(2,1)} %get-tuple-element.20), channel_id=1, source_target_pairs={{0,24},{8,0},{16,8},{24,16},{1,25},{9,1},{17,9},{25,17},{2,26},{10... | collective-permute-start | bytes 393224 | tf_op jit(solution)/shard_map/ppermute | solution.py:19
  42.0 3.1 %collective-permute-done.12.refs_1_ = bf16[4,64,256]{2,1,0:T(8,128)(2,1)S(1)} collective-permute-done((bf16[4,64,256]{2,1,0:T(8,128)(2,1)}, bf16[4,64,256]{2,1,0:T(8,128)(2,1)S(1)}, u32[]{:S(2)}, u32[]{:S(2)}) %collective-permute-start.12) | collective-permute-done | bytes 131104 | tf_op jit(solution)/shard_map/ppermute | solution.py:19
  45.1 1.0 %collective-permute-done.13.refs_2_ = bf16[4,64,256]{2,1,0:T(8,128)(2,1)S(1)} collective-permute-done((bf16[4,64,256]{2,1,0:T(8,128)(2,1)}, bf16[4,64,256]{2,1,0:T(8,128)(2,1)S(1)}, u32[]{:S(2)}, u32[]{:S(2)}) %collective-permute-start.13) | collective-permute-done | bytes 131104 | tf_op jit(solution)/shard_map/ppermute | solution.py:19
  46.1 1.0 %collective-permute-done.14.refs_3_ = bf16[4,64,256]{2,1,0:T(8,128)(2,1)S(1)} collective-permute-done((bf16[4,64,256]{2,1,0:T(8,128)(2,1)}, bf16[4,64,256]{2,1,0:T(8,128)(2,1)S(1)}, u32[]{:S(2)}, u32[]{:S(2)}) %collective-permute-start.14) | collective-permute-done | bytes 131104 | tf_op jit(solution)/shard_map/ppermute | solution.py:19
  47.8 1.8 %merge_groups.1 = (f32[64,256]{1,0:T(8,128)}, bf16[64,256]{1,0:T(8,128)(2,1)}, bf16[64,256]{1,0:T(8,128)(2,1)}, bf16[64,256]{1,0:T(8,128)(2,1)}) custom-call(f32[4,64,256]{2,1,0:T(8,128)} %get-tuple-element.17.refs_0_, bf16[4,64,256]{2,1,0:T(8,128)(2,1)} %copy-done.4, bf16[4,64,256]{2,1,0:T(8,128)(2,1)} %copy-done.5, bf16[4,64,256]{2,1,0:T(8,128)(2,1)} %copy-done.6), custom_call_target="tpu_custom_call" | custom-call | tf_op jit(solution)/shard_map/merge_groups/pallas_call | solution.py:172
  49.6 2.6 %collective-permute-start.16 = (bf16[64,256]{1,0:T(8,128)(2,1)}, bf16[64,256]{1,0:T(8,128)(2,1)S(1)}, u32[]{:S(2)}, u32[]{:S(2)}) collective-permute-start(bf16[64,256]{1,0:T(8,128)(2,1)} %get-tuple-element.23), channel_id=1, source_target_pairs={{0,4},{1,5},{2,6},{3,7},{4,0},{5,1},{6,2},{7,3},{8,12},{9,13},{10,... | collective-permute-start | bytes 98312 | tf_op jit(solution)/shard_map/ppermute | solution.py:19
  52.2 1.2 %collective-permute-start.17 = (bf16[64,256]{1,0:T(8,128)(2,1)}, bf16[64,256]{1,0:T(8,128)(2,1)S(1)}, u32[]{:S(2)}, u32[]{:S(2)}) collective-permute-start(bf16[64,256]{1,0:T(8,128)(2,1)} %get-tuple-element.24), channel_id=1, source_target_pairs={{0,6},{1,7},{2,0},{3,1},{4,2},{5,3},{6,4},{7,5},{8,14},{9,15},{10,... | collective-permute-start | bytes 98312 | tf_op jit(solution)/shard_map/ppermute | solution.py:19
  53.4 2.2 %collective-permute-done.15 = bf16[64,256]{1,0:T(8,128)(2,1)S(1)} collective-permute-done((bf16[64,256]{1,0:T(8,128)(2,1)}, bf16[64,256]{1,0:T(8,128)(2,1)S(1)}, u32[]{:S(2)}, u32[]{:S(2)}) %collective-permute-start.15) | collective-permute-done | bytes 32800 | tf_op jit(solution)/shard_map/ppermute | solution.py:19
  56.3 1.5 %fusion.5 = bf16[1,64,256]{2,1,0:T(8,128)(2,1)} fusion(bf16[64,256]{1,0:T(8,128)(2,1)S(1)} %collective-permute-done.17, bf16[64,256]{1,0:T(8,128)(2,1)S(1)} %collective-permute-done.16, f32[64,256]{1,0:T(8,128)} %get-tuple-element.21, bf16[64,256]{1,0:T(8,128)(2,1)S(1)} %collective-permute-done.15, s32[]{:T(128)} %bitcast.6, pred[64]{0:T(512)(128)(4,1)S(1)} %add_compare_fusion), kind=kLoop, calls=%fused_computation.10 | loop fusion | flops 163840 | bytes 196676 | tf_op jit(solution)/shard_map/convert_element_type | solution.py:183
  (50 shorter events, 4.8 us)
Async XLA Ops:
  2.2 7.1 %collective-permute-start.1 = (bf16[1,64,256]{2,1,0:T(8,128)(2,1)S(1)}, bf16[1,64,256]{2,1,0:T(8,128)(2,1)S(1)}, u32[]{:S(2)}, u32[]{:S(2)}) collective-permute-start(bf16[1,64,256]{2,1,0:T(8,128)(2,1)S(1)} %fusion.4), channel_id=1, source_target_pairs={{0,2},{1,3},{2,4},{3,5},{4,6},{5,7},{6,0},{7,1},{8,10},{9,11},{10,... | collective-permute-start | bytes 98312 | tf_op jit(solution)/shard_map/ppermute | solution.py:19
  5.3 6.9 %collective-permute-start.3 = (bf16[1,64,256]{2,1,0:T(8,128)(2,1)S(1)}, bf16[1,64,256]{2,1,0:T(8,128)(2,1)S(1)}, u32[]{:S(2)}, u32[]{:S(2)}) collective-permute-start(bf16[1,64,256]{2,1,0:T(8,128)(2,1)S(1)} %fusion.4), channel_id=1, source_target_pairs={{0,6},{1,7},{2,0},{3,1},{4,2},{5,3},{6,4},{7,5},{8,14},{9,15},{10,... | collective-permute-start | bytes 98312 | tf_op jit(solution)/shard_map/ppermute | solution.py:19
  7.4 4.8 %collective-permute-start.2 = (bf16[1,64,256]{2,1,0:T(8,128)(2,1)S(1)}, bf16[1,64,256]{2,1,0:T(8,128)(2,1)S(1)}, u32[]{:S(2)}, u32[]{:S(2)}) collective-permute-start(bf16[1,64,256]{2,1,0:T(8,128)(2,1)S(1)} %fusion.4), channel_id=1, source_target_pairs={{0,4},{1,5},{2,6},{3,7},{4,0},{5,1},{6,2},{7,3},{8,12},{9,13},{10,... | collective-permute-start | bytes 98312 | tf_op jit(solution)/shard_map/ppermute | solution.py:19
  12.2 10.0 %copy-start.2 = (bf16[3,64,256]{2,1,0:T(8,128)(2,1)}, bf16[3,64,256]{2,1,0:T(8,128)(2,1)S(1)}, u32[]{:S(2)}) copy-start(bf16[3,64,256]{2,1,0:T(8,128)(2,1)S(1)} %constant_dynamic-update-slice_fusion.refs_4_) | copy-start | bytes 294916
  12.2 5.3 %collective-permute-start.6 = (bf16[3,64,256]{2,1,0:T(8,128)(2,1)S(1)}, bf16[3,64,256]{2,1,0:T(8,128)(2,1)S(1)}, u32[]{:S(2)}, u32[]{:S(2)}) collective-permute-start(bf16[3,64,256]{2,1,0:T(8,128)(2,1)S(1)} %constant_dynamic-update-slice_fusion.refs_4_), channel_id=1, source_target_pairs={{0,24},{8,0},{16,8},{24,16},{1,25},{9,1},{17,9},{25,17},{2,26},{10... | collective-permute-start | bytes 294920 | tf_op jit(solution)/shard_map/ppermute | solution.py:19
  14.8 4.6 %collective-permute-start.5 = (bf16[3,64,256]{2,1,0:T(8,128)(2,1)S(1)}, bf16[3,64,256]{2,1,0:T(8,128)(2,1)S(1)}, u32[]{:S(2)}, u32[]{:S(2)}) collective-permute-start(bf16[3,64,256]{2,1,0:T(8,128)(2,1)S(1)} %constant_dynamic-update-slice_fusion.refs_4_), channel_id=1, source_target_pairs={{0,16},{8,24},{16,0},{24,8},{1,17},{9,25},{17,1},{25,9},{2,18},{10... | collective-permute-start | bytes 294920 | tf_op jit(solution)/shard_map/ppermute | solution.py:19
  15.4 5.5 %collective-permute-start.4 = (bf16[3,64,256]{2,1,0:T(8,128)(2,1)S(1)}, bf16[3,64,256]{2,1,0:T(8,128)(2,1)S(1)}, u32[]{:S(2)}, u32[]{:S(2)}) collective-permute-start(bf16[3,64,256]{2,1,0:T(8,128)(2,1)S(1)} %constant_dynamic-update-slice_fusion.refs_4_), channel_id=1, source_target_pairs={{0,8},{8,16},{16,24},{24,0},{1,9},{9,17},{17,25},{25,1},{2,10},{10... | collective-permute-start | bytes 294920 | tf_op jit(solution)/shard_map/ppermute | solution.py:19
  16.9 5.3 %copy-start = (bf16[1,256,256]{2,1,0:T(8,128)(2,1)}, bf16[1,256,256]{2,1,0:T(8,128)(2,1)S(1)}, u32[]{:S(2)}) copy-start(bf16[1,256,256]{2,1,0:T(8,128)(2,1)S(1)} %fusion.1.refs_2_) | copy-start | bytes 393220
  16.9 4.0 %collective-permute-start = (bf16[1,256,256]{2,1,0:T(8,128)(2,1)S(1)}, bf16[1,256,256]{2,1,0:T(8,128)(2,1)S(1)}, u32[]{:S(2)}, u32[]{:S(2)}) collective-permute-start(bf16[1,256,256]{2,1,0:T(8,128)(2,1)S(1)} %fusion.1.refs_2_), channel_id=1, source_target_pairs={{0,1},{1,0},{2,3},{3,2},{4,5},{5,4},{6,7},{7,6},{8,9},{9,8},{10,11... | collective-permute-start | bytes 393224 | tf_op jit(solution)/shard_map/ppermute | solution.py:23
  17.0 3.9 %collective-permute-start.7 = (bf16[3,64,256]{2,1,0:T(8,128)(2,1)S(1)}, bf16[3,64,256]{2,1,0:T(8,128)(2,1)S(1)}, u32[]{:S(2)}, u32[]{:S(2)}) collective-permute-start(bf16[3,64,256]{2,1,0:T(8,128)(2,1)S(1)} %constant_dynamic-update-slice_fusion.refs_4_), channel_id=1, source_target_pairs={{0,1},{1,0},{2,3},{3,2},{4,5},{5,4},{6,7},{7,6},{8,9},{9,8},{10,11... | collective-permute-start | bytes 294920 | tf_op jit(solution)/shard_map/ppermute | solution.py:23
  17.5 4.7 %copy-start.7 = (bf16[3,64,256]{2,1,0:T(8,128)(2,1)}, bf16[3,64,256]{2,1,0:T(8,128)(2,1)S(1)}, u32[]{:S(2)}) copy-start(bf16[3,64,256]{2,1,0:T(8,128)(2,1)S(1)} %collective-permute-done.6.refs_7_) | copy-start | bytes 294916
  17.5 3.4 %collective-permute-start.10 = (bf16[3,64,256]{2,1,0:T(8,128)(2,1)S(1)}, bf16[3,64,256]{2,1,0:T(8,128)(2,1)S(1)}, u32[]{:S(2)}, u32[]{:S(2)}) collective-permute-start(bf16[3,64,256]{2,1,0:T(8,128)(2,1)S(1)} %collective-permute-done.6.refs_7_), channel_id=1, source_target_pairs={{0,1},{1,0},{2,3},{3,2},{4,5},{5,4},{6,7},{7,6},{8,9},{9,8},{10,11... | collective-permute-start | bytes 294920 | tf_op jit(solution)/shard_map/ppermute | solution.py:23
  19.5 2.7 %copy-start.8 = (bf16[3,64,256]{2,1,0:T(8,128)(2,1)}, bf16[3,64,256]{2,1,0:T(8,128)(2,1)S(1)}, u32[]{:S(2)}) copy-start(bf16[3,64,256]{2,1,0:T(8,128)(2,1)S(1)} %collective-permute-done.5.refs_6_) | copy-start | bytes 294916
  19.5 1.5 %collective-permute-start.9 = (bf16[3,64,256]{2,1,0:T(8,128)(2,1)S(1)}, bf16[3,64,256]{2,1,0:T(8,128)(2,1)S(1)}, u32[]{:S(2)}, u32[]{:S(2)}) collective-permute-start(bf16[3,64,256]{2,1,0:T(8,128)(2,1)S(1)} %collective-permute-done.5.refs_6_), channel_id=1, source_target_pairs={{0,1},{1,0},{2,3},{3,2},{4,5},{5,4},{6,7},{7,6},{8,9},{9,8},{10,11... | collective-permute-start | bytes 294920 | tf_op jit(solution)/shard_map/ppermute | solution.py:23
  20.9 1.3 %copy-start.9 = (bf16[3,64,256]{2,1,0:T(8,128)(2,1)}, bf16[3,64,256]{2,1,0:T(8,128)(2,1)S(1)}, u32[]{:S(2)}) copy-start(bf16[3,64,256]{2,1,0:T(8,128)(2,1)S(1)} %collective-permute-done.4.refs_5_) | copy-start | bytes 294916
  20.9 1.3 %collective-permute-start.8 = (bf16[3,64,256]{2,1,0:T(8,128)(2,1)S(1)}, bf16[3,64,256]{2,1,0:T(8,128)(2,1)S(1)}, u32[]{:S(2)}, u32[]{:S(2)}) collective-permute-start(bf16[3,64,256]{2,1,0:T(8,128)(2,1)S(1)} %collective-permute-done.4.refs_5_), channel_id=1, source_target_pairs={{0,1},{1,0},{2,3},{3,2},{4,5},{5,4},{6,7},{7,6},{8,9},{9,8},{10,11... | collective-permute-start | bytes 294920 | tf_op jit(solution)/shard_map/ppermute | solution.py:23
  32.3 2.2 %collective-permute-start.11 = (bf16[4,4,64,256]{3,2,1,0:T(8,128)(2,1)}, bf16[4,4,64,256]{3,2,1,0:T(8,128)(2,1)S(1)}, u32[]{:S(2)}, u32[]{:S(2)}) collective-permute-start(bf16[4,4,64,256]{3,2,1,0:T(8,128)(2,1)} %get-tuple-element.16), channel_id=1, source_target_pairs={{0,1},{1,0},{2,3},{3,2},{4,5},{5,4},{6,7},{7,6},{8,9},{9,8},{10,11... | collective-permute-start | bytes 1572872 | tf_op jit(solution)/shard_map/ppermute | solution.py:23
  37.5 7.5 %collective-permute-start.12 = (bf16[4,64,256]{2,1,0:T(8,128)(2,1)}, bf16[4,64,256]{2,1,0:T(8,128)(2,1)S(1)}, u32[]{:S(2)}, u32[]{:S(2)}) collective-permute-start(bf16[4,64,256]{2,1,0:T(8,128)(2,1)} %get-tuple-element.18), channel_id=1, source_target_pairs={{0,8},{8,16},{16,24},{24,0},{1,9},{9,17},{17,25},{25,1},{2,10},{10... | collective-permute-start | bytes 393224 | tf_op jit(solution)/shard_map/ppermute | solution.py:19
  37.5 8.6 %collective-permute-start.13 = (bf16[4,64,256]{2,1,0:T(8,128)(2,1)}, bf16[4,64,256]{2,1,0:T(8,128)(2,1)S(1)}, u32[]{:S(2)}, u32[]{:S(2)}) collective-permute-start(bf16[4,64,256]{2,1,0:T(8,128)(2,1)} %get-tuple-element.19), channel_id=1, source_target_pairs={{0,16},{8,24},{16,0},{24,8},{1,17},{9,25},{17,1},{25,9},{2,18},{10... | collective-permute-start | bytes 393224 | tf_op jit(solution)/shard_map/ppermute | solution.py:19
  39.1 8.0 %collective-permute-start.14 = (bf16[4,64,256]{2,1,0:T(8,128)(2,1)}, bf16[4,64,256]{2,1,0:T(8,128)(2,1)S(1)}, u32[]{:S(2)}, u32[]{:S(2)}) collective-permute-start(bf16[4,64,256]{2,1,0:T(8,128)(2,1)} %get-tuple-element.20), channel_id=1, source_target_pairs={{0,24},{8,0},{16,8},{24,16},{1,25},{9,1},{17,9},{25,17},{2,26},{10... | collective-permute-start | bytes 393224 | tf_op jit(solution)/shard_map/ppermute | solution.py:19
  45.1 2.0 %copy-start.4 = (bf16[4,64,256]{2,1,0:T(8,128)(2,1)}, bf16[4,64,256]{2,1,0:T(8,128)(2,1)S(1)}, u32[]{:S(2)}) copy-start(bf16[4,64,256]{2,1,0:T(8,128)(2,1)S(1)} %collective-permute-done.12.refs_1_) | copy-start | bytes 393220
  49.6 6.0 %collective-permute-start.15 = (bf16[64,256]{1,0:T(8,128)(2,1)}, bf16[64,256]{1,0:T(8,128)(2,1)S(1)}, u32[]{:S(2)}, u32[]{:S(2)}) collective-permute-start(bf16[64,256]{1,0:T(8,128)(2,1)} %get-tuple-element.22), channel_id=1, source_target_pairs={{0,2},{1,3},{2,4},{3,5},{4,6},{5,7},{6,0},{7,1},{8,10},{9,11},{10,... | collective-permute-start | bytes 98312 | tf_op jit(solution)/shard_map/ppermute | solution.py:19
  49.6 6.0 %collective-permute-start.16 = (bf16[64,256]{1,0:T(8,128)(2,1)}, bf16[64,256]{1,0:T(8,128)(2,1)S(1)}, u32[]{:S(2)}, u32[]{:S(2)}) collective-permute-start(bf16[64,256]{1,0:T(8,128)(2,1)} %get-tuple-element.23), channel_id=1, source_target_pairs={{0,4},{1,5},{2,6},{3,7},{4,0},{5,1},{6,2},{7,3},{8,12},{9,13},{10,... | collective-permute-start | bytes 98312 | tf_op jit(solution)/shard_map/ppermute | solution.py:19
  52.2 4.1 %collective-permute-start.17 = (bf16[64,256]{1,0:T(8,128)(2,1)}, bf16[64,256]{1,0:T(8,128)(2,1)S(1)}, u32[]{:S(2)}, u32[]{:S(2)}) collective-permute-start(bf16[64,256]{1,0:T(8,128)(2,1)} %get-tuple-element.24), channel_id=1, source_target_pairs={{0,6},{1,7},{2,0},{3,1},{4,2},{5,3},{6,4},{7,5},{8,14},{9,15},{10,... | collective-permute-start | bytes 98312 | tf_op jit(solution)/shard_map/ppermute | solution.py:19
  (8 other events, 8.3 us)

commit v2 on v0

v2 whole, which is shorter than its diff:
```python
import functools
import math

import jax
import jax.numpy as jnp
from jax import lax
from jax.experimental import pallas as pl
from jax.experimental.pallas import tpu as pltpu
from jax.sharding import PartitionSpec as P

CORES = 2
UNROLL = 4
VMEM_BYTES = 67043328
SLACK = 1 << 20
VMEM = pltpu.VMEM
SMEM = pltpu.SMEM
BF16 = jnp.bfloat16
F32 = jnp.float32


def shift(value, axis, distance, stride=1):
    size = lax.axis_size(axis)
    ring = size // stride
    pairs = [(i, (i // stride + distance) % ring * stride + i % stride) for i in range(size)]
    return lax.ppermute(value, axis, pairs)


def swap(value):
    return lax.ppermute(value, "sec", [(i, i ^ 1) for i in range(lax.axis_size("sec"))])


def array(shape, dtype):
    return jax.ShapeDtypeStruct(shape, dtype)


def grant(scratch, *operands):
    mine, others = (sum(math.prod(a.shape) * a.dtype.itemsize for a in group) for group in (scratch, operands))
    return mine + SLACK if 2 * (mine + others) < VMEM_BYTES else min(mine + others + 2 * SLACK, VMEM_BYTES)


def call(kernel, name, out_shape, operands, scratch=(), scalars=0, cost=None, aliases=None, streamed=()):
    one = not isinstance(out_shape, tuple)
    outs = (out_shape,) if one else out_shape
    specs = [pl.BlockSpec(memory_space=SMEM)] * scalars
    specs += [pl.BlockSpec(memory_space=VMEM)] * (len(operands) - scalars)
    for n in streamed:
        specs[n] = pl.BlockSpec(memory_space=pl.ANY)
    results = pl.pallas_call(
        kernel,
        out_shape=outs,
        in_specs=specs,
        out_specs=(pl.BlockSpec(memory_space=VMEM),) * len(outs),
        scratch_shapes=scratch,
        cost_estimate=cost,
        input_output_aliases=aliases or {},
        compiler_params=pltpu.CompilerParams(
            vmem_limit_bytes=grant(
                [s for s in scratch if getattr(s, "memory_space", None) == VMEM], *outs, *operands[scalars:]
            )
        ),
        name=name,
    )(*operands)
    return results[0] if one else results


def clear(acc):
    acc[...] = jnp.zeros_like(acc)


def products(distances, late, task_in, task_out, blocks, left, right, acc, order, middle, *stage):
    tasks = left.shape[0]
    depth = acc.shape[0] // CORES
    layer = lax.axis_index("sec") // CORES
    others = [d for d in range(depth) if d not in distances]
    shorter = min(distances, others, key=len)
    layers = [lax.rem(layer + depth - d, depth) for d in shorter]
    count = jnp.int32(0)
    for t in range(tasks):
        source = lax.div(task_in[t], CORES)
        listed = functools.reduce(jnp.logical_or, [source == it for it in layers])
        order[count] = t
        count += jnp.where(listed, *((1, 0) if late == (shorter is others) else (0, 1)))
    for u in range(2 * UNROLL):
        order[count + u] = tasks

    def task(slot):
        t = order[slot]
        return jnp.where(t < tasks, t, 0), t < tasks

    def fetch(which, t, u):
        source = (left, right)[which]
        if not stage:
            return source[t]
        target, sems = stage
        copy = pltpu.make_async_copy(source.at[t], target.at[which, u], sems.at[which, u])
        copy.start()
        copy.wait()
        return target[which, u]

    def first(n):
        for u in range(UNROLL):
            t, _ = task(n * UNROLL + u)
            product = jnp.dot(fetch(0, t, u), blocks[task_in[t]], preferred_element_type=F32)
            middle[u] = product.astype(BF16)

    def second(n):
        for u in range(UNROLL):
            t, real = task(n * UNROLL + u)
            target = jnp.where(real, task_out[t], acc.shape[0] - 1)
            acc[target] += lax.dot_general(
                middle[u], fetch(1, t, u), (((1,), (1,)), ((), ())), preferred_element_type=F32
            )

    def step(n, _):
        second(n)
        first(n + 1)
        return 0

    first(0)
    lax.fori_loop(0, (count + UNROLL - 1) // UNROLL, step, 0)


def place(blocks, distances, found):
    depth = blocks.shape[0] // CORES
    sec = lax.axis_index("sec")
    layer, core = sec // CORES, sec % CORES
    parts = len(found) // max(1, CORES * len(distances))
    found = iter(found)
    for distance in distances:
        base = lax.rem(layer + depth - distance, depth) * CORES
        for sector in (base + core, base + 1 - core):
            for part in range(parts):
                block = next(found)
                size = block.shape[1]
                blocks[sector, part * size : (part + 1) * size] = block[0]


def contract_early(sources, near, count, task_in, task_out, *refs):
    found, (left, right, _, acc, blocks), rest = refs[:count], refs[count : count + 5], refs[count + 5 :]
    place(blocks, sources, found)
    products(near, False, task_in, task_out, blocks, left, right, acc, *rest)


def contract_late(sources, near, count, task_in, task_out, *refs):
    found, (left, right, _, acc), refs = refs[:count], refs[count : count + 4], refs[count + 4 :]
    groups = lax.axis_size("mpo")
    sends, keeps, (blocks, *rest) = refs[:groups], refs[groups : 2 * groups], refs[2 * groups :]
    if sources:
        place(blocks, sources, found)
        products(near, True, task_in, task_out, blocks, left, right, acc, *rest)
    depth, quarter = sends[0].shape[:2]
    sec = lax.axis_index("sec")
    layer, core = sec // CORES, sec % CORES
    group = lax.axis_index("mpo")

    def put(k, _):
        base = lax.rem(layer + k, depth) * CORES
        for j in range(groups):
            rows = pl.ds(pl.multiple_of(lax.rem(group + j, groups) * quarter, quarter), quarter)
            keeps[j][k] = acc[base + core, rows]
            sends[j][k] = acc[base + 1 - core, rows].astype(BF16)
        return 0

    lax.fori_loop(0, depth, put, 0)


def merge_cores(keep, got, send):
    send[...] = (keep[...] + got[...].astype(F32)).astype(BF16)


def merge_groups(depth, *refs):
    terms, (total, *sends) = refs[:-depth], refs[-depth:]
    for k in range(depth):
        value = functools.reduce(jnp.add, [term[k].astype(F32) for term in terms])
        if k == 0:
            total[...] = value
        else:
            sends[k - 1][...] = value.astype(BF16)


def on_device(
    wavefunction, left_dims, right_dims, left_environment_block, right_env, task_out, task_in
):
    rows, cols = wavefunction.shape[1:]
    groups = lax.axis_size("mpo")
    sectors = lax.axis_size("sec")
    depth = sectors // CORES
    quarter = rows // groups
    tasks = task_out.shape[0]
    group = lax.axis_index("mpo")

    def live(shape, first_row):
        row_ids = lax.broadcasted_iota(jnp.int32, shape, 1) + first_row
        col_ids = lax.broadcasted_iota(jnp.int32, shape, 2)
        return (row_ids < left_dims[:, None, None]) & (col_ids < right_dims[:, None, None])

    own = jnp.where(live(wavefunction.shape, 0), wavefunction, jnp.zeros_like(wavefunction))
    near = sorted({0, 1 % depth, depth - 1})
    far = [d for d in range(depth) if d not in near]
    mine = {d: [shift(own, "sec", d, CORES) if d else own] for d in near}
    half = rows // 2
    for d in far:
        if far == [2]:
            up, down = mine[1][0][:, :half], mine[3][0][:, half:]
            mine[d] = [shift(up, "sec", 1, CORES), shift(down, "sec", 3, CORES)]
        else:
            mine[d] = [shift(own, "sec", d, CORES)]
    found = {d: [*blocks, *(swap(block) for block in blocks)] for d, blocks in mine.items()}

    work = (left_environment_block, right_env)
    cost = pl.CostEstimate(
        flops=4 * tasks * rows * cols * rows, bytes_accessed=4 * tasks * rows * cols, transcendentals=0
    )
    slow = pl.CostEstimate(flops=4 * cost.flops, bytes_accessed=4 * cost.bytes_accessed, transcendentals=0)
    sums = array((sectors + 1, rows, cols), F32)
    acc = call(clear, "clear", sums, (), cost=slow)
    scratch = (
        VMEM((sectors, rows, cols), BF16),
        SMEM((tasks + 2 * UNROLL,), jnp.int32),
        VMEM((UNROLL, rows, cols), BF16),
    )
    streamed = 16 * sums.size > VMEM_BYTES
    if streamed:
        scratch += (VMEM((2, UNROLL, rows, cols), BF16), pltpu.SemaphoreType.DMA((2, UNROLL)))

    def contract(kernel, sources, outs, **options):
        blocks = [b for d in sources for b in found[d]]
        operands = (task_in, task_out, *blocks, *work, acc)
        last = len(operands) - 1
        return call(
            functools.partial(kernel, sources, near, len(blocks)),
            kernel.__name__,
            outs,
            operands,
            scratch,
            scalars=2,
            aliases={last: 0},
            streamed=(last - 2, last - 1) if streamed else (),
            **options,
        )

    acc = contract(contract_early, near, sums, cost=cost)
    piece = (depth, quarter, cols)
    late_outs = (sums, *(array(piece, BF16),) * groups, *(array(piece, F32),) * groups)
    _, *pieces = contract(contract_late, far, late_outs)
    sends, keeps = pieces[:groups], pieces[groups:]

    gots = {}
    for j in [*range(1, groups), 0]:
        got = swap(sends[j])
        if j:
            gots[j] = shift(call(merge_cores, "merge_cores", array(piece, BF16), (keeps[j], got)), "mpo", j)
        else:
            gots[j] = got
    total, *sends = call(
        functools.partial(merge_groups, depth),
        "merge_groups",
        (array(piece[1:], F32), *(array(piece[1:], BF16),) * (depth - 1)),
        (keeps[0], *(gots[j] for j in range(groups))),
    )
    for k, sent in enumerate(sends):
        total = total + shift(sent, "sec", k + 1, CORES).astype(F32)
    total = total[None]
    return jnp.where(live(total.shape, group * quarter), total, jnp.zeros_like(total)).astype(BF16)


def solution(mesh):
    return jax.shard_map(
        on_device,
        mesh=mesh,
        in_specs=(
            P("sec", None, None),
            P("sec"),
            P("sec"),
            P(("mpo", "sec"), None, None),
            P(("mpo", "sec"), None, None),
            P(("mpo", "sec")),
            P(("mpo", "sec")),
        ),
        out_specs=P("sec", "mpo", None),
        check_vma=False,
    )
```

time: 145 us -> 48.2 us (0.33)
  waiting for transfers between devices: 92.1 us -> 16.9 us
  starting transfers between devices: 0.09 us -> 19.8 us
  other arithmetic: 19.3 us -> 1.66 us
  between operations: 14.5 us -> 1.5 us
  matrix products: 11.4 us -> 0 us
  Pallas kernels: 0 us -> 8.16 us
  local copies, waits for them, and re-layouts: 7.49 us -> 0.05 us
    unnamed x4 -> x0, waiting for transfers between devices: 34.8 us -> none
    reduce_scatter x1 -> x0, waiting for transfers between devices: 33.6 us -> none  [on_device(): lax.psum_scatter(row_sums[0], 'sec', scatter_dimension=0, tiled=True)]
    all_gather x1 -> x0, waiting for transfers between devices: 23.7 us -> none  [on_device(): blocks = lax.all_gather(masked, 'sec', axis=0, tiled=True)]
    ppermute x0 -> x19, starting transfers between devices: none -> 19.8 us  [the longest x10 18.1 us: shift(): return lax.ppermute(value, axis, pairs)]
    ppermute x0 -> x19, waiting for transfers between devices: none -> 16.9 us  [the longest x10 16.6 us: shift(): return lax.ppermute(value, axis, pairs)]
    scatter-add x1 -> x0, other arithmetic: 14.8 us -> none  [sector_sums(): return jax.ops.segment_sum(terms, task_out, num_segments=sectors)]
    dot_general x2 -> x0, matrix products: 11.4 us -> none  [the longest x1 5.84 us: on_device(): jnp.einsum('xvz,xzy->xvy', left_environment_block, picked_tasks, preferre...]
    pallas_call x0 -> x7, Pallas kernels: none -> 8.16 us  [call(): pl.pallas_call(kernel, out_shape=outs, in_specs=specs, out_specs=(pl.Bloc...]
  transfers between devices with their start and end apart: 3 -> 19, of which waited for: 3 -> 9; matrix products, arithmetic and copies ran while one was open for 1% -> 0% of each run, Pallas kernels for 0% -> 10%
where the time goes in v2:
time: 48.2 us; the launch traced here: 48 us
  starting transfers between devices  19.8 us (41%)
  waiting for transfers between devices  16.9 us (35%)
  Pallas kernels  8.16 us (17%)
  other arithmetic  1.66 us (3%)
  between operations  1.5 us (3%)
    ppermute x10, starting transfers between devices, shift(): return lax.ppermute(value, axis, pairs)  18.1 us
    ppermute x10, waiting for transfers between devices, shift(): return lax.ppermute(value, axis, pairs)  16.6 us
    pallas_call x7, Pallas kernels, call(): pl.pallas_call(kernel, out_shape=outs, in_specs=specs, out_specs=(pl.Bloc...  8.16 us
    ppermute x9, starting transfers between devices, swap(): lax.ppermute(value, 'sec', [(i, i ^ 1) for i in range(lax.axis_size('sec'...  1.65 us
  transfers between devices with their start and end apart: 19, of which 9 were waited for; matrix products, arithmetic and copies ran while one was open for 0% of the time, Pallas kernels for 10%

profile of v2, /device:TPU:0, one launch (start us, length us, event | category | flops | bytes accessed | tf_op | source)
XLA Modules:
  0.0 48.0 jit_solution(11183485120659051769)
XLA Ops:
  1.3 1.0 %fusion.1.refs_0_ = bf16[1,256,256]{2,1,0:T(8,128)(2,1)S(1)} fusion(bf16[1,256,256]{2,1,0:T(8,128)(2,1)} %param.7, s32[]{:T(128)} %bitcast.7, s32[]{:T(128)} %bitcast.5), kind=kLoop, calls=%fused_computation.3 | loop fusion | flops 262144 | bytes 262152 | tf_op jit(solution)/shard_map/jit(_where)/select_n | solution.py:197
  2.3 5.1 %collective-permute-start.2 = (bf16[1,256,256]{2,1,0:T(8,128)(2,1)S(1)}, bf16[1,256,256]{2,1,0:T(8,128)(2,1)S(1)}, u32[]{:S(2)}, u32[]{:S(2)}) collective-permute-start(bf16[1,256,256]{2,1,0:T(8,128)(2,1)S(1)} %fusion.1.refs_0_), channel_id=1, source_target_pairs={{0,6},{1,7},{2,0},{3,1},{4,2},{5,3},{6,4},{7,5},{8,14},{9,15},{10,... | collective-permute-start | bytes 393224 | tf_op jit(solution)/shard_map/ppermute | solution.py:25
  7.4 3.9 %collective-permute-done.2.refs_4_ = bf16[1,256,256]{2,1,0:T(8,128)(2,1)S(1)} collective-permute-done((bf16[1,256,256]{2,1,0:T(8,128)(2,1)S(1)}, bf16[1,256,256]{2,1,0:T(8,128)(2,1)S(1)}, u32[]{:S(2)}, u32[]{:S(2)}) %collective-permute-start.2) | collective-permute-done | bytes 131104 | tf_op jit(solution)/shard_map/ppermute | solution.py:25
  11.3 4.3 %collective-permute-start.3 = (bf16[1,128,256]{2,1,0:T(8,128)(2,1)S(1)}, bf16[1,128,256]{2,1,0:T(8,128)(2,1)S(1)}, u32[]{:S(2)}, u32[]{:S(2)}) collective-permute-start(bf16[1,128,256]{2,1,0:T(8,128)(2,1)S(1)} %slice.9), channel_id=1, source_target_pairs={{0,6},{1,7},{2,0},{3,1},{4,2},{5,3},{6,4},{7,5},{8,14},{9,15},{10,... | collective-permute-start | bytes 196616 | tf_op jit(solution)/shard_map/ppermute | solution.py:25
  15.8 0.5 %collective-permute-start.7 = (bf16[1,256,256]{2,1,0:T(8,128)(2,1)S(1)}, bf16[1,256,256]{2,1,0:T(8,128)(2,1)S(1)}, u32[]{:S(2)}, u32[]{:S(2)}) collective-permute-start(bf16[1,256,256]{2,1,0:T(8,128)(2,1)S(1)} %collective-permute-done.refs_2_), channel_id=1, source_target_pairs={{0,1},{1,0},{2,3},{3,2},{4,5},{5,4},{6,7},{7,6},{8,9},{9,8},{10,11... | collective-permute-start | bytes 393224 | tf_op jit(solution)/shard_map/ppermute | solution.py:29
  16.3 0.2 clear.1.refs_8_
  16.4 1.0 %collective-permute-done.3.refs_1_ = bf16[1,128,256]{2,1,0:T(8,128)(2,1)S(1)} collective-permute-done((bf16[1,128,256]{2,1,0:T(8,128)(2,1)S(1)}, bf16[1,128,256]{2,1,0:T(8,128)(2,1)S(1)}, u32[]{:S(2)}, u32[]{:S(2)}) %collective-permute-start.3) | collective-permute-done | bytes 65568 | tf_op jit(solution)/shard_map/ppermute | solution.py:25
  17.5 4.3 %collective-permute-done.1.refs_0_ = bf16[1,128,256]{2,1,0:T(8,128)(2,1)S(1)} collective-permute-done((bf16[1,128,256]{2,1,0:T(8,128)(2,1)S(1)}, bf16[1,128,256]{2,1,0:T(8,128)(2,1)S(1)}, u32[]{:S(2)}, u32[]{:S(2)}) %collective-permute-start.1) | collective-permute-done | bytes 65568 | tf_op jit(solution)/shard_map/ppermute | solution.py:25
  21.8 4.6 %contract_early.1.refs_6_ = f32[9,256,256]{2,1,0:T(8,128)S(1)} custom-call(s32[40]{0:T(128)S(1)} %copy-done, s32[40]{0:T(128)S(1)} %copy-done.1, bf16[1,256,256]{2,1,0:T(8,128)(2,1)S(1)} %fusion.1.refs_0_, bf16[1,256,256]{2,1,0:T(8,128)(2,1)S(1)} %collective-permute-done.6.refs_1_, ...), custom_call_target="tpu_custom_call", output_to_operand_aliasing={{}: (10, {})} | custom-call | flops 2684354560 | bytes 10485760 | tf_op jit(solution)/shard_map/contract_early/pallas_call | solution.py:48
  26.5 3.2 %contract_late.1 = (f32[9,256,256]{2,1,0:T(8,128)S(1)}, bf16[4,64,256]{2,1,0:T(8,128)(2,1)S(1)}, bf16[4,64,256]{2,1,0:T(8,128)(2,1)S(1)}, bf16[4,64,256]{2,1,0:T...) custom-call(s32[40]{0:T(128)S(1)} %copy-done, ...), custom_call_target="tpu_custom_call", output_to_operand_aliasing={{0}: (8, {})} | custom-call | tf_op jit(solution)/shard_map/contract_late/pallas_call | solution.py:48
  29.8 0.5 %collective-permute-start.12 = (bf16[4,64,256]{2,1,0:T(8,128)(2,1)S(1)}, bf16[4,64,256]{2,1,0:T(8,128)(2,1)S(1)}, u32[]{:S(2)}, u32[]{:S(2)}) collective-permute-start(bf16[4,64,256]{2,1,0:T(8,128)(2,1)S(1)} %get-tuple-element.22), channel_id=1, source_target_pairs={{0,1},{1,0},{2,3},{3,2},{4,5},{5,4},{6,7},{7,6},{8,9},{9,8},{10,11... | collective-permute-start | bytes 393224 | tf_op jit(solution)/shard_map/ppermute | solution.py:29
  30.4 0.4 collective-permute-start.9
  30.8 0.3 collective-permute-done.10.got
  31.2 1.2 %collective-permute-start.11 = (bf16[4,64,256]{2,1,0:T(8,128)(2,1)S(1)}, bf16[4,64,256]{2,1,0:T(8,128)(2,1)S(1)}, u32[]{:S(2)}, u32[]{:S(2)}) collective-permute-start(bf16[4,64,256]{2,1,0:T(8,128)(2,1)S(1)} %merge_cores.3), channel_id=1, source_target_pairs={{0,8},{8,16},{16,24},{24,0},{1,9},{9,17},{17,25},{25,1},{2,10},{10... | collective-permute-start | bytes 393224 | tf_op jit(solution)/shard_map/ppermute | solution.py:25
  32.4 2.1 %collective-permute-start.13 = (bf16[4,64,256]{2,1,0:T(8,128)(2,1)S(1)}, bf16[4,64,256]{2,1,0:T(8,128)(2,1)S(1)}, u32[]{:S(2)}, u32[]{:S(2)}) collective-permute-start(bf16[4,64,256]{2,1,0:T(8,128)(2,1)S(1)} %merge_cores.4), channel_id=1, source_target_pairs={{0,16},{8,24},{16,0},{24,8},{1,17},{9,25},{17,1},{25,9},{2,18},{10... | collective-permute-start | bytes 393224 | tf_op jit(solution)/shard_map/ppermute | solution.py:25
  34.5 1.5 %collective-permute-start.15 = (bf16[4,64,256]{2,1,0:T(8,128)(2,1)S(1)}, bf16[4,64,256]{2,1,0:T(8,128)(2,1)S(1)}, u32[]{:S(2)}, u32[]{:S(2)}) collective-permute-start(bf16[4,64,256]{2,1,0:T(8,128)(2,1)S(1)} %merge_cores.5), channel_id=1, source_target_pairs={{0,24},{8,0},{16,8},{24,16},{1,25},{9,1},{17,9},{25,17},{2,26},{10... | collective-permute-start | bytes 393224 | tf_op jit(solution)/shard_map/ppermute | solution.py:25
  36.0 2.5 %collective-permute-done.11.refs_2_ = bf16[4,64,256]{2,1,0:T(8,128)(2,1)S(1)} collective-permute-done((bf16[4,64,256]{2,1,0:T(8,128)(2,1)S(1)}, bf16[4,64,256]{2,1,0:T(8,128)(2,1)S(1)}, u32[]{:S(2)}, u32[]{:S(2)}) %collective-permute-start.11) | collective-permute-done | bytes 131104 | tf_op jit(solution)/shard_map/ppermute | solution.py:25
  38.5 2.1 %collective-permute-done.13.refs_3_ = bf16[4,64,256]{2,1,0:T(8,128)(2,1)S(1)} collective-permute-done((bf16[4,64,256]{2,1,0:T(8,128)(2,1)S(1)}, bf16[4,64,256]{2,1,0:T(8,128)(2,1)S(1)}, u32[]{:S(2)}, u32[]{:S(2)}) %collective-permute-start.13) | collective-permute-done | bytes 131104 | tf_op jit(solution)/shard_map/ppermute | solution.py:25
  40.6 0.3 collective-permute-done.15.refs_4_
  41.1 0.6 %collective-permute-start.17 = (bf16[64,256]{1,0:T(8,128)(2,1)S(1)}, bf16[64,256]{1,0:T(8,128)(2,1)S(1)}, u32[]{:S(2)}, u32[]{:S(2)}) collective-permute-start(bf16[64,256]{1,0:T(8,128)(2,1)S(1)} %get-tuple-element.27), channel_id=1, source_target_pairs={{0,4},{1,5},{2,6},{3,7},{4,0},{5,1},{6,2},{7,3},{8,12},{9,13},{10,... | collective-permute-start | bytes 98312 | tf_op jit(solution)/shard_map/ppermute | solution.py:25
  41.6 3.3 %collective-permute-start.18 = (bf16[64,256]{1,0:T(8,128)(2,1)S(1)}, bf16[64,256]{1,0:T(8,128)(2,1)S(1)}, u32[]{:S(2)}, u32[]{:S(2)}) collective-permute-start(bf16[64,256]{1,0:T(8,128)(2,1)S(1)} %get-tuple-element.28), channel_id=1, source_target_pairs={{0,6},{1,7},{2,0},{3,1},{4,2},{5,3},{6,4},{7,5},{8,14},{9,15},{10,... | collective-permute-start | bytes 98312 | tf_op jit(solution)/shard_map/ppermute | solution.py:25
  44.9 1.9 %collective-permute-done.16 = bf16[64,256]{1,0:T(8,128)(2,1)S(1)} collective-permute-done((bf16[64,256]{1,0:T(8,128)(2,1)S(1)}, bf16[64,256]{1,0:T(8,128)(2,1)S(1)}, u32[]{:S(2)}, u32[]{:S(2)}) %collective-permute-start.16) | collective-permute-done | bytes 32800 | tf_op jit(solution)/shard_map/ppermute | solution.py:25
  46.8 0.6 %collective-permute-done.18 = bf16[64,256]{1,0:T(8,128)(2,1)S(1)} collective-permute-done((bf16[64,256]{1,0:T(8,128)(2,1)S(1)}, bf16[64,256]{1,0:T(8,128)(2,1)S(1)}, u32[]{:S(2)}, u32[]{:S(2)}) %collective-permute-start.18) | collective-permute-done | bytes 32800 | tf_op jit(solution)/shard_map/ppermute | solution.py:25
  47.3 0.7 %fusion.3 = bf16[1,64,256]{2,1,0:T(8,128)(2,1)} fusion(bf16[64,256]{1,0:T(8,128)(2,1)S(1)} %collective-permute-done.18, bf16[64,256]{1,0:T(8,128)(2,1)S(1)} %collective-permute-done.17, f32[64,256]{1,0:T(8,128)S(1)} %get-tuple-element.25, bf16[64,256]{1,0:T(8,128)(2,1)S(1)} %collective-permute-done.16, s32[]{:T(128)} %bitcast.6, ...), kind=kLoop, calls=%fused_computation.7 | loop fusion | flops 163840 | bytes 196676 | tf_op jit(solution)/shard_map/convert_element_type | solution.py:264
  (40 shorter events, 0.6 us)
Async XLA Ops:
  2.3 9.0 %collective-permute-start.2 = (bf16[1,256,256]{2,1,0:T(8,128)(2,1)S(1)}, bf16[1,256,256]{2,1,0:T(8,128)(2,1)S(1)}, u32[]{:S(2)}, u32[]{:S(2)}) collective-permute-start(bf16[1,256,256]{2,1,0:T(8,128)(2,1)S(1)} %fusion.1.refs_0_), channel_id=1, source_target_pairs={{0,6},{1,7},{2,0},{3,1},{4,2},{5,3},{6,4},{7,5},{8,14},{9,15},{10,... | collective-permute-start | bytes 393224 | tf_op jit(solution)/shard_map/ppermute | solution.py:25
  7.4 8.2 %collective-permute-start = (bf16[1,256,256]{2,1,0:T(8,128)(2,1)S(1)}, bf16[1,256,256]{2,1,0:T(8,128)(2,1)S(1)}, u32[]{:S(2)}, u32[]{:S(2)}) collective-permute-start(bf16[1,256,256]{2,1,0:T(8,128)(2,1)S(1)} %fusion.1.refs_0_), channel_id=1, source_target_pairs={{0,2},{1,3},{2,4},{3,5},{4,6},{5,7},{6,0},{7,1},{8,10},{9,11},{10,... | collective-permute-start | bytes 393224 | tf_op jit(solution)/shard_map/ppermute | solution.py:25
  7.4 14.4 %collective-permute-start.6 = (bf16[1,256,256]{2,1,0:T(8,128)(2,1)S(1)}, bf16[1,256,256]{2,1,0:T(8,128)(2,1)S(1)}, u32[]{:S(2)}, u32[]{:S(2)}) collective-permute-start(bf16[1,256,256]{2,1,0:T(8,128)(2,1)S(1)} %fusion.1.refs_0_), channel_id=1, source_target_pairs={{0,1},{1,0},{2,3},{3,2},{4,5},{5,4},{6,7},{7,6},{8,9},{9,8},{10,11... | collective-permute-start | bytes 393224 | tf_op jit(solution)/shard_map/ppermute | solution.py:29
  11.3 6.2 %collective-permute-start.3 = (bf16[1,128,256]{2,1,0:T(8,128)(2,1)S(1)}, bf16[1,128,256]{2,1,0:T(8,128)(2,1)S(1)}, u32[]{:S(2)}, u32[]{:S(2)}) collective-permute-start(bf16[1,128,256]{2,1,0:T(8,128)(2,1)S(1)} %slice.9), channel_id=1, source_target_pairs={{0,6},{1,7},{2,0},{3,1},{4,2},{5,3},{6,4},{7,5},{8,14},{9,15},{10,... | collective-permute-start | bytes 196616 | tf_op jit(solution)/shard_map/ppermute | solution.py:25
  15.6 6.2 %slice-start = ((s8[5242880]{0:T(1024)(128)(4,1)}), s8[4194304]{0:T(1024)(128)(4,1)S(1)}, s32[]{:S(2)}) async-start(s8[5242880]{0:T(1024)(128)(4,1)} %bitcast.8), calls=%async_computation | async-start | bytes 8388608
  15.6 6.2 %slice-start.2 = ((s8[5242880]{0:T(1024)(128)(4,1)}), s8[4194304]{0:T(1024)(128)(4,1)S(1)}, s32[]{:S(2)}) async-start(s8[5242880]{0:T(1024)(128)(4,1)} %bitcast.10), calls=%async_computation.2 | async-start | bytes 8388608
  15.6 6.2 %slice-start.1 = ((s8[5242880]{0:T(1024)(128)(4,1)}), s8[1048576]{0:T(1024)(128)(4,1)S(1)}, s32[]{:S(2)}) async-start(s8[5242880]{0:T(1024)(128)(4,1)} %bitcast.8), calls=%async_computation.1 | async-start | bytes 2097152
  15.6 6.2 %slice-start.3 = ((s8[5242880]{0:T(1024)(128)(4,1)}), s8[1048576]{0:T(1024)(128)(4,1)S(1)}, s32[]{:S(2)}) async-start(s8[5242880]{0:T(1024)(128)(4,1)} %bitcast.10), calls=%async_computation.3 | async-start | bytes 2097152
  15.6 6.2 %copy-start = (s32[40]{0:T(128)S(1)}, s32[40]{0:T(128)}, u32[]{:S(2)}) copy-start(s32[40]{0:T(128)} %task_in.3) | copy-start | bytes 484
  15.6 6.1 %collective-permute-start.1 = (bf16[1,128,256]{2,1,0:T(8,128)(2,1)S(1)}, bf16[1,128,256]{2,1,0:T(8,128)(2,1)S(1)}, u32[]{:S(2)}, u32[]{:S(2)}) collective-permute-start(bf16[1,128,256]{2,1,0:T(8,128)(2,1)S(1)} %slice.8), channel_id=1, source_target_pairs={{0,2},{1,3},{2,4},{3,5},{4,6},{5,7},{6,0},{7,1},{8,10},{9,11},{10,... | collective-permute-start | bytes 196616 | tf_op jit(solution)/shard_map/ppermute | solution.py:25
  15.7 6.1 %collective-permute-start.8 = (bf16[1,256,256]{2,1,0:T(8,128)(2,1)S(1)}, bf16[1,256,256]{2,1,0:T(8,128)(2,1)S(1)}, u32[]{:S(2)}, u32[]{:S(2)}) collective-permute-start(bf16[1,256,256]{2,1,0:T(8,128)(2,1)S(1)} %collective-permute-done.2.refs_4_), channel_id=1, source_target_pairs={{0,1},{1,0},{2,3},{3,2},{4,5},{5,4},{6,7},{7,6},{8,9},{9,8},{10,11... | collective-permute-start | bytes 393224 | tf_op jit(solution)/shard_map/ppermute | solution.py:29
  15.8 6.0 %collective-permute-start.7 = (bf16[1,256,256]{2,1,0:T(8,128)(2,1)S(1)}, bf16[1,256,256]{2,1,0:T(8,128)(2,1)S(1)}, u32[]{:S(2)}, u32[]{:S(2)}) collective-permute-start(bf16[1,256,256]{2,1,0:T(8,128)(2,1)S(1)} %collective-permute-done.refs_2_), channel_id=1, source_target_pairs={{0,1},{1,0},{2,3},{3,2},{4,5},{5,4},{6,7},{7,6},{8,9},{9,8},{10,11... | collective-permute-start | bytes 393224 | tf_op jit(solution)/shard_map/ppermute | solution.py:29
  17.5 9.0 %collective-permute-start.5 = (bf16[1,128,256]{2,1,0:T(8,128)(2,1)S(1)}, bf16[1,128,256]{2,1,0:T(8,128)(2,1)S(1)}, u32[]{:S(2)}, u32[]{:S(2)}) collective-permute-start(bf16[1,128,256]{2,1,0:T(8,128)(2,1)S(1)} %collective-permute-done.3.refs_1_), channel_id=1, source_target_pairs={{0,1},{1,0},{2,3},{3,2},{4,5},{5,4},{6,7},{7,6},{8,9},{9,8},{10,11... | collective-permute-start | bytes 196616 | tf_op jit(solution)/shard_map/ppermute | solution.py:29
  21.7 4.7 %collective-permute-start.4 = (bf16[1,128,256]{2,1,0:T(8,128)(2,1)S(1)}, bf16[1,128,256]{2,1,0:T(8,128)(2,1)S(1)}, u32[]{:S(2)}, u32[]{:S(2)}) collective-permute-start(bf16[1,128,256]{2,1,0:T(8,128)(2,1)S(1)} %collective-permute-done.1.refs_0_), channel_id=1, source_target_pairs={{0,1},{1,0},{2,3},{3,2},{4,5},{5,4},{6,7},{7,6},{8,9},{9,8},{10,11... | collective-permute-start | bytes 196616 | tf_op jit(solution)/shard_map/ppermute | solution.py:29
  29.7 1.4 %collective-permute-start.10 = (bf16[4,64,256]{2,1,0:T(8,128)(2,1)S(1)}, bf16[4,64,256]{2,1,0:T(8,128)(2,1)S(1)}, u32[]{:S(2)}, u32[]{:S(2)}) collective-permute-start(bf16[4,64,256]{2,1,0:T(8,128)(2,1)S(1)} %get-tuple-element.20), channel_id=1, source_target_pairs={{0,1},{1,0},{2,3},{3,2},{4,5},{5,4},{6,7},{7,6},{8,9},{9,8},{10,11... | collective-permute-start | bytes 393224 | tf_op jit(solution)/shard_map/ppermute | solution.py:29
  29.8 2.5 %collective-permute-start.12 = (bf16[4,64,256]{2,1,0:T(8,128)(2,1)S(1)}, bf16[4,64,256]{2,1,0:T(8,128)(2,1)S(1)}, u32[]{:S(2)}, u32[]{:S(2)}) collective-permute-start(bf16[4,64,256]{2,1,0:T(8,128)(2,1)S(1)} %get-tuple-element.22), channel_id=1, source_target_pairs={{0,1},{1,0},{2,3},{3,2},{4,5},{5,4},{6,7},{7,6},{8,9},{9,8},{10,11... | collective-permute-start | bytes 393224 | tf_op jit(solution)/shard_map/ppermute | solution.py:29
  30.3 4.2 %collective-permute-start.14 = (bf16[4,64,256]{2,1,0:T(8,128)(2,1)S(1)}, bf16[4,64,256]{2,1,0:T(8,128)(2,1)S(1)}, u32[]{:S(2)}, u32[]{:S(2)}) collective-permute-start(bf16[4,64,256]{2,1,0:T(8,128)(2,1)S(1)} %get-tuple-element.24), channel_id=1, source_target_pairs={{0,1},{1,0},{2,3},{3,2},{4,5},{5,4},{6,7},{7,6},{8,9},{9,8},{10,11... | collective-permute-start | bytes 393224 | tf_op jit(solution)/shard_map/ppermute | solution.py:29
  30.4 5.6 %collective-permute-start.9 = (bf16[4,64,256]{2,1,0:T(8,128)(2,1)S(1)}, bf16[4,64,256]{2,1,0:T(8,128)(2,1)S(1)}, u32[]{:S(2)}, u32[]{:S(2)}) collective-permute-start(bf16[4,64,256]{2,1,0:T(8,128)(2,1)S(1)} %get-tuple-element.18), channel_id=1, source_target_pairs={{0,1},{1,0},{2,3},{3,2},{4,5},{5,4},{6,7},{7,6},{8,9},{9,8},{10,11... | collective-permute-start | bytes 393224 | tf_op jit(solution)/shard_map/ppermute | solution.py:29
  31.2 7.4 %collective-permute-start.11 = (bf16[4,64,256]{2,1,0:T(8,128)(2,1)S(1)}, bf16[4,64,256]{2,1,0:T(8,128)(2,1)S(1)}, u32[]{:S(2)}, u32[]{:S(2)}) collective-permute-start(bf16[4,64,256]{2,1,0:T(8,128)(2,1)S(1)} %merge_cores.3), channel_id=1, source_target_pairs={{0,8},{8,16},{16,24},{24,0},{1,9},{9,17},{17,25},{25,1},{2,10},{10... | collective-permute-start | bytes 393224 | tf_op jit(solution)/shard_map/ppermute | solution.py:25
  32.4 8.3 %collective-permute-start.13 = (bf16[4,64,256]{2,1,0:T(8,128)(2,1)S(1)}, bf16[4,64,256]{2,1,0:T(8,128)(2,1)S(1)}, u32[]{:S(2)}, u32[]{:S(2)}) collective-permute-start(bf16[4,64,256]{2,1,0:T(8,128)(2,1)S(1)} %merge_cores.4), channel_id=1, source_target_pairs={{0,16},{8,24},{16,0},{24,8},{1,17},{9,25},{17,1},{25,9},{2,18},{10... | collective-permute-start | bytes 393224 | tf_op jit(solution)/shard_map/ppermute | solution.py:25
  34.5 6.4 %collective-permute-start.15 = (bf16[4,64,256]{2,1,0:T(8,128)(2,1)S(1)}, bf16[4,64,256]{2,1,0:T(8,128)(2,1)S(1)}, u32[]{:S(2)}, u32[]{:S(2)}) collective-permute-start(bf16[4,64,256]{2,1,0:T(8,128)(2,1)S(1)} %merge_cores.5), channel_id=1, source_target_pairs={{0,24},{8,0},{16,8},{24,16},{1,25},{9,1},{17,9},{25,17},{2,26},{10... | collective-permute-start | bytes 393224 | tf_op jit(solution)/shard_map/ppermute | solution.py:25
  41.0 5.8 %collective-permute-start.16 = (bf16[64,256]{1,0:T(8,128)(2,1)S(1)}, bf16[64,256]{1,0:T(8,128)(2,1)S(1)}, u32[]{:S(2)}, u32[]{:S(2)}) collective-permute-start(bf16[64,256]{1,0:T(8,128)(2,1)S(1)} %get-tuple-element.26), channel_id=1, source_target_pairs={{0,2},{1,3},{2,4},{3,5},{4,6},{5,7},{6,0},{7,1},{8,10},{9,11},{10,... | collective-permute-start | bytes 98312 | tf_op jit(solution)/shard_map/ppermute | solution.py:25
  41.1 5.7 %collective-permute-start.17 = (bf16[64,256]{1,0:T(8,128)(2,1)S(1)}, bf16[64,256]{1,0:T(8,128)(2,1)S(1)}, u32[]{:S(2)}, u32[]{:S(2)}) collective-permute-start(bf16[64,256]{1,0:T(8,128)(2,1)S(1)} %get-tuple-element.27), channel_id=1, source_target_pairs={{0,4},{1,5},{2,6},{3,7},{4,0},{5,1},{6,2},{7,3},{8,12},{9,13},{10,... | collective-permute-start | bytes 98312 | tf_op jit(solution)/shard_map/ppermute | solution.py:25
  41.6 5.7 %collective-permute-start.18 = (bf16[64,256]{1,0:T(8,128)(2,1)S(1)}, bf16[64,256]{1,0:T(8,128)(2,1)S(1)}, u32[]{:S(2)}, u32[]{:S(2)}) collective-permute-start(bf16[64,256]{1,0:T(8,128)(2,1)S(1)} %get-tuple-element.28), channel_id=1, source_target_pairs={{0,6},{1,7},{2,0},{3,1},{4,2},{5,3},{6,4},{7,5},{8,14},{9,15},{10,... | collective-permute-start | bytes 98312 | tf_op jit(solution)/shard_map/ppermute | solution.py:25
  (1 other events, 6.2 us)

commit v3 on v0

v3 whole, which is shorter than its diff:
```python
import functools
import math

import jax
import jax.numpy as jnp
from jax import lax
from jax.experimental import pallas as pl
from jax.experimental.pallas import tpu as pltpu
from jax.sharding import PartitionSpec as P


CORES = 2
UNROLL = 20
DIRECT = (0, 1)
VMEM_BYTES = 67043328
SLACK = 1 << 20
VMEM = pltpu.VMEM
SMEM = pltpu.SMEM
BF16 = jnp.bfloat16
F32 = jnp.float32


def partner(layer, k, depth, back=False):
    if depth & (depth - 1) == 0:
        return layer ^ k
    return lax.rem(layer + (depth - k if back else k), depth) if isinstance(layer, jax.Array) else (layer + k) % depth


def send(value, axis, target):
    return lax.ppermute(value, axis, [(i, target(i)) for i in range(lax.axis_size(axis))])


def along_z(value, k, rule=partner):
    depth = lax.axis_size("sec") // CORES
    return send(value, "sec", lambda i: rule(i // CORES, k, depth) * CORES + i % CORES)


def round_z(layer, k, depth):
    return lax.rem(layer + k, depth) if isinstance(k, jax.Array) else (layer + k) % depth


def along_mpo(value, j):
    groups = lax.axis_size("mpo")
    return send(value, "mpo", lambda i: (i + j) % groups)


def swap(value):
    return send(value, "sec", lambda i: i ^ 1)


def array(shape, dtype):
    return jax.ShapeDtypeStruct(shape, dtype)


def grant(scratch, *operands):
    mine, others = (sum(math.prod(a.shape) * a.dtype.itemsize for a in group) for group in (scratch, operands))
    return mine + SLACK if 2 * (mine + others) < VMEM_BYTES else min(mine + others + 2 * SLACK, VMEM_BYTES)


def call(kernel, out_shape, operands, scratch=(), scalars=0, cost=None, aliases=None, streamed=()):
    one = not isinstance(out_shape, tuple)
    outs = (out_shape,) if one else out_shape
    specs = [pl.BlockSpec(memory_space=SMEM)] * scalars
    specs += [pl.BlockSpec(memory_space=VMEM)] * (len(operands) - scalars)
    for n in streamed:
        specs[n] = pl.BlockSpec(memory_space=pl.ANY)
    run = pl.pallas_call(
        kernel,
        out_shape=outs,
        in_specs=specs,
        out_specs=(pl.BlockSpec(memory_space=VMEM),) * len(outs),
        scratch_shapes=scratch,
        cost_estimate=cost,
        input_output_aliases=aliases or {},
        compiler_params=pltpu.CompilerParams(
            vmem_limit_bytes=grant(
                [s for s in scratch if getattr(s, "memory_space", None) == VMEM], *outs, *operands[scalars:]
            )
        ),
    )
    results = run(*operands)
    return results[0] if one else results


def clear(acc):
    acc[...] = jnp.zeros_like(acc)


def take_rows(own, part):
    quarter = part.shape[1]
    part[...] = own[:, pl.ds(pl.multiple_of(lax.axis_index("mpo") * quarter, quarter), quarter)]


def products(task_in, task_out, blocks, left, right, acc, *stage):
    tasks = left.shape[0]
    limit = stage[0].shape[1] if stage else UNROLL
    unroll = max(n for n in range(1, limit + 1) if tasks % n == 0)

    def fetch(which, t, u):
        source = (left, right)[which]
        if not stage:
            return source[t]
        target, sems = stage
        copy = pltpu.make_async_copy(source.at[t], target.at[which, u], sems.at[which, u])
        copy.start()
        copy.wait()
        return target[which, u]

    def step(n, _):
        for u in range(unroll):
            t = n * unroll + u
            middle = jnp.dot(fetch(0, t, u), blocks[task_in[t]], preferred_element_type=F32).astype(BF16)
            acc[task_out[t]] += lax.dot_general(
                middle, fetch(1, t, u), (((1,), (1,)), ((), ())), preferred_element_type=F32
            )
        return 0

    lax.fori_loop(0, tasks // unroll, step, 0)


def contract(task_in, task_out, *refs):
    groups = lax.axis_size("mpo")
    direct, refs = refs[: CORES * len(DIRECT)], refs[CORES * len(DIRECT) :]
    spread, (left, right, _, acc), refs = refs[: CORES * groups], refs[CORES * groups :][:4], refs[CORES * groups + 4 :]
    sends, keeps, (blocks, *stage) = refs[:groups], refs[groups : 2 * groups], refs[2 * groups :]
    depth, quarter = sends[0].shape[:2]
    sec = lax.axis_index("sec")
    layer, core = sec // CORES, sec % CORES
    group = lax.axis_index("mpo")
    for n, k in enumerate(DIRECT):
        base = partner(layer, k, depth, back=True) * CORES
        blocks[base + core] = direct[CORES * n][0]
        blocks[base + 1 - core] = direct[CORES * n + 1][0]
    for n in range(spread[0].shape[0]):
        base = partner(layer, len(DIRECT) + n, depth, back=True) * CORES
        for j in range(groups):
            start = lax.rem(group + groups - j, groups) * quarter
            rows = pl.ds(pl.multiple_of(start, quarter), quarter)
            blocks[base + core, rows] = spread[CORES * j][n]
            blocks[base + 1 - core, rows] = spread[CORES * j + 1][n]
    products(task_in, task_out, blocks, left, right, acc, *stage)

    def put(k, _):
        base = round_z(layer, k, depth) * CORES
        for j in range(groups):
            rows = pl.ds(pl.multiple_of(lax.rem(group + j, groups) * quarter, quarter), quarter)
            keeps[j][k] = acc[base + core, rows]
            sends[j][k] = acc[base + 1 - core, rows].astype(BF16)
        return 0

    lax.fori_loop(0, depth, put, 0)


def merge_cores(keep, got, away, here):
    value = keep[...] + got[...].astype(F32)
    here[...] = value[:1].astype(BF16)
    away[...] = value[1:].astype(BF16)


def merge_away(depth, *refs):
    terms, sends = refs[: 1 - depth], refs[1 - depth :]
    for k in range(1, depth):
        values = [term[k + term.shape[0] - depth].astype(F32) for term in terms]
        sends[k - 1][...] = functools.reduce(jnp.add, values).astype(BF16)


def merge_here(*refs):
    *terms, total = refs
    total[...] = functools.reduce(jnp.add, [term[0].astype(F32) for term in terms])


def device_step(
    wavefunction, left_dims, right_dims, left_environment_block, right_env, task_out, task_in
):
    rows, cols = wavefunction.shape[1:]
    groups = lax.axis_size("mpo")
    sectors = lax.axis_size("sec")
    depth = sectors // CORES
    quarter = rows // groups
    tasks = task_out.shape[0]
    group = lax.axis_index("mpo")

    def live(shape, first_row):
        row_ids = lax.broadcasted_iota(jnp.int32, shape, 1) + first_row
        col_ids = lax.broadcasted_iota(jnp.int32, shape, 2)
        return (row_ids < left_dims[:, None, None]) & (col_ids < right_dims[:, None, None])

    own = jnp.where(live(wavefunction.shape, 0), wavefunction, jnp.zeros_like(wavefunction))
    part = call(take_rows, array((1, quarter, cols), BF16), (own,))
    far = [along_z(part, k) for k in range(len(DIRECT), depth)]
    near = [own, *(along_z(own, k) for k in DIRECT[1:])]
    pieces = [jnp.concatenate(far, axis=0)]
    pieces += [along_mpo(pieces[0], j) for j in range(1, groups)]
    blocks = [b for block in near for b in (block, swap(block))]
    blocks += [b for piece in pieces for b in (piece, swap(piece))]

    work = (left_environment_block, right_env)
    cost = pl.CostEstimate(
        flops=4 * tasks * rows * cols * rows, bytes_accessed=4 * tasks * rows * cols, transcendentals=0
    )
    slow = pl.CostEstimate(flops=4 * cost.flops, bytes_accessed=4 * cost.bytes_accessed, transcendentals=0)
    sums = array((sectors, rows, cols), F32)
    acc = call(clear, sums, (), cost=slow)
    scratch = (VMEM((sectors, rows, cols), BF16),)
    streamed = 16 * sums.size > VMEM_BYTES
    if streamed:
        scratch += (VMEM((2, 4, rows, cols), BF16), pltpu.SemaphoreType.DMA((2, 4)))
    operands = (task_in, task_out, *blocks, *work, acc)
    last = len(operands) - 1
    piece = (depth, quarter, cols)
    _, *pieces = call(
        contract,
        (sums, *(array(piece, BF16),) * groups, *(array(piece, F32),) * groups),
        operands,
        scratch,
        scalars=2,
        cost=cost,
        aliases={last: 0},
        streamed=(last - 2, last - 1) if streamed else (),
    )
    sends, keeps = pieces[:groups], pieces[groups:]

    away, here = [], [keeps[0]]
    for j in [*range(1, groups), 0]:
        got = swap(sends[j])
        if j:
            first, last = call(
                merge_cores, (array((depth - 1, *piece[1:]), BF16), array((1, *piece[1:]), BF16)), (keeps[j], got)
            )
            away.append(along_mpo(first, j))
            here.append(along_mpo(last, j))
        else:
            here.append(got)
            away = [keeps[0], got, *away]
    sent = call(functools.partial(merge_away, depth), (array(piece[1:], BF16),) * (depth - 1), away)
    total = call(merge_here, array(piece[1:], F32), here)
    for k, block in enumerate(sent):
        total = total + along_z(block, k + 1, round_z).astype(F32)
    total = total[None]
    return jnp.where(live(total.shape, group * quarter), total, jnp.zeros_like(total)).astype(BF16)


def solution(mesh):
    return jax.shard_map(
        device_step,
        mesh=mesh,
        in_specs=(
            P("sec", None, None),
            P("sec"),
            P("sec"),
            P(("mpo", "sec"), None, None),
            P(("mpo", "sec"), None, None),
            P(("mpo", "sec")),
            P(("mpo", "sec")),
        ),
        out_specs=P("sec", "mpo", None),
        check_vma=False,
    )
```

time: 145 us -> 44.4 us (0.31)
  waiting for transfers between devices: 92.1 us -> 14.8 us
  starting transfers between devices: 0.09 us -> 21.6 us
  other arithmetic: 19.3 us -> 1.66 us
  between operations: 14.5 us -> 1.48 us
  matrix products: 11.4 us -> 0 us
  local copies, waits for them, and re-layouts: 7.49 us -> 0.04 us
  Pallas kernels: 0 us -> 4.73 us
    unnamed x4 -> x0, waiting for transfers between devices: 34.8 us -> none
    reduce_scatter x1 -> x0, waiting for transfers between devices: 33.6 us -> none  [on_device(): lax.psum_scatter(row_sums[0], 'sec', scatter_dimension=0, tiled=True)]
    all_gather x1 -> x0, waiting for transfers between devices: 23.7 us -> none  [on_device(): blocks = lax.all_gather(masked, 'sec', axis=0, tiled=True)]
    ppermute x0 -> x25, starting transfers between devices: none -> 21.6 us  [send(): lax.ppermute(value, axis, [(i, target(i)) for i in range(lax.axis_size(ax...]
    scatter-add x1 -> x0, other arithmetic: 14.8 us -> none  [sector_sums(): return jax.ops.segment_sum(terms, task_out, num_segments=sectors)]
    ppermute x0 -> x25, waiting for transfers between devices: none -> 14.8 us  [send(): lax.ppermute(value, axis, [(i, target(i)) for i in range(lax.axis_size(ax...]
    dot_general x2 -> x0, matrix products: 11.4 us -> none  [the longest x1 5.84 us: on_device(): jnp.einsum('xvz,xzy->xvy', left_environment_block, picked_tasks, preferre...]
    gather x1 -> x0, local copies, waits for them, and re-layouts: 5.9 us -> none  [on_device(): picked_tasks = jnp.take(blocks, task_in, axis=0)]
  transfers between devices with their start and end apart: 3 -> 25, of which waited for: 3 -> 14; matrix products, arithmetic and copies ran while one was open for 1% -> 0% of each run, Pallas kernels for 0% -> 1%
where the time goes in v3:
time: 44.4 us; the launch traced here: 44.3 us
  starting transfers between devices  21.6 us (49%)
  waiting for transfers between devices  14.8 us (33%)
  Pallas kernels  4.73 us (11%)
  other arithmetic  1.66 us (4%)
  between operations  1.48 us (3%)
    ppermute x25, starting transfers between devices, send(): lax.ppermute(value, axis, [(i, target(i)) for i in range(lax.axis_size(ax...  21.6 us
    ppermute x25, waiting for transfers between devices, send(): lax.ppermute(value, axis, [(i, target(i)) for i in range(lax.axis_size(ax...  14.8 us
    pallas_call x8, Pallas kernels, call(): results = run(*operands)  4.73 us
    select_n x1, other arithmetic, device_step(): jnp.where(live(wavefunction.shape, 0), wavefunction, jnp.zeros_like(wavef...  0.95 us
  transfers between devices with their start and end apart: 25, of which 14 were waited for; matrix products, arithmetic and copies ran while one was open for 0% of the time, Pallas kernels for 1%

profile of v3, /device:TPU:0, one launch (start us, length us, event | category | flops | bytes accessed | tf_op | source)
XLA Modules:
  0.0 44.3 jit_solution(5931702629214866588)
XLA Ops:
  1.3 1.0 %fusion.1.own.refs_0_ = bf16[1,256,256]{2,1,0:T(8,128)(2,1)S(1)} fusion(bf16[1,256,256]{2,1,0:T(8,128)(2,1)} %param.7, s32[]{:T(128)} %bitcast.7, s32[]{:T(128)} %bitcast.5), kind=kLoop, calls=%fused_computation.3 | loop fusion | flops 262144 | bytes 262152 | tf_op jit(solution)/shard_map/jit(_where)/select_n | solution.py:188
  2.3 4.1 %collective-permute-start.3 = (bf16[1,64,256]{2,1,0:T(8,128)(2,1)S(1)}, bf16[1,64,256]{2,1,0:T(8,128)(2,1)S(1)}, u32[]{:S(2)}, u32[]{:S(2)}) collective-permute-start(bf16[1,64,256]{2,1,0:T(8,128)(2,1)S(1)} %shard_map.73), channel_id=1, source_target_pairs={{0,4},{1,5},{2,6},{3,7},{4,0},{5,1},{6,2},{7,3},{8,12},{9,13},{10,... | collective-permute-start | bytes 98312 | tf_op jit(solution)/shard_map/ppermute | solution.py:30
  6.4 1.3 %collective-permute-start.4 = (bf16[1,64,256]{2,1,0:T(8,128)(2,1)S(1)}, bf16[1,64,256]{2,1,0:T(8,128)(2,1)S(1)}, u32[]{:S(2)}, u32[]{:S(2)}) collective-permute-start(bf16[1,64,256]{2,1,0:T(8,128)(2,1)S(1)} %shard_map.73), channel_id=1, source_target_pairs={{0,6},{1,7},{2,4},{3,5},{4,2},{5,3},{6,0},{7,1},{8,14},{9,15},{10,... | collective-permute-start | bytes 98312 | tf_op jit(solution)/shard_map/ppermute | solution.py:30
  8.0 0.7 %collective-permute-done.3 = bf16[1,64,256]{2,1,0:T(8,128)(2,1)S(1)} collective-permute-done((bf16[1,64,256]{2,1,0:T(8,128)(2,1)S(1)}, bf16[1,64,256]{2,1,0:T(8,128)(2,1)S(1)}, u32[]{:S(2)}, u32[]{:S(2)}) %collective-permute-start.3) | collective-permute-done | bytes 32800 | tf_op jit(solution)/shard_map/ppermute | solution.py:30
  8.7 3.8 %collective-permute-done.4 = bf16[1,64,256]{2,1,0:T(8,128)(2,1)S(1)} collective-permute-done((bf16[1,64,256]{2,1,0:T(8,128)(2,1)S(1)}, bf16[1,64,256]{2,1,0:T(8,128)(2,1)S(1)}, u32[]{:S(2)}, u32[]{:S(2)}) %collective-permute-start.4) | collective-permute-done | bytes 32800 | tf_op jit(solution)/shard_map/ppermute | solution.py:30
  12.5 2.5 %collective-permute-start.10 = (bf16[2,64,256]{2,1,0:T(8,128)(2,1)S(1)}, bf16[2,64,256]{2,1,0:T(8,128)(2,1)S(1)}, u32[]{:S(2)}, u32[]{:S(2)}) collective-permute-start(bf16[2,64,256]{2,1,0:T(8,128)(2,1)S(1)} %constant_dynamic-update-slice_fusion.refs_4_), channel_id=1, source_target_pairs={{0,24},{8,0},{16,8},{24,16},{1,25},{9,1},{17,9},{25,17},{2,26},{10... | collective-permute-start | bytes 196616 | tf_op jit(solution)/shard_map/ppermute | solution.py:30
  15.0 0.5 %collective-permute-start.8 = (bf16[2,64,256]{2,1,0:T(8,128)(2,1)S(1)}, bf16[2,64,256]{2,1,0:T(8,128)(2,1)S(1)}, u32[]{:S(2)}, u32[]{:S(2)}) collective-permute-start(bf16[2,64,256]{2,1,0:T(8,128)(2,1)S(1)} %constant_dynamic-update-slice_fusion.refs_4_), channel_id=1, source_target_pairs={{0,16},{8,24},{16,0},{24,8},{1,17},{9,25},{17,1},{25,9},{2,18},{10... | collective-permute-start | bytes 196616 | tf_op jit(solution)/shard_map/ppermute | solution.py:30
  15.5 0.6 %collective-permute-start.6 = (bf16[2,64,256]{2,1,0:T(8,128)(2,1)S(1)}, bf16[2,64,256]{2,1,0:T(8,128)(2,1)S(1)}, u32[]{:S(2)}, u32[]{:S(2)}) collective-permute-start(bf16[2,64,256]{2,1,0:T(8,128)(2,1)S(1)} %constant_dynamic-update-slice_fusion.refs_4_), channel_id=1, source_target_pairs={{0,8},{8,16},{16,24},{24,0},{1,9},{9,17},{17,25},{25,1},{2,10},{10... | collective-permute-start | bytes 196616 | tf_op jit(solution)/shard_map/ppermute | solution.py:30
  16.1 0.9 %collective-permute-done.10.refs_10_ = bf16[2,64,256]{2,1,0:T(8,128)(2,1)S(1)} collective-permute-done((bf16[2,64,256]{2,1,0:T(8,128)(2,1)S(1)}, bf16[2,64,256]{2,1,0:T(8,128)(2,1)S(1)}, u32[]{:S(2)}, u32[]{:S(2)}) %collective-permute-start.10) | collective-permute-done | bytes 65568 | tf_op jit(solution)/shard_map/ppermute | solution.py:30
  17.0 2.3 %collective-permute-done.8.refs_8_ = bf16[2,64,256]{2,1,0:T(8,128)(2,1)S(1)} collective-permute-done((bf16[2,64,256]{2,1,0:T(8,128)(2,1)S(1)}, bf16[2,64,256]{2,1,0:T(8,128)(2,1)S(1)}, u32[]{:S(2)}, u32[]{:S(2)}) %collective-permute-start.8) | collective-permute-done | bytes 65568 | tf_op jit(solution)/shard_map/ppermute | solution.py:30
  19.3 1.4 %collective-permute-done.6.refs_6_ = bf16[2,64,256]{2,1,0:T(8,128)(2,1)S(1)} collective-permute-done((bf16[2,64,256]{2,1,0:T(8,128)(2,1)S(1)}, bf16[2,64,256]{2,1,0:T(8,128)(2,1)S(1)}, u32[]{:S(2)}, u32[]{:S(2)}) %collective-permute-start.6) | collective-permute-done | bytes 65568 | tf_op jit(solution)/shard_map/ppermute | solution.py:30
  20.7 0.5 %collective-permute-start.7 = (bf16[2,64,256]{2,1,0:T(8,128)(2,1)S(1)}, bf16[2,64,256]{2,1,0:T(8,128)(2,1)S(1)}, u32[]{:S(2)}, u32[]{:S(2)}) collective-permute-start(bf16[2,64,256]{2,1,0:T(8,128)(2,1)S(1)} %collective-permute-done.6.refs_6_), channel_id=1, source_target_pairs={{0,1},{1,0},{2,3},{3,2},{4,5},{5,4},{6,7},{7,6},{8,9},{9,8},{10,11... | collective-permute-start | bytes 196616 | tf_op jit(solution)/shard_map/ppermute | solution.py:30
  22.6 4.4 %shard_map.75 = (f32[8,256,256]{2,1,0:T(8,128)S(1)}, bf16[4,64,256]{2,1,0:T(8,128)(2,1)S(1)}, bf16[4,64,256]{2,1,0:T(8,128)(2,1)S(1)}, bf16[4,64,256]{2,1,0:T(8,...) custom-call(s32[40]{0:T(128)S(1)} %copy-done, ...), custom_call_target="tpu_custom_call", output_to_operand_aliasing={{0}: (16, {})} | custom-call | flops 2684354560 | bytes 10485760 | tf_op jit(solution)/shard_map/pallas_call | solution.py:81
  28.7 1.6 %collective-permute-start.20 = (bf16[3,64,256]{2,1,0:T(8,128)(2,1)S(1)}, bf16[3,64,256]{2,1,0:T(8,128)(2,1)S(1)}, u32[]{:S(2)}, u32[]{:S(2)}) collective-permute-start(bf16[3,64,256]{2,1,0:T(8,128)(2,1)S(1)} %get-tuple-element.34), channel_id=1, source_target_pairs={{0,16},{8,24},{16,0},{24,8},{1,17},{9,25},{17,1},{25,9},{2,18},{10... | collective-permute-start | bytes 294920 | tf_op jit(solution)/shard_map/ppermute | solution.py:30
  30.3 2.9 %collective-permute-start.21 = (bf16[3,64,256]{2,1,0:T(8,128)(2,1)S(1)}, bf16[3,64,256]{2,1,0:T(8,128)(2,1)S(1)}, u32[]{:S(2)}, u32[]{:S(2)}) collective-permute-start(bf16[3,64,256]{2,1,0:T(8,128)(2,1)S(1)} %get-tuple-element.35), channel_id=1, source_target_pairs={{0,24},{8,0},{16,8},{24,16},{1,25},{9,1},{17,9},{25,17},{2,26},{10... | collective-permute-start | bytes 294920 | tf_op jit(solution)/shard_map/ppermute | solution.py:30
  33.2 0.6 %collective-permute-start.15 = (bf16[1,64,256]{2,1,0:T(8,128)(2,1)S(1)}, bf16[1,64,256]{2,1,0:T(8,128)(2,1)S(1)}, u32[]{:S(2)}, u32[]{:S(2)}) collective-permute-start(bf16[1,64,256]{2,1,0:T(8,128)(2,1)S(1)} %get-tuple-element.28), channel_id=1, source_target_pairs={{0,16},{8,24},{16,0},{24,8},{1,17},{9,25},{17,1},{25,9},{2,18},{10... | collective-permute-start | bytes 98312 | tf_op jit(solution)/shard_map/ppermute | solution.py:30
  33.8 1.2 %collective-permute-done.19.refs_2_ = bf16[3,64,256]{2,1,0:T(8,128)(2,1)S(1)} collective-permute-done((bf16[3,64,256]{2,1,0:T(8,128)(2,1)S(1)}, bf16[3,64,256]{2,1,0:T(8,128)(2,1)S(1)}, u32[]{:S(2)}, u32[]{:S(2)}) %collective-permute-start.19) | collective-permute-done | bytes 98336 | tf_op jit(solution)/shard_map/ppermute | solution.py:30
  35.0 1.6 %collective-permute-start.17 = (bf16[1,64,256]{2,1,0:T(8,128)(2,1)S(1)}, bf16[1,64,256]{2,1,0:T(8,128)(2,1)S(1)}, u32[]{:S(2)}, u32[]{:S(2)}) collective-permute-start(bf16[1,64,256]{2,1,0:T(8,128)(2,1)S(1)} %get-tuple-element.31), channel_id=1, source_target_pairs={{0,24},{8,0},{16,8},{24,16},{1,25},{9,1},{17,9},{25,17},{2,26},{10... | collective-permute-start | bytes 98312 | tf_op jit(solution)/shard_map/ppermute | solution.py:30
  36.6 0.6 %collective-permute-done.21.refs_4_ = bf16[3,64,256]{2,1,0:T(8,128)(2,1)S(1)} collective-permute-done((bf16[3,64,256]{2,1,0:T(8,128)(2,1)S(1)}, bf16[3,64,256]{2,1,0:T(8,128)(2,1)S(1)}, u32[]{:S(2)}, u32[]{:S(2)}) %collective-permute-start.21) | collective-permute-done | bytes 98336 | tf_op jit(solution)/shard_map/ppermute | solution.py:30
  37.3 1.9 %collective-permute-start.23 = (bf16[64,256]{1,0:T(8,128)(2,1)S(1)}, bf16[64,256]{1,0:T(8,128)(2,1)S(1)}, u32[]{:S(2)}, u32[]{:S(2)}) collective-permute-start(bf16[64,256]{1,0:T(8,128)(2,1)S(1)} %get-tuple-element.37), channel_id=1, source_target_pairs={{0,4},{1,5},{2,6},{3,7},{4,0},{5,1},{6,2},{7,3},{8,12},{9,13},{10,... | collective-permute-start | bytes 98312 | tf_op jit(solution)/shard_map/ppermute | solution.py:30
  39.2 1.9 %collective-permute-start.24 = (bf16[64,256]{1,0:T(8,128)(2,1)S(1)}, bf16[64,256]{1,0:T(8,128)(2,1)S(1)}, u32[]{:S(2)}, u32[]{:S(2)}) collective-permute-start(bf16[64,256]{1,0:T(8,128)(2,1)S(1)} %get-tuple-element.38), channel_id=1, source_target_pairs={{0,6},{1,7},{2,0},{3,1},{4,2},{5,3},{6,4},{7,5},{8,14},{9,15},{10,... | collective-permute-start | bytes 98312 | tf_op jit(solution)/shard_map/ppermute | solution.py:30
  41.2 1.8 %collective-permute-done.22 = bf16[64,256]{1,0:T(8,128)(2,1)S(1)} collective-permute-done((bf16[64,256]{1,0:T(8,128)(2,1)S(1)}, bf16[64,256]{1,0:T(8,128)(2,1)S(1)}, u32[]{:S(2)}, u32[]{:S(2)}) %collective-permute-start.22) | collective-permute-done | bytes 32800 | tf_op jit(solution)/shard_map/ppermute | solution.py:30
  43.0 0.6 %collective-permute-done.24 = bf16[64,256]{1,0:T(8,128)(2,1)S(1)} collective-permute-done((bf16[64,256]{1,0:T(8,128)(2,1)S(1)}, bf16[64,256]{1,0:T(8,128)(2,1)S(1)}, u32[]{:S(2)}, u32[]{:S(2)}) %collective-permute-start.24) | collective-permute-done | bytes 32800 | tf_op jit(solution)/shard_map/ppermute | solution.py:30
  43.6 0.7 %fusion.3 = bf16[1,64,256]{2,1,0:T(8,128)(2,1)} fusion(bf16[64,256]{1,0:T(8,128)(2,1)S(1)} %collective-permute-done.24, bf16[64,256]{1,0:T(8,128)(2,1)S(1)} %collective-permute-done.23, f32[64,256]{1,0:T(8,128)S(1)} %shard_map.79, bf16[64,256]{1,0:T(8,128)(2,1)S(1)} %collective-permute-done.22, s32[]{:T(128)} %bitcast.6, pred[64]{0:T(512)(128)(4,1)S(1)} %add_compare_fusion), kind=kLoop, calls=%fused_computation.7 | loop fusion | flops 163840 | bytes 196676 | tf_op jit(solution)/shard_map/convert_element_type | solution.py:240
  (53 shorter events, 3.5 us)
Async XLA Ops:
  2.3 6.4 %collective-permute-start.3 = (bf16[1,64,256]{2,1,0:T(8,128)(2,1)S(1)}, bf16[1,64,256]{2,1,0:T(8,128)(2,1)S(1)}, u32[]{:S(2)}, u32[]{:S(2)}) collective-permute-start(bf16[1,64,256]{2,1,0:T(8,128)(2,1)S(1)} %shard_map.73), channel_id=1, source_target_pairs={{0,4},{1,5},{2,6},{3,7},{4,0},{5,1},{6,2},{7,3},{8,12},{9,13},{10,... | collective-permute-start | bytes 98312 | tf_op jit(solution)/shard_map/ppermute | solution.py:30
  6.4 6.1 %collective-permute-start.4 = (bf16[1,64,256]{2,1,0:T(8,128)(2,1)S(1)}, bf16[1,64,256]{2,1,0:T(8,128)(2,1)S(1)}, u32[]{:S(2)}, u32[]{:S(2)}) collective-permute-start(bf16[1,64,256]{2,1,0:T(8,128)(2,1)S(1)} %shard_map.73), channel_id=1, source_target_pairs={{0,6},{1,7},{2,4},{3,5},{4,2},{5,3},{6,0},{7,1},{8,14},{9,15},{10,... | collective-permute-start | bytes 98312 | tf_op jit(solution)/shard_map/ppermute | solution.py:30
  7.8 13.5 %collective-permute-start.1 = (bf16[1,256,256]{2,1,0:T(8,128)(2,1)S(1)}, bf16[1,256,256]{2,1,0:T(8,128)(2,1)S(1)}, u32[]{:S(2)}, u32[]{:S(2)}) collective-permute-start(bf16[1,256,256]{2,1,0:T(8,128)(2,1)S(1)} %fusion.1.own.refs_0_), channel_id=1, source_target_pairs={{0,2},{1,3},{2,0},{3,1},{4,6},{5,7},{6,4},{7,5},{8,10},{9,11},{10,... | collective-permute-start | bytes 393224 | tf_op jit(solution)/shard_map/ppermute | solution.py:30
  12.5 4.5 %collective-permute-start.10 = (bf16[2,64,256]{2,1,0:T(8,128)(2,1)S(1)}, bf16[2,64,256]{2,1,0:T(8,128)(2,1)S(1)}, u32[]{:S(2)}, u32[]{:S(2)}) collective-permute-start(bf16[2,64,256]{2,1,0:T(8,128)(2,1)S(1)} %constant_dynamic-update-slice_fusion.refs_4_), channel_id=1, source_target_pairs={{0,24},{8,0},{16,8},{24,16},{1,25},{9,1},{17,9},{25,17},{2,26},{10... | collective-permute-start | bytes 196616 | tf_op jit(solution)/shard_map/ppermute | solution.py:30
  15.0 4.3 %collective-permute-start.8 = (bf16[2,64,256]{2,1,0:T(8,128)(2,1)S(1)}, bf16[2,64,256]{2,1,0:T(8,128)(2,1)S(1)}, u32[]{:S(2)}, u32[]{:S(2)}) collective-permute-start(bf16[2,64,256]{2,1,0:T(8,128)(2,1)S(1)} %constant_dynamic-update-slice_fusion.refs_4_), channel_id=1, source_target_pairs={{0,16},{8,24},{16,0},{24,8},{1,17},{9,25},{17,1},{25,9},{2,18},{10... | collective-permute-start | bytes 196616 | tf_op jit(solution)/shard_map/ppermute | solution.py:30
  15.5 5.2 %collective-permute-start.6 = (bf16[2,64,256]{2,1,0:T(8,128)(2,1)S(1)}, bf16[2,64,256]{2,1,0:T(8,128)(2,1)S(1)}, u32[]{:S(2)}, u32[]{:S(2)}) collective-permute-start(bf16[2,64,256]{2,1,0:T(8,128)(2,1)S(1)} %constant_dynamic-update-slice_fusion.refs_4_), channel_id=1, source_target_pairs={{0,8},{8,16},{16,24},{24,0},{1,9},{9,17},{17,25},{25,1},{2,10},{10... | collective-permute-start | bytes 196616 | tf_op jit(solution)/shard_map/ppermute | solution.py:30
  16.1 4.6 %collective-permute-start.5 = (bf16[2,64,256]{2,1,0:T(8,128)(2,1)S(1)}, bf16[2,64,256]{2,1,0:T(8,128)(2,1)S(1)}, u32[]{:S(2)}, u32[]{:S(2)}) collective-permute-start(bf16[2,64,256]{2,1,0:T(8,128)(2,1)S(1)} %constant_dynamic-update-slice_fusion.refs_4_), channel_id=1, source_target_pairs={{0,1},{1,0},{2,3},{3,2},{4,5},{5,4},{6,7},{7,6},{8,9},{9,8},{10,11... | collective-permute-start | bytes 196616 | tf_op jit(solution)/shard_map/ppermute | solution.py:30
  17.0 4.4 %collective-permute-start = (bf16[1,256,256]{2,1,0:T(8,128)(2,1)S(1)}, bf16[1,256,256]{2,1,0:T(8,128)(2,1)S(1)}, u32[]{:S(2)}, u32[]{:S(2)}) collective-permute-start(bf16[1,256,256]{2,1,0:T(8,128)(2,1)S(1)} %fusion.1.own.refs_0_), channel_id=1, source_target_pairs={{0,1},{1,0},{2,3},{3,2},{4,5},{5,4},{6,7},{7,6},{8,9},{9,8},{10,11... | collective-permute-start | bytes 393224 | tf_op jit(solution)/shard_map/ppermute | solution.py:30
  19.3 2.1 %collective-permute-start.11 = (bf16[2,64,256]{2,1,0:T(8,128)(2,1)S(1)}, bf16[2,64,256]{2,1,0:T(8,128)(2,1)S(1)}, u32[]{:S(2)}, u32[]{:S(2)}) collective-permute-start(bf16[2,64,256]{2,1,0:T(8,128)(2,1)S(1)} %collective-permute-done.10.refs_10_), channel_id=1, source_target_pairs={{0,1},{1,0},{2,3},{3,2},{4,5},{5,4},{6,7},{7,6},{8,9},{9,8},{10,11... | collective-permute-start | bytes 196616 | tf_op jit(solution)/shard_map/ppermute | solution.py:30
  20.7 1.4 %collective-permute-start.7 = (bf16[2,64,256]{2,1,0:T(8,128)(2,1)S(1)}, bf16[2,64,256]{2,1,0:T(8,128)(2,1)S(1)}, u32[]{:S(2)}, u32[]{:S(2)}) collective-permute-start(bf16[2,64,256]{2,1,0:T(8,128)(2,1)S(1)} %collective-permute-done.6.refs_6_), channel_id=1, source_target_pairs={{0,1},{1,0},{2,3},{3,2},{4,5},{5,4},{6,7},{7,6},{8,9},{9,8},{10,11... | collective-permute-start | bytes 196616 | tf_op jit(solution)/shard_map/ppermute | solution.py:30
  21.2 1.3 %collective-permute-start.2 = (bf16[1,256,256]{2,1,0:T(8,128)(2,1)S(1)}, bf16[1,256,256]{2,1,0:T(8,128)(2,1)S(1)}, u32[]{:S(2)}, u32[]{:S(2)}) collective-permute-start(bf16[1,256,256]{2,1,0:T(8,128)(2,1)S(1)} %collective-permute-done.1.refs_2_), channel_id=1, source_target_pairs={{0,1},{1,0},{2,3},{3,2},{4,5},{5,4},{6,7},{7,6},{8,9},{9,8},{10,11... | collective-permute-start | bytes 393224 | tf_op jit(solution)/shard_map/ppermute | solution.py:30
  27.0 1.4 %collective-permute-start.12 = (bf16[4,64,256]{2,1,0:T(8,128)(2,1)S(1)}, bf16[4,64,256]{2,1,0:T(8,128)(2,1)S(1)}, u32[]{:S(2)}, u32[]{:S(2)}) collective-permute-start(bf16[4,64,256]{2,1,0:T(8,128)(2,1)S(1)} %get-tuple-element.24), channel_id=1, source_target_pairs={{0,1},{1,0},{2,3},{3,2},{4,5},{5,4},{6,7},{7,6},{8,9},{9,8},{10,11... | collective-permute-start | bytes 393224 | tf_op jit(solution)/shard_map/ppermute | solution.py:30
  27.2 1.4 %collective-permute-start.14 = (bf16[4,64,256]{2,1,0:T(8,128)(2,1)S(1)}, bf16[4,64,256]{2,1,0:T(8,128)(2,1)S(1)}, u32[]{:S(2)}, u32[]{:S(2)}) collective-permute-start(bf16[4,64,256]{2,1,0:T(8,128)(2,1)S(1)} %get-tuple-element.27), channel_id=1, source_target_pairs={{0,1},{1,0},{2,3},{3,2},{4,5},{5,4},{6,7},{7,6},{8,9},{9,8},{10,11... | collective-permute-start | bytes 393224 | tf_op jit(solution)/shard_map/ppermute | solution.py:30
  27.6 2.7 %collective-permute-start.16 = (bf16[4,64,256]{2,1,0:T(8,128)(2,1)S(1)}, bf16[4,64,256]{2,1,0:T(8,128)(2,1)S(1)}, u32[]{:S(2)}, u32[]{:S(2)}) collective-permute-start(bf16[4,64,256]{2,1,0:T(8,128)(2,1)S(1)} %get-tuple-element.30), channel_id=1, source_target_pairs={{0,1},{1,0},{2,3},{3,2},{4,5},{5,4},{6,7},{7,6},{8,9},{9,8},{10,11... | collective-permute-start | bytes 393224 | tf_op jit(solution)/shard_map/ppermute | solution.py:30
  27.7 5.4 %collective-permute-start.18 = (bf16[4,64,256]{2,1,0:T(8,128)(2,1)S(1)}, bf16[4,64,256]{2,1,0:T(8,128)(2,1)S(1)}, u32[]{:S(2)}, u32[]{:S(2)}) collective-permute-start(bf16[4,64,256]{2,1,0:T(8,128)(2,1)S(1)} %get-tuple-element.32), channel_id=1, source_target_pairs={{0,1},{1,0},{2,3},{3,2},{4,5},{5,4},{6,7},{7,6},{8,9},{9,8},{10,11... | collective-permute-start | bytes 393224 | tf_op jit(solution)/shard_map/ppermute | solution.py:30
  28.5 6.5 %collective-permute-start.19 = (bf16[3,64,256]{2,1,0:T(8,128)(2,1)S(1)}, bf16[3,64,256]{2,1,0:T(8,128)(2,1)S(1)}, u32[]{:S(2)}, u32[]{:S(2)}) collective-permute-start(bf16[3,64,256]{2,1,0:T(8,128)(2,1)S(1)} %get-tuple-element.33), channel_id=1, source_target_pairs={{0,8},{8,16},{16,24},{24,0},{1,9},{9,17},{17,25},{25,1},{2,10},{10... | collective-permute-start | bytes 294920 | tf_op jit(solution)/shard_map/ppermute | solution.py:30
  28.7 8.0 %collective-permute-start.20 = (bf16[3,64,256]{2,1,0:T(8,128)(2,1)S(1)}, bf16[3,64,256]{2,1,0:T(8,128)(2,1)S(1)}, u32[]{:S(2)}, u32[]{:S(2)}) collective-permute-start(bf16[3,64,256]{2,1,0:T(8,128)(2,1)S(1)} %get-tuple-element.34), channel_id=1, source_target_pairs={{0,16},{8,24},{16,0},{24,8},{1,17},{9,25},{17,1},{25,9},{2,18},{10... | collective-permute-start | bytes 294920 | tf_op jit(solution)/shard_map/ppermute | solution.py:30
  30.3 6.9 %collective-permute-start.21 = (bf16[3,64,256]{2,1,0:T(8,128)(2,1)S(1)}, bf16[3,64,256]{2,1,0:T(8,128)(2,1)S(1)}, u32[]{:S(2)}, u32[]{:S(2)}) collective-permute-start(bf16[3,64,256]{2,1,0:T(8,128)(2,1)S(1)} %get-tuple-element.35), channel_id=1, source_target_pairs={{0,24},{8,0},{16,8},{24,16},{1,25},{9,1},{17,9},{25,17},{2,26},{10... | collective-permute-start | bytes 294920 | tf_op jit(solution)/shard_map/ppermute | solution.py:30
  33.2 6.0 %collective-permute-start.13 = (bf16[1,64,256]{2,1,0:T(8,128)(2,1)S(1)}, bf16[1,64,256]{2,1,0:T(8,128)(2,1)S(1)}, u32[]{:S(2)}, u32[]{:S(2)}) collective-permute-start(bf16[1,64,256]{2,1,0:T(8,128)(2,1)S(1)} %get-tuple-element.25), channel_id=1, source_target_pairs={{0,8},{8,16},{16,24},{24,0},{1,9},{9,17},{17,25},{25,1},{2,10},{10... | collective-permute-start | bytes 98312 | tf_op jit(solution)/shard_map/ppermute | solution.py:30
  33.2 8.0 %collective-permute-start.15 = (bf16[1,64,256]{2,1,0:T(8,128)(2,1)S(1)}, bf16[1,64,256]{2,1,0:T(8,128)(2,1)S(1)}, u32[]{:S(2)}, u32[]{:S(2)}) collective-permute-start(bf16[1,64,256]{2,1,0:T(8,128)(2,1)S(1)} %get-tuple-element.28), channel_id=1, source_target_pairs={{0,16},{8,24},{16,0},{24,8},{1,17},{9,25},{17,1},{25,9},{2,18},{10... | collective-permute-start | bytes 98312 | tf_op jit(solution)/shard_map/ppermute | solution.py:30
  35.0 6.1 %collective-permute-start.17 = (bf16[1,64,256]{2,1,0:T(8,128)(2,1)S(1)}, bf16[1,64,256]{2,1,0:T(8,128)(2,1)S(1)}, u32[]{:S(2)}, u32[]{:S(2)}) collective-permute-start(bf16[1,64,256]{2,1,0:T(8,128)(2,1)S(1)} %get-tuple-element.31), channel_id=1, source_target_pairs={{0,24},{8,0},{16,8},{24,16},{1,25},{9,1},{17,9},{25,17},{2,26},{10... | collective-permute-start | bytes 98312 | tf_op jit(solution)/shard_map/ppermute | solution.py:30
  37.3 5.8 %collective-permute-start.22 = (bf16[64,256]{1,0:T(8,128)(2,1)S(1)}, bf16[64,256]{1,0:T(8,128)(2,1)S(1)}, u32[]{:S(2)}, u32[]{:S(2)}) collective-permute-start(bf16[64,256]{1,0:T(8,128)(2,1)S(1)} %get-tuple-element.36), channel_id=1, source_target_pairs={{0,2},{1,3},{2,4},{3,5},{4,6},{5,7},{6,0},{7,1},{8,10},{9,11},{10,... | collective-permute-start | bytes 98312 | tf_op jit(solution)/shard_map/ppermute | solution.py:30
  37.3 5.7 %collective-permute-start.23 = (bf16[64,256]{1,0:T(8,128)(2,1)S(1)}, bf16[64,256]{1,0:T(8,128)(2,1)S(1)}, u32[]{:S(2)}, u32[]{:S(2)}) collective-permute-start(bf16[64,256]{1,0:T(8,128)(2,1)S(1)} %get-tuple-element.37), channel_id=1, source_target_pairs={{0,4},{1,5},{2,6},{3,7},{4,0},{5,1},{6,2},{7,3},{8,12},{9,13},{10,... | collective-permute-start | bytes 98312 | tf_op jit(solution)/shard_map/ppermute | solution.py:30
  39.2 4.4 %collective-permute-start.24 = (bf16[64,256]{1,0:T(8,128)(2,1)S(1)}, bf16[64,256]{1,0:T(8,128)(2,1)S(1)}, u32[]{:S(2)}, u32[]{:S(2)}) collective-permute-start(bf16[64,256]{1,0:T(8,128)(2,1)S(1)} %get-tuple-element.38), channel_id=1, source_target_pairs={{0,6},{1,7},{2,0},{3,1},{4,2},{5,3},{6,4},{7,5},{8,14},{9,15},{10,... | collective-permute-start | bytes 98312 | tf_op jit(solution)/shard_map/ppermute | solution.py:30
  (7 other events, 61.8 us)

commit v4 on v3

--- a/solution.py
+++ b/solution.py
@@ -10,7 +10,7 @@
 
 
 CORES = 2
-UNROLL = 20
+UNROLL = 40
 DIRECT = (0, 1)
 VMEM_BYTES = 67043328
 SLACK = 1 << 20
@@ -37,6 +37,22 @@
 
 def round_z(layer, k, depth):
     return lax.rem(layer + k, depth) if isinstance(k, jax.Array) else (layer + k) % depth
+
+
+def far_layer(group, n, groups, depth):
+    return len(DIRECT) + group // 2 * (2 * (depth - len(DIRECT)) // groups) + n
+
+
+def fetch_far(value, n):
+    groups, sectors = lax.axis_size("mpo"), lax.axis_size("sec")
+    depth = sectors // CORES
+
+    def target(i):
+        group, sec = divmod(i, sectors)
+        layer = partner(sec // CORES, far_layer(group, n, groups, depth), depth)
+        return (group * depth + layer) * CORES + sec % CORES
+
+    return lax.ppermute(value, ("mpo", "sec"), [(i, target(i)) for i in range(groups * sectors)])
 
 
 def along_mpo(value, j):
@@ -87,11 +103,12 @@
 
 
 def take_rows(own, part):
-    quarter = part.shape[1]
-    part[...] = own[:, pl.ds(pl.multiple_of(lax.axis_index("mpo") * quarter, quarter), quarter)]
-
-
-def products(task_in, task_out, blocks, left, right, acc, *stage):
+    half = part.shape[1]
+    start = lax.rem(lax.axis_index("mpo"), 2) * half
+    part[...] = own[:, pl.ds(pl.multiple_of(start, half), half)]
+
+
+def products(ids, blocks, left, right, acc, *stage):
     tasks = left.shape[0]
     limit = stage[0].shape[1] if stage else UNROLL
     unroll = max(n for n in range(1, limit + 1) if tasks % n == 0)
@@ -106,11 +123,16 @@
         copy.wait()
         return target[which, u]
 
+    lanes = lax.broadcasted_iota(jnp.int32, ids.shape, 1)
+    sectors = blocks.shape[0]
+
     def step(n, _):
         for u in range(unroll):
             t = n * unroll + u
-            middle = jnp.dot(fetch(0, t, u), blocks[task_in[t]], preferred_element_type=F32).astype(BF16)
-            acc[task_out[t]] += lax.dot_general(
+            code = jnp.max(jnp.where(lanes == t, ids[...], 0.0)).astype(jnp.int32)
+            source, target = lax.div(code, sectors), lax.rem(code, sectors)
+            middle = jnp.dot(fetch(0, t, u), blocks[source], preferred_element_type=F32).astype(BF16)
+            acc[target] += lax.dot_general(
                 middle, fetch(1, t, u), (((1,), (1,)), ((), ())), preferred_element_type=F32
             )
         return 0
@@ -118,7 +140,7 @@
     lax.fori_loop(0, tasks // unroll, step, 0)
 
 
-def contract(task_in, task_out, *refs):
+def contract(ids, *refs):
     groups = lax.axis_size("mpo")
     direct, refs = refs[: CORES * len(DIRECT)], refs[CORES * len(DIRECT) :]
     spread, (left, right, _, acc), refs = refs[: CORES * groups], refs[CORES * groups :][:4], refs[CORES * groups + 4 :]
@@ -131,14 +153,16 @@
         base = partner(layer, k, depth, back=True) * CORES
         blocks[base + core] = direct[CORES * n][0]
         blocks[base + 1 - core] = direct[CORES * n + 1][0]
-    for n in range(spread[0].shape[0]):
-        base = partner(layer, len(DIRECT) + n, depth, back=True) * CORES
-        for j in range(groups):
-            start = lax.rem(group + groups - j, groups) * quarter
-            rows = pl.ds(pl.multiple_of(start, quarter), quarter)
+    rounds, half = spread[0].shape[:2]
+    for j in range(groups):
+        source = lax.rem(group + groups - j, groups)
+        rows = pl.ds(pl.multiple_of(lax.rem(source, 2) * half, half), half)
+        for n in range(rounds):
+            k = len(DIRECT) + lax.div(source, 2) * rounds + n
+            base = partner(layer, k, depth, back=True) * CORES
             blocks[base + core, rows] = spread[CORES * j][n]
             blocks[base + 1 - core, rows] = spread[CORES * j + 1][n]
-    products(task_in, task_out, blocks, left, right, acc, *stage)
+    products(ids, blocks, left, right, acc, *stage)
 
     def put(k, _):
         base = round_z(layer, k, depth) * CORES
@@ -186,10 +210,12 @@
         return (row_ids < left_dims[:, None, None]) & (col_ids < right_dims[:, None, None])
 
     own = jnp.where(live(wavefunction.shape, 0), wavefunction, jnp.zeros_like(wavefunction))
-    part = call(take_rows, array((1, quarter, cols), BF16), (own,))
-    far = [along_z(part, k) for k in range(len(DIRECT), depth)]
+    part = call(take_rows, array((1, rows // 2, cols), BF16), (own,))
+    assert groups % 2 == 0 and 2 * (depth - len(DIRECT)) % groups == 0
+    rounds = 2 * (depth - len(DIRECT)) // groups
+    far = [fetch_far(part, n) for n in range(rounds)]
     near = [own, *(along_z(own, k) for k in DIRECT[1:])]
-    pieces = [jnp.concatenate(far, axis=0)]
+    pieces = [jnp.concatenate(far, axis=0) if rounds > 1 else far[0]]
     pieces += [along_mpo(pieces[0], j) for j in range(1, groups)]
     blocks = [b for block in near for b in (block, swap(block))]
     blocks += [b for piece in pieces for b in (piece, swap(piece))]
@@ -205,7 +231,8 @@
     streamed = 16 * sums.size > VMEM_BYTES
     if streamed:
         scratch += (VMEM((2, 4, rows, cols), BF16), pltpu.SemaphoreType.DMA((2, 4)))
-    operands = (task_in, task_out, *blocks, *work, acc)
+    ids = (task_in * sectors + task_out).astype(F32)[None]
+    operands = (ids, *blocks, *work, acc)
     last = len(operands) - 1
     piece = (depth, quarter, cols)
     _, *pieces = call(
@@ -213,7 +240,6 @@
         (sums, *(array(piece, BF16),) * groups, *(array(piece, F32),) * groups),
         operands,
         scratch,
-        scalars=2,
         cost=cost,
         aliases={last: 0},
         streamed=(last - 2, last - 1) if streamed else (),

time: 44.4 us -> 43.6 us (0.982)
  waiting for transfers between devices: 14.8 us -> 12 us
  starting transfers between devices: 21.6 us -> 24.3 us
  Pallas kernels: 4.73 us -> 4.03 us
    ppermute x25 -> x23, waiting for transfers between devices: 14.8 us -> 10.5 us  [send(): lax.ppermute(value, axis, [(i, target(i)) for i in range(lax.axis_size(ax...]
    ppermute x0 -> x1, starting transfers between devices: none -> 4.13 us  [fetch_far(): lax.ppermute(value, ('mpo', 'sec'), [(i, target(i)) for i in range(groups...]
    ppermute x0 -> x1, waiting for transfers between devices: none -> 1.47 us  [fetch_far(): lax.ppermute(value, ('mpo', 'sec'), [(i, target(i)) for i in range(groups...]
    ppermute x25 -> x23, starting transfers between devices: 21.6 us -> 20.1 us  [send(): lax.ppermute(value, axis, [(i, target(i)) for i in range(lax.axis_size(ax...]
    pallas_call x8, Pallas kernels: 4.73 us -> 4.03 us  [call(): results = run(*operands)]
  transfers between devices with their start and end apart: 25 -> 24, of which waited for: 14 -> 13; matrix products, arithmetic and copies ran while one was open for 0% -> 0% of each run, Pallas kernels for 1% -> 1%
where the time goes in v4:
time: 43.6 us; the launch traced here: 43.4 us
  starting transfers between devices  24.3 us (56%)
  waiting for transfers between devices  12 us (28%)
  Pallas kernels  4.03 us (9%)
  other arithmetic  1.66 us (4%)
  between operations  1.46 us (3%)
    ppermute x23, starting transfers between devices, send(): lax.ppermute(value, axis, [(i, target(i)) for i in range(lax.axis_size(ax...  20.1 us
    ppermute x23, waiting for transfers between devices, send(): lax.ppermute(value, axis, [(i, target(i)) for i in range(lax.axis_size(ax...  10.5 us
    ppermute x1, starting transfers between devices, fetch_far(): lax.ppermute(value, ('mpo', 'sec'), [(i, target(i)) for i in range(groups...  4.13 us
    pallas_call x8, Pallas kernels, call(): results = run(*operands)  4.03 us
    ppermute x1, waiting for transfers between devices, fetch_far(): lax.ppermute(value, ('mpo', 'sec'), [(i, target(i)) for i in range(groups...  1.47 us
    select_n x1, other arithmetic, device_step(): jnp.where(live(wavefunction.shape, 0), wavefunction, jnp.zeros_like(wavef...  0.95 us
  transfers between devices with their start and end apart: 24, of which 13 were waited for; matrix products, arithmetic and copies ran while one was open for 0% of the time, Pallas kernels for 1%

profile of v4, /device:TPU:0, one launch (start us, length us, event | category | flops | bytes accessed | tf_op | source)
XLA Modules:
  0.0 43.4 jit_solution(9450307283772347838)
XLA Ops:
  1.3 1.0 %fusion.1.own.refs_0_ = bf16[1,256,256]{2,1,0:T(8,128)(2,1)S(1)} fusion(bf16[1,256,256]{2,1,0:T(8,128)(2,1)} %param.7, s32[]{:T(128)} %bitcast.9, s32[]{:T(128)} %bitcast.7), kind=kLoop, calls=%fused_computation.3 | loop fusion | flops 262144 | bytes 262152 | tf_op jit(solution)/shard_map/jit(_where)/select_n | solution.py:212
  2.4 4.1 %collective-permute-start.3 = (bf16[1,128,256]{2,1,0:T(8,128)(2,1)S(1)}, bf16[1,128,256]{2,1,0:T(8,128)(2,1)S(1)}, u32[]{:S(2)}, u32[]{:S(2)}) collective-permute-start(bf16[1,128,256]{2,1,0:T(8,128)(2,1)S(1)} %shard_map.73), channel_id=1, source_target_pairs={{0,4},{1,5},{2,6},{3,7},{4,0},{5,1},{6,2},{7,3},{8,12},{9,13},{10,... | collective-permute-start | bytes 196616 | tf_op jit(solution)/shard_map/ppermute | solution.py:55
  6.5 1.6 %collective-permute-start.1 = (bf16[1,256,256]{2,1,0:T(8,128)(2,1)S(1)}, bf16[1,256,256]{2,1,0:T(8,128)(2,1)S(1)}, u32[]{:S(2)}, u32[]{:S(2)}) collective-permute-start(bf16[1,256,256]{2,1,0:T(8,128)(2,1)S(1)} %fusion.1.own.refs_0_), channel_id=1, source_target_pairs={{0,2},{1,3},{2,0},{3,1},{4,6},{5,7},{6,4},{7,5},{8,10},{9,11},{10,... | collective-permute-start | bytes 393224 | tf_op jit(solution)/shard_map/ppermute | solution.py:30
  8.1 1.5 %collective-permute-done.3.refs_4_ = bf16[1,128,256]{2,1,0:T(8,128)(2,1)S(1)} collective-permute-done((bf16[1,128,256]{2,1,0:T(8,128)(2,1)S(1)}, bf16[1,128,256]{2,1,0:T(8,128)(2,1)S(1)}, u32[]{:S(2)}, u32[]{:S(2)}) %collective-permute-start.3) | collective-permute-done | bytes 65568 | tf_op jit(solution)/shard_map/ppermute | solution.py:55
  9.5 3.6 %collective-permute-start.9 = (bf16[1,128,256]{2,1,0:T(8,128)(2,1)S(1)}, bf16[1,128,256]{2,1,0:T(8,128)(2,1)S(1)}, u32[]{:S(2)}, u32[]{:S(2)}) collective-permute-start(bf16[1,128,256]{2,1,0:T(8,128)(2,1)S(1)} %collective-permute-done.3.refs_4_), channel_id=1, source_target_pairs={{0,24},{8,0},{16,8},{24,16},{1,25},{9,1},{17,9},{25,17},{2,26},{10... | collective-permute-start | bytes 196616 | tf_op jit(solution)/shard_map/ppermute | solution.py:30
  13.1 1.1 %collective-permute-start.5 = (bf16[1,128,256]{2,1,0:T(8,128)(2,1)S(1)}, bf16[1,128,256]{2,1,0:T(8,128)(2,1)S(1)}, u32[]{:S(2)}, u32[]{:S(2)}) collective-permute-start(bf16[1,128,256]{2,1,0:T(8,128)(2,1)S(1)} %collective-permute-done.3.refs_4_), channel_id=1, source_target_pairs={{0,8},{8,16},{16,24},{24,0},{1,9},{9,17},{17,25},{25,1},{2,10},{10... | collective-permute-start | bytes 196616 | tf_op jit(solution)/shard_map/ppermute | solution.py:30
  14.4 0.7 %collective-permute-done.9.refs_10_ = bf16[1,128,256]{2,1,0:T(8,128)(2,1)S(1)} collective-permute-done((bf16[1,128,256]{2,1,0:T(8,128)(2,1)S(1)}, bf16[1,128,256]{2,1,0:T(8,128)(2,1)S(1)}, u32[]{:S(2)}, u32[]{:S(2)}) %collective-permute-start.9) | collective-permute-done | bytes 65568 | tf_op jit(solution)/shard_map/ppermute | solution.py:30
  15.0 2.4 %collective-permute-done.7.refs_8_ = bf16[1,128,256]{2,1,0:T(8,128)(2,1)S(1)} collective-permute-done((bf16[1,128,256]{2,1,0:T(8,128)(2,1)S(1)}, bf16[1,128,256]{2,1,0:T(8,128)(2,1)S(1)}, u32[]{:S(2)}, u32[]{:S(2)}) %collective-permute-start.7) | collective-permute-done | bytes 65568 | tf_op jit(solution)/shard_map/ppermute | solution.py:30
  17.4 0.9 %collective-permute-done.5.refs_6_ = bf16[1,128,256]{2,1,0:T(8,128)(2,1)S(1)} collective-permute-done((bf16[1,128,256]{2,1,0:T(8,128)(2,1)S(1)}, bf16[1,128,256]{2,1,0:T(8,128)(2,1)S(1)}, u32[]{:S(2)}, u32[]{:S(2)}) %collective-permute-start.5) | collective-permute-done | bytes 65568 | tf_op jit(solution)/shard_map/ppermute | solution.py:30
  18.3 0.5 %collective-permute-start.6 = (bf16[1,128,256]{2,1,0:T(8,128)(2,1)S(1)}, bf16[1,128,256]{2,1,0:T(8,128)(2,1)S(1)}, u32[]{:S(2)}, u32[]{:S(2)}) collective-permute-start(bf16[1,128,256]{2,1,0:T(8,128)(2,1)S(1)} %collective-permute-done.5.refs_6_), channel_id=1, source_target_pairs={{0,1},{1,0},{2,3},{3,2},{4,5},{5,4},{6,7},{7,6},{8,9},{9,8},{10,11... | collective-permute-start | bytes 196616 | tf_op jit(solution)/shard_map/ppermute | solution.py:30
  18.9 0.6 %collective-permute-done.8.refs_9_ = bf16[1,128,256]{2,1,0:T(8,128)(2,1)S(1)} collective-permute-done((bf16[1,128,256]{2,1,0:T(8,128)(2,1)S(1)}, bf16[1,128,256]{2,1,0:T(8,128)(2,1)S(1)}, u32[]{:S(2)}, u32[]{:S(2)}) %collective-permute-start.8) | collective-permute-done | bytes 65568 | tf_op jit(solution)/shard_map/ppermute | solution.py:30
  19.7 0.4 %collective-permute-done.2.refs_3_ = bf16[1,256,256]{2,1,0:T(8,128)(2,1)S(1)} collective-permute-done((bf16[1,256,256]{2,1,0:T(8,128)(2,1)S(1)}, bf16[1,256,256]{2,1,0:T(8,128)(2,1)S(1)}, u32[]{:S(2)}, u32[]{:S(2)}) %collective-permute-start.2) | collective-permute-done | bytes 131104 | tf_op jit(solution)/shard_map/ppermute | solution.py:30
  20.2 3.7 %shard_map.75 = (f32[8,256,256]{2,1,0:T(8,128)S(1)}, bf16[4,64,256]{2,1,0:T(8,128)(2,1)S(1)}, bf16[4,64,256]{2,1,0:T(8,128)(2,1)S(1)}, bf16[4,64,256]{2,1,0:T(8,...) custom-call(f32[1,40]{1,0:T(1,128)S(1)} %convert_bitcast_fusion.ids,, ...), custom_call_target="tpu_custom_call", output_to_operand_aliasing={{0}: (15, {})} | custom-call | flops 2684354560 | bytes 10485760 | tf_op jit(solution)/shard_map/pallas_call | solution.py:97
  24.1 0.4 collective-permute-start.13
  25.7 2.0 %collective-permute-start.19 = (bf16[3,64,256]{2,1,0:T(8,128)(2,1)S(1)}, bf16[3,64,256]{2,1,0:T(8,128)(2,1)S(1)}, u32[]{:S(2)}, u32[]{:S(2)}) collective-permute-start(bf16[3,64,256]{2,1,0:T(8,128)(2,1)S(1)} %get-tuple-element.34), channel_id=1, source_target_pairs={{0,16},{8,24},{16,0},{24,8},{1,17},{9,25},{17,1},{25,9},{2,18},{10... | collective-permute-start | bytes 294920 | tf_op jit(solution)/shard_map/ppermute | solution.py:30
  27.7 2.9 %collective-permute-start.20 = (bf16[3,64,256]{2,1,0:T(8,128)(2,1)S(1)}, bf16[3,64,256]{2,1,0:T(8,128)(2,1)S(1)}, u32[]{:S(2)}, u32[]{:S(2)}) collective-permute-start(bf16[3,64,256]{2,1,0:T(8,128)(2,1)S(1)} %get-tuple-element.35), channel_id=1, source_target_pairs={{0,24},{8,0},{16,8},{24,16},{1,25},{9,1},{17,9},{25,17},{2,26},{10... | collective-permute-start | bytes 294920 | tf_op jit(solution)/shard_map/ppermute | solution.py:30
  30.5 0.6 %collective-permute-start.14 = (bf16[1,64,256]{2,1,0:T(8,128)(2,1)S(1)}, bf16[1,64,256]{2,1,0:T(8,128)(2,1)S(1)}, u32[]{:S(2)}, u32[]{:S(2)}) collective-permute-start(bf16[1,64,256]{2,1,0:T(8,128)(2,1)S(1)} %get-tuple-element.28), channel_id=1, source_target_pairs={{0,16},{8,24},{16,0},{24,8},{1,17},{9,25},{17,1},{25,9},{2,18},{10... | collective-permute-start | bytes 98312 | tf_op jit(solution)/shard_map/ppermute | solution.py:30
  31.4 2.1 %collective-permute-start.16 = (bf16[1,64,256]{2,1,0:T(8,128)(2,1)S(1)}, bf16[1,64,256]{2,1,0:T(8,128)(2,1)S(1)}, u32[]{:S(2)}, u32[]{:S(2)}) collective-permute-start(bf16[1,64,256]{2,1,0:T(8,128)(2,1)S(1)} %get-tuple-element.31), channel_id=1, source_target_pairs={{0,24},{8,0},{16,8},{24,16},{1,25},{9,1},{17,9},{25,17},{2,26},{10... | collective-permute-start | bytes 98312 | tf_op jit(solution)/shard_map/ppermute | solution.py:30
  33.5 1.0 %collective-permute-done.20.refs_4_ = bf16[3,64,256]{2,1,0:T(8,128)(2,1)S(1)} collective-permute-done((bf16[3,64,256]{2,1,0:T(8,128)(2,1)S(1)}, bf16[3,64,256]{2,1,0:T(8,128)(2,1)S(1)}, u32[]{:S(2)}, u32[]{:S(2)}) %collective-permute-start.20) | collective-permute-done | bytes 98336 | tf_op jit(solution)/shard_map/ppermute | solution.py:30
  34.8 4.1 %collective-permute-start.22 = (bf16[64,256]{1,0:T(8,128)(2,1)S(1)}, bf16[64,256]{1,0:T(8,128)(2,1)S(1)}, u32[]{:S(2)}, u32[]{:S(2)}) collective-permute-start(bf16[64,256]{1,0:T(8,128)(2,1)S(1)} %get-tuple-element.37), channel_id=1, source_target_pairs={{0,4},{1,5},{2,6},{3,7},{4,0},{5,1},{6,2},{7,3},{8,12},{9,13},{10,... | collective-permute-start | bytes 98312 | tf_op jit(solution)/shard_map/ppermute | solution.py:30
  39.0 1.4 %collective-permute-done.21 = bf16[64,256]{1,0:T(8,128)(2,1)S(1)} collective-permute-done((bf16[64,256]{1,0:T(8,128)(2,1)S(1)}, bf16[64,256]{1,0:T(8,128)(2,1)S(1)}, u32[]{:S(2)}, u32[]{:S(2)}) %collective-permute-start.21) | collective-permute-done | bytes 32800 | tf_op jit(solution)/shard_map/ppermute | solution.py:30
  40.4 0.7 %collective-permute-done.22 = bf16[64,256]{1,0:T(8,128)(2,1)S(1)} collective-permute-done((bf16[64,256]{1,0:T(8,128)(2,1)S(1)}, bf16[64,256]{1,0:T(8,128)(2,1)S(1)}, u32[]{:S(2)}, u32[]{:S(2)}) %collective-permute-start.22) | collective-permute-done | bytes 32800 | tf_op jit(solution)/shard_map/ppermute | solution.py:30
  41.1 1.7 %collective-permute-done.23 = bf16[64,256]{1,0:T(8,128)(2,1)S(1)} collective-permute-done((bf16[64,256]{1,0:T(8,128)(2,1)S(1)}, bf16[64,256]{1,0:T(8,128)(2,1)S(1)}, u32[]{:S(2)}, u32[]{:S(2)}) %collective-permute-start.23) | collective-permute-done | bytes 32800 | tf_op jit(solution)/shard_map/ppermute | solution.py:30
  42.8 0.7 %fusion.3 = bf16[1,64,256]{2,1,0:T(8,128)(2,1)} fusion(bf16[64,256]{1,0:T(8,128)(2,1)S(1)} %collective-permute-done.23, bf16[64,256]{1,0:T(8,128)(2,1)S(1)} %collective-permute-done.22, f32[64,256]{1,0:T(8,128)S(1)} %shard_map.79, bf16[64,256]{1,0:T(8,128)(2,1)S(1)} %collective-permute-done.21, s32[]{:T(128)} %bitcast.8, pred[64]{0:T(512)(128)(4,1)S(1)} %add_compare_fusion), kind=kLoop, calls=%fused_computation.7 | loop fusion | flops 163840 | bytes 196676 | tf_op jit(solution)/shard_map/convert_element_type | solution.py:266
  (50 shorter events, 2.5 us)
Async XLA Ops:
  2.4 7.2 %collective-permute-start.3 = (bf16[1,128,256]{2,1,0:T(8,128)(2,1)S(1)}, bf16[1,128,256]{2,1,0:T(8,128)(2,1)S(1)}, u32[]{:S(2)}, u32[]{:S(2)}) collective-permute-start(bf16[1,128,256]{2,1,0:T(8,128)(2,1)S(1)} %shard_map.73), channel_id=1, source_target_pairs={{0,4},{1,5},{2,6},{3,7},{4,0},{5,1},{6,2},{7,3},{8,12},{9,13},{10,... | collective-permute-start | bytes 196616 | tf_op jit(solution)/shard_map/ppermute | solution.py:55
  6.5 12.3 %collective-permute-start.1 = (bf16[1,256,256]{2,1,0:T(8,128)(2,1)S(1)}, bf16[1,256,256]{2,1,0:T(8,128)(2,1)S(1)}, u32[]{:S(2)}, u32[]{:S(2)}) collective-permute-start(bf16[1,256,256]{2,1,0:T(8,128)(2,1)S(1)} %fusion.1.own.refs_0_), channel_id=1, source_target_pairs={{0,2},{1,3},{2,0},{3,1},{4,6},{5,7},{6,4},{7,5},{8,10},{9,11},{10,... | collective-permute-start | bytes 393224 | tf_op jit(solution)/shard_map/ppermute | solution.py:30
  9.5 5.5 %collective-permute-start.9 = (bf16[1,128,256]{2,1,0:T(8,128)(2,1)S(1)}, bf16[1,128,256]{2,1,0:T(8,128)(2,1)S(1)}, u32[]{:S(2)}, u32[]{:S(2)}) collective-permute-start(bf16[1,128,256]{2,1,0:T(8,128)(2,1)S(1)} %collective-permute-done.3.refs_4_), channel_id=1, source_target_pairs={{0,24},{8,0},{16,8},{24,16},{1,25},{9,1},{17,9},{25,17},{2,26},{10... | collective-permute-start | bytes 196616 | tf_op jit(solution)/shard_map/ppermute | solution.py:30
  13.1 4.3 %collective-permute-start.7 = (bf16[1,128,256]{2,1,0:T(8,128)(2,1)S(1)}, bf16[1,128,256]{2,1,0:T(8,128)(2,1)S(1)}, u32[]{:S(2)}, u32[]{:S(2)}) collective-permute-start(bf16[1,128,256]{2,1,0:T(8,128)(2,1)S(1)} %collective-permute-done.3.refs_4_), channel_id=1, source_target_pairs={{0,16},{8,24},{16,0},{24,8},{1,17},{9,25},{17,1},{25,9},{2,18},{10... | collective-permute-start | bytes 196616 | tf_op jit(solution)/shard_map/ppermute | solution.py:30
  13.1 5.2 %collective-permute-start.5 = (bf16[1,128,256]{2,1,0:T(8,128)(2,1)S(1)}, bf16[1,128,256]{2,1,0:T(8,128)(2,1)S(1)}, u32[]{:S(2)}, u32[]{:S(2)}) collective-permute-start(bf16[1,128,256]{2,1,0:T(8,128)(2,1)S(1)} %collective-permute-done.3.refs_4_), channel_id=1, source_target_pairs={{0,8},{8,16},{16,24},{24,0},{1,9},{9,17},{17,25},{25,1},{2,10},{10... | collective-permute-start | bytes 196616 | tf_op jit(solution)/shard_map/ppermute | solution.py:30
  14.2 4.1 %collective-permute-start.4 = (bf16[1,128,256]{2,1,0:T(8,128)(2,1)S(1)}, bf16[1,128,256]{2,1,0:T(8,128)(2,1)S(1)}, u32[]{:S(2)}, u32[]{:S(2)}) collective-permute-start(bf16[1,128,256]{2,1,0:T(8,128)(2,1)S(1)} %collective-permute-done.3.refs_4_), channel_id=1, source_target_pairs={{0,1},{1,0},{2,3},{3,2},{4,5},{5,4},{6,7},{7,6},{8,9},{9,8},{10,11... | collective-permute-start | bytes 196616 | tf_op jit(solution)/shard_map/ppermute | solution.py:30
  15.0 3.9 %collective-permute-start = (bf16[1,256,256]{2,1,0:T(8,128)(2,1)S(1)}, bf16[1,256,256]{2,1,0:T(8,128)(2,1)S(1)}, u32[]{:S(2)}, u32[]{:S(2)}) collective-permute-start(bf16[1,256,256]{2,1,0:T(8,128)(2,1)S(1)} %fusion.1.own.refs_0_), channel_id=1, source_target_pairs={{0,1},{1,0},{2,3},{3,2},{4,5},{5,4},{6,7},{7,6},{8,9},{9,8},{10,11... | collective-permute-start | bytes 393224 | tf_op jit(solution)/shard_map/ppermute | solution.py:30
  17.4 1.5 %collective-permute-start.10 = (bf16[1,128,256]{2,1,0:T(8,128)(2,1)S(1)}, bf16[1,128,256]{2,1,0:T(8,128)(2,1)S(1)}, u32[]{:S(2)}, u32[]{:S(2)}) collective-permute-start(bf16[1,128,256]{2,1,0:T(8,128)(2,1)S(1)} %collective-permute-done.9.refs_10_), channel_id=1, source_target_pairs={{0,1},{1,0},{2,3},{3,2},{4,5},{5,4},{6,7},{7,6},{8,9},{9,8},{10,11... | collective-permute-start | bytes 196616 | tf_op jit(solution)/shard_map/ppermute | solution.py:30
  18.3 1.3 %collective-permute-start.8 = (bf16[1,128,256]{2,1,0:T(8,128)(2,1)S(1)}, bf16[1,128,256]{2,1,0:T(8,128)(2,1)S(1)}, u32[]{:S(2)}, u32[]{:S(2)}) collective-permute-start(bf16[1,128,256]{2,1,0:T(8,128)(2,1)S(1)} %collective-permute-done.7.refs_8_), channel_id=1, source_target_pairs={{0,1},{1,0},{2,3},{3,2},{4,5},{5,4},{6,7},{7,6},{8,9},{9,8},{10,11... | collective-permute-start | bytes 196616 | tf_op jit(solution)/shard_map/ppermute | solution.py:30
  18.3 1.4 %collective-permute-start.6 = (bf16[1,128,256]{2,1,0:T(8,128)(2,1)S(1)}, bf16[1,128,256]{2,1,0:T(8,128)(2,1)S(1)}, u32[]{:S(2)}, u32[]{:S(2)}) collective-permute-start(bf16[1,128,256]{2,1,0:T(8,128)(2,1)S(1)} %collective-permute-done.5.refs_6_), channel_id=1, source_target_pairs={{0,1},{1,0},{2,3},{3,2},{4,5},{5,4},{6,7},{7,6},{8,9},{9,8},{10,11... | collective-permute-start | bytes 196616 | tf_op jit(solution)/shard_map/ppermute | solution.py:30
  18.8 1.3 %collective-permute-start.2 = (bf16[1,256,256]{2,1,0:T(8,128)(2,1)S(1)}, bf16[1,256,256]{2,1,0:T(8,128)(2,1)S(1)}, u32[]{:S(2)}, u32[]{:S(2)}) collective-permute-start(bf16[1,256,256]{2,1,0:T(8,128)(2,1)S(1)} %collective-permute-done.1.refs_2_), channel_id=1, source_target_pairs={{0,1},{1,0},{2,3},{3,2},{4,5},{5,4},{6,7},{7,6},{8,9},{9,8},{10,11... | collective-permute-start | bytes 393224 | tf_op jit(solution)/shard_map/ppermute | solution.py:30
  23.9 1.4 %collective-permute-start.11 = (bf16[4,64,256]{2,1,0:T(8,128)(2,1)S(1)}, bf16[4,64,256]{2,1,0:T(8,128)(2,1)S(1)}, u32[]{:S(2)}, u32[]{:S(2)}) collective-permute-start(bf16[4,64,256]{2,1,0:T(8,128)(2,1)S(1)} %get-tuple-element.24), channel_id=1, source_target_pairs={{0,1},{1,0},{2,3},{3,2},{4,5},{5,4},{6,7},{7,6},{8,9},{9,8},{10,11... | collective-permute-start | bytes 393224 | tf_op jit(solution)/shard_map/ppermute | solution.py:30
  24.1 1.5 %collective-permute-start.13 = (bf16[4,64,256]{2,1,0:T(8,128)(2,1)S(1)}, bf16[4,64,256]{2,1,0:T(8,128)(2,1)S(1)}, u32[]{:S(2)}, u32[]{:S(2)}) collective-permute-start(bf16[4,64,256]{2,1,0:T(8,128)(2,1)S(1)} %get-tuple-element.27), channel_id=1, source_target_pairs={{0,1},{1,0},{2,3},{3,2},{4,5},{5,4},{6,7},{7,6},{8,9},{9,8},{10,11... | collective-permute-start | bytes 393224 | tf_op jit(solution)/shard_map/ppermute | solution.py:30
  24.5 3.2 %collective-permute-start.15 = (bf16[4,64,256]{2,1,0:T(8,128)(2,1)S(1)}, bf16[4,64,256]{2,1,0:T(8,128)(2,1)S(1)}, u32[]{:S(2)}, u32[]{:S(2)}) collective-permute-start(bf16[4,64,256]{2,1,0:T(8,128)(2,1)S(1)} %get-tuple-element.30), channel_id=1, source_target_pairs={{0,1},{1,0},{2,3},{3,2},{4,5},{5,4},{6,7},{7,6},{8,9},{9,8},{10,11... | collective-permute-start | bytes 393224 | tf_op jit(solution)/shard_map/ppermute | solution.py:30
  24.6 5.9 %collective-permute-start.17 = (bf16[4,64,256]{2,1,0:T(8,128)(2,1)S(1)}, bf16[4,64,256]{2,1,0:T(8,128)(2,1)S(1)}, u32[]{:S(2)}, u32[]{:S(2)}) collective-permute-start(bf16[4,64,256]{2,1,0:T(8,128)(2,1)S(1)} %get-tuple-element.32), channel_id=1, source_target_pairs={{0,1},{1,0},{2,3},{3,2},{4,5},{5,4},{6,7},{7,6},{8,9},{9,8},{10,11... | collective-permute-start | bytes 393224 | tf_op jit(solution)/shard_map/ppermute | solution.py:30
  25.3 6.0 %collective-permute-start.18 = (bf16[3,64,256]{2,1,0:T(8,128)(2,1)S(1)}, bf16[3,64,256]{2,1,0:T(8,128)(2,1)S(1)}, u32[]{:S(2)}, u32[]{:S(2)}) collective-permute-start(bf16[3,64,256]{2,1,0:T(8,128)(2,1)S(1)} %get-tuple-element.33), channel_id=1, source_target_pairs={{0,8},{8,16},{16,24},{24,0},{1,9},{9,17},{17,25},{25,1},{2,10},{10... | collective-permute-start | bytes 294920 | tf_op jit(solution)/shard_map/ppermute | solution.py:30
  25.7 7.9 %collective-permute-start.19 = (bf16[3,64,256]{2,1,0:T(8,128)(2,1)S(1)}, bf16[3,64,256]{2,1,0:T(8,128)(2,1)S(1)}, u32[]{:S(2)}, u32[]{:S(2)}) collective-permute-start(bf16[3,64,256]{2,1,0:T(8,128)(2,1)S(1)} %get-tuple-element.34), channel_id=1, source_target_pairs={{0,16},{8,24},{16,0},{24,8},{1,17},{9,25},{17,1},{25,9},{2,18},{10... | collective-permute-start | bytes 294920 | tf_op jit(solution)/shard_map/ppermute | solution.py:30
  27.7 6.9 %collective-permute-start.20 = (bf16[3,64,256]{2,1,0:T(8,128)(2,1)S(1)}, bf16[3,64,256]{2,1,0:T(8,128)(2,1)S(1)}, u32[]{:S(2)}, u32[]{:S(2)}) collective-permute-start(bf16[3,64,256]{2,1,0:T(8,128)(2,1)S(1)} %get-tuple-element.35), channel_id=1, source_target_pairs={{0,24},{8,0},{16,8},{24,16},{1,25},{9,1},{17,9},{25,17},{2,26},{10... | collective-permute-start | bytes 294920 | tf_op jit(solution)/shard_map/ppermute | solution.py:30
  30.5 8.3 %collective-permute-start.12 = (bf16[1,64,256]{2,1,0:T(8,128)(2,1)S(1)}, bf16[1,64,256]{2,1,0:T(8,128)(2,1)S(1)}, u32[]{:S(2)}, u32[]{:S(2)}) collective-permute-start(bf16[1,64,256]{2,1,0:T(8,128)(2,1)S(1)} %get-tuple-element.25), channel_id=1, source_target_pairs={{0,8},{8,16},{16,24},{24,0},{1,9},{9,17},{17,25},{25,1},{2,10},{10... | collective-permute-start | bytes 98312 | tf_op jit(solution)/shard_map/ppermute | solution.py:30
  30.5 8.4 %collective-permute-start.14 = (bf16[1,64,256]{2,1,0:T(8,128)(2,1)S(1)}, bf16[1,64,256]{2,1,0:T(8,128)(2,1)S(1)}, u32[]{:S(2)}, u32[]{:S(2)}) collective-permute-start(bf16[1,64,256]{2,1,0:T(8,128)(2,1)S(1)} %get-tuple-element.28), channel_id=1, source_target_pairs={{0,16},{8,24},{16,0},{24,8},{1,17},{9,25},{17,1},{25,9},{2,18},{10... | collective-permute-start | bytes 98312 | tf_op jit(solution)/shard_map/ppermute | solution.py:30
  31.4 7.6 %collective-permute-start.16 = (bf16[1,64,256]{2,1,0:T(8,128)(2,1)S(1)}, bf16[1,64,256]{2,1,0:T(8,128)(2,1)S(1)}, u32[]{:S(2)}, u32[]{:S(2)}) collective-permute-start(bf16[1,64,256]{2,1,0:T(8,128)(2,1)S(1)} %get-tuple-element.31), channel_id=1, source_target_pairs={{0,24},{8,0},{16,8},{24,16},{1,25},{9,1},{17,9},{25,17},{2,26},{10... | collective-permute-start | bytes 98312 | tf_op jit(solution)/shard_map/ppermute | solution.py:30
  34.6 5.8 %collective-permute-start.21 = (bf16[64,256]{1,0:T(8,128)(2,1)S(1)}, bf16[64,256]{1,0:T(8,128)(2,1)S(1)}, u32[]{:S(2)}, u32[]{:S(2)}) collective-permute-start(bf16[64,256]{1,0:T(8,128)(2,1)S(1)} %get-tuple-element.36), channel_id=1, source_target_pairs={{0,2},{1,3},{2,4},{3,5},{4,6},{5,7},{6,0},{7,1},{8,10},{9,11},{10,... | collective-permute-start | bytes 98312 | tf_op jit(solution)/shard_map/ppermute | solution.py:30
  34.8 6.3 %collective-permute-start.22 = (bf16[64,256]{1,0:T(8,128)(2,1)S(1)}, bf16[64,256]{1,0:T(8,128)(2,1)S(1)}, u32[]{:S(2)}, u32[]{:S(2)}) collective-permute-start(bf16[64,256]{1,0:T(8,128)(2,1)S(1)} %get-tuple-element.37), channel_id=1, source_target_pairs={{0,4},{1,5},{2,6},{3,7},{4,0},{5,1},{6,2},{7,3},{8,12},{9,13},{10,... | collective-permute-start | bytes 98312 | tf_op jit(solution)/shard_map/ppermute | solution.py:30
  38.8 3.9 %collective-permute-start.23 = (bf16[64,256]{1,0:T(8,128)(2,1)S(1)}, bf16[64,256]{1,0:T(8,128)(2,1)S(1)}, u32[]{:S(2)}, u32[]{:S(2)}) collective-permute-start(bf16[64,256]{1,0:T(8,128)(2,1)S(1)} %get-tuple-element.38), channel_id=1, source_target_pairs={{0,6},{1,7},{2,0},{3,1},{4,2},{5,3},{6,4},{7,5},{8,14},{9,15},{10,... | collective-permute-start | bytes 98312 | tf_op jit(solution)/shard_map/ppermute | solution.py:30
  (6 other events, 104.5 us)

commit v5 on v4

--- a/solution.py
+++ b/solution.py
@@ -100,12 +100,6 @@
 
 def clear(acc):
     acc[...] = jnp.zeros_like(acc)
-
-
-def take_rows(own, part):
-    half = part.shape[1]
-    start = lax.rem(lax.axis_index("mpo"), 2) * half
-    part[...] = own[:, pl.ds(pl.multiple_of(start, half), half)]
 
 
 def products(ids, blocks, left, right, acc, *stage):
@@ -210,7 +204,10 @@
         return (row_ids < left_dims[:, None, None]) & (col_ids < right_dims[:, None, None])
 
     own = jnp.where(live(wavefunction.shape, 0), wavefunction, jnp.zeros_like(wavefunction))
-    part = call(take_rows, array((1, rows // 2, cols), BF16), (own,))
+    half = rows // 2
+    start = lax.rem(group, 2) * half
+    part = lax.dynamic_slice_in_dim(wavefunction, start, half, axis=1)
+    part = jnp.where(live(part.shape, start), part, jnp.zeros_like(part))
     assert groups % 2 == 0 and 2 * (depth - len(DIRECT)) % groups == 0
     rounds = 2 * (depth - len(DIRECT)) // groups
     far = [fetch_far(part, n) for n in range(rounds)]

time: 43.6 us -> 43.4 us (level)
  starting transfers between devices: 24.3 us -> 22.9 us
  other arithmetic: 1.66 us -> 2.74 us
    ppermute x23, starting transfers between devices: 20.1 us -> 18.8 us  [send(): lax.ppermute(value, axis, [(i, target(i)) for i in range(lax.axis_size(ax...]
    ppermute x23, waiting for transfers between devices: 10.5 us -> 11.7 us  [send(): lax.ppermute(value, axis, [(i, target(i)) for i in range(lax.axis_size(ax...]
    ppermute x1, waiting for transfers between devices: 1.47 us -> 0.45 us  [fetch_far(): lax.ppermute(value, ('mpo', 'sec'), [(i, target(i)) for i in range(groups...]
    select_n x0 -> x1, other arithmetic: none -> 0.93 us  [device_step(): part = jnp.where(live(part.shape, start), part, jnp.zeros_like(part))]
    pallas_call x8 -> x7, Pallas kernels: 4.03 us -> 4.01 us  [call(): results = run(*operands)]
  transfers between devices with their start and end apart: 24 -> 24, of which waited for: 13 -> 14; matrix products, arithmetic and copies ran while one was open for 0% -> 3% of each run, Pallas kernels for 1% -> 1%
where the time goes in v5:
time: 43.4 us; the launch traced here: 43.3 us
  starting transfers between devices  22.9 us (53%)
  waiting for transfers between devices  12.1 us (28%)
  Pallas kernels  4.01 us (9%)
  other arithmetic  2.74 us (6%)
  between operations  1.47 us (3%)
    ppermute x23, starting transfers between devices, send(): lax.ppermute(value, axis, [(i, target(i)) for i in range(lax.axis_size(ax...  18.8 us
    ppermute x23, waiting for transfers between devices, send(): lax.ppermute(value, axis, [(i, target(i)) for i in range(lax.axis_size(ax...  11.7 us
    ppermute x1, starting transfers between devices, fetch_far(): lax.ppermute(value, ('mpo', 'sec'), [(i, target(i)) for i in range(groups...  4.13 us
    pallas_call x7, Pallas kernels, call(): results = run(*operands)  4.01 us
    select_n x1, other arithmetic, device_step(): jnp.where(live(wavefunction.shape, 0), wavefunction, jnp.zeros_like(wavef...  1.1 us
    select_n x1, other arithmetic, device_step(): part = jnp.where(live(part.shape, start), part, jnp.zeros_like(part))  0.93 us
  transfers between devices with their start and end apart: 24, of which 14 were waited for; matrix products, arithmetic and copies ran while one was open for 3% of the time, Pallas kernels for 1%

profile of v5, /device:TPU:0, one launch (start us, length us, event | category | flops | bytes accessed | tf_op | source)
XLA Modules:
  0.0 43.3 jit_solution(13323814128126436602)
XLA Ops:
  1.3 0.9 %fusion.3 = bf16[1,128,256]{2,1,0:T(8,128)(2,1)S(1)} fusion(bf16[1,256,256]{2,1,0:T(8,128)(2,1)} %param.7, s32[]{:T(128)S(6)} %select_n.17, s32[]{:T(128)} %bitcast.11, pred[128]{0:T(512)(128)(4,1)S(1)} %add_compare_fusion), kind=kLoop, calls=%fused_computation.6 | loop fusion | flops 98304 | bytes 131208 | tf_op jit(solution)/shard_map/jit(_where)/select_n | solution.py:210
  2.3 4.1 %collective-permute-start.3 = (bf16[1,128,256]{2,1,0:T(8,128)(2,1)S(1)}, bf16[1,128,256]{2,1,0:T(8,128)(2,1)S(1)}, u32[]{:S(2)}, u32[]{:S(2)}) collective-permute-start(bf16[1,128,256]{2,1,0:T(8,128)(2,1)S(1)} %fusion.3), channel_id=1, source_target_pairs={{0,4},{1,5},{2,6},{3,7},{4,0},{5,1},{6,2},{7,3},{8,12},{9,13},{10,... | collective-permute-start | bytes 196616 | tf_op jit(solution)/shard_map/ppermute | solution.py:55
  6.4 1.1 %fusion.1.refs_0_ = bf16[1,256,256]{2,1,0:T(8,128)(2,1)S(1)} fusion(bf16[1,256,256]{2,1,0:T(8,128)(2,1)} %param.7, s32[]{:T(128)} %bitcast.10, s32[]{:T(128)} %bitcast.7), kind=kLoop, calls=%fused_computation.3 | loop fusion | flops 262144 | bytes 262152 | tf_op jit(solution)/shard_map/jit(_where)/select_n | solution.py:206
  7.5 1.6 %collective-permute-start.1 = (bf16[1,256,256]{2,1,0:T(8,128)(2,1)S(1)}, bf16[1,256,256]{2,1,0:T(8,128)(2,1)S(1)}, u32[]{:S(2)}, u32[]{:S(2)}) collective-permute-start(bf16[1,256,256]{2,1,0:T(8,128)(2,1)S(1)} %fusion.1.refs_0_), channel_id=1, source_target_pairs={{0,2},{1,3},{2,0},{3,1},{4,6},{5,7},{6,4},{7,5},{8,10},{9,11},{10,... | collective-permute-start | bytes 393224 | tf_op jit(solution)/shard_map/ppermute | solution.py:30
  9.6 2.9 %collective-permute-start.9 = (bf16[1,128,256]{2,1,0:T(8,128)(2,1)S(1)}, bf16[1,128,256]{2,1,0:T(8,128)(2,1)S(1)}, u32[]{:S(2)}, u32[]{:S(2)}) collective-permute-start(bf16[1,128,256]{2,1,0:T(8,128)(2,1)S(1)} %collective-permute-done.3.refs_4_), channel_id=1, source_target_pairs={{0,24},{8,0},{16,8},{24,16},{1,25},{9,1},{17,9},{25,17},{2,26},{10... | collective-permute-start | bytes 196616 | tf_op jit(solution)/shard_map/ppermute | solution.py:30
  13.0 0.6 %collective-permute-start.5 = (bf16[1,128,256]{2,1,0:T(8,128)(2,1)S(1)}, bf16[1,128,256]{2,1,0:T(8,128)(2,1)S(1)}, u32[]{:S(2)}, u32[]{:S(2)}) collective-permute-start(bf16[1,128,256]{2,1,0:T(8,128)(2,1)S(1)} %collective-permute-done.3.refs_4_), channel_id=1, source_target_pairs={{0,8},{8,16},{16,24},{24,0},{1,9},{9,17},{17,25},{25,1},{2,10},{10... | collective-permute-start | bytes 196616 | tf_op jit(solution)/shard_map/ppermute | solution.py:30
  13.8 0.7 %collective-permute-done.9.refs_10_ = bf16[1,128,256]{2,1,0:T(8,128)(2,1)S(1)} collective-permute-done((bf16[1,128,256]{2,1,0:T(8,128)(2,1)S(1)}, bf16[1,128,256]{2,1,0:T(8,128)(2,1)S(1)}, u32[]{:S(2)}, u32[]{:S(2)}) %collective-permute-start.9) | collective-permute-done | bytes 65568 | tf_op jit(solution)/shard_map/ppermute | solution.py:30
  14.4 2.4 %collective-permute-done.7.refs_8_ = bf16[1,128,256]{2,1,0:T(8,128)(2,1)S(1)} collective-permute-done((bf16[1,128,256]{2,1,0:T(8,128)(2,1)S(1)}, bf16[1,128,256]{2,1,0:T(8,128)(2,1)S(1)}, u32[]{:S(2)}, u32[]{:S(2)}) %collective-permute-start.7) | collective-permute-done | bytes 65568 | tf_op jit(solution)/shard_map/ppermute | solution.py:30
  16.8 1.4 %collective-permute-done.5.refs_6_ = bf16[1,128,256]{2,1,0:T(8,128)(2,1)S(1)} collective-permute-done((bf16[1,128,256]{2,1,0:T(8,128)(2,1)S(1)}, bf16[1,128,256]{2,1,0:T(8,128)(2,1)S(1)}, u32[]{:S(2)}, u32[]{:S(2)}) %collective-permute-start.5) | collective-permute-done | bytes 65568 | tf_op jit(solution)/shard_map/ppermute | solution.py:30
  18.2 0.5 %collective-permute-start.6 = (bf16[1,128,256]{2,1,0:T(8,128)(2,1)S(1)}, bf16[1,128,256]{2,1,0:T(8,128)(2,1)S(1)}, u32[]{:S(2)}, u32[]{:S(2)}) collective-permute-start(bf16[1,128,256]{2,1,0:T(8,128)(2,1)S(1)} %collective-permute-done.5.refs_6_), channel_id=1, source_target_pairs={{0,1},{1,0},{2,3},{3,2},{4,5},{5,4},{6,7},{7,6},{8,9},{9,8},{10,11... | collective-permute-start | bytes 196616 | tf_op jit(solution)/shard_map/ppermute | solution.py:30
  18.8 0.6 %collective-permute-done.8.refs_9_ = bf16[1,128,256]{2,1,0:T(8,128)(2,1)S(1)} collective-permute-done((bf16[1,128,256]{2,1,0:T(8,128)(2,1)S(1)}, bf16[1,128,256]{2,1,0:T(8,128)(2,1)S(1)}, u32[]{:S(2)}, u32[]{:S(2)}) %collective-permute-start.8) | collective-permute-done | bytes 65568 | tf_op jit(solution)/shard_map/ppermute | solution.py:30
  20.1 3.7 %shard_map.74 = (f32[8,256,256]{2,1,0:T(8,128)S(1)}, bf16[4,64,256]{2,1,0:T(8,128)(2,1)S(1)}, bf16[4,64,256]{2,1,0:T(8,128)(2,1)S(1)}, bf16[4,64,256]{2,1,0:T(8,...) custom-call(f32[1,40]{1,0:T(1,128)S(1)} %convert_bitcast_fusion.ids,, ...), custom_call_target="tpu_custom_call", output_to_operand_aliasing={{0}: (15, {})} | custom-call | flops 2684354560 | bytes 10485760 | tf_op jit(solution)/shard_map/pallas_call | solution.py:97
  25.4 1.6 %collective-permute-start.19 = (bf16[3,64,256]{2,1,0:T(8,128)(2,1)S(1)}, bf16[3,64,256]{2,1,0:T(8,128)(2,1)S(1)}, u32[]{:S(2)}, u32[]{:S(2)}) collective-permute-start(bf16[3,64,256]{2,1,0:T(8,128)(2,1)S(1)} %get-tuple-element.34), channel_id=1, source_target_pairs={{0,16},{8,24},{16,0},{24,8},{1,17},{9,25},{17,1},{25,9},{2,18},{10... | collective-permute-start | bytes 294920 | tf_op jit(solution)/shard_map/ppermute | solution.py:30
  27.1 2.9 %collective-permute-start.20 = (bf16[3,64,256]{2,1,0:T(8,128)(2,1)S(1)}, bf16[3,64,256]{2,1,0:T(8,128)(2,1)S(1)}, u32[]{:S(2)}, u32[]{:S(2)}) collective-permute-start(bf16[3,64,256]{2,1,0:T(8,128)(2,1)S(1)} %get-tuple-element.35), channel_id=1, source_target_pairs={{0,24},{8,0},{16,8},{24,16},{1,25},{9,1},{17,9},{25,17},{2,26},{10... | collective-permute-start | bytes 294920 | tf_op jit(solution)/shard_map/ppermute | solution.py:30
  29.9 0.6 %collective-permute-start.14 = (bf16[1,64,256]{2,1,0:T(8,128)(2,1)S(1)}, bf16[1,64,256]{2,1,0:T(8,128)(2,1)S(1)}, u32[]{:S(2)}, u32[]{:S(2)}) collective-permute-start(bf16[1,64,256]{2,1,0:T(8,128)(2,1)S(1)} %get-tuple-element.28), channel_id=1, source_target_pairs={{0,16},{8,24},{16,0},{24,8},{1,17},{9,25},{17,1},{25,9},{2,18},{10... | collective-permute-start | bytes 98312 | tf_op jit(solution)/shard_map/ppermute | solution.py:30
  30.6 1.2 %collective-permute-done.18.refs_2_ = bf16[3,64,256]{2,1,0:T(8,128)(2,1)S(1)} collective-permute-done((bf16[3,64,256]{2,1,0:T(8,128)(2,1)S(1)}, bf16[3,64,256]{2,1,0:T(8,128)(2,1)S(1)}, u32[]{:S(2)}, u32[]{:S(2)}) %collective-permute-start.18) | collective-permute-done | bytes 98336 | tf_op jit(solution)/shard_map/ppermute | solution.py:30
  31.8 1.6 %collective-permute-start.16 = (bf16[1,64,256]{2,1,0:T(8,128)(2,1)S(1)}, bf16[1,64,256]{2,1,0:T(8,128)(2,1)S(1)}, u32[]{:S(2)}, u32[]{:S(2)}) collective-permute-start(bf16[1,64,256]{2,1,0:T(8,128)(2,1)S(1)} %get-tuple-element.31), channel_id=1, source_target_pairs={{0,24},{8,0},{16,8},{24,16},{1,25},{9,1},{17,9},{25,17},{2,26},{10... | collective-permute-start | bytes 98312 | tf_op jit(solution)/shard_map/ppermute | solution.py:30
  33.4 0.6 %collective-permute-done.20.refs_4_ = bf16[3,64,256]{2,1,0:T(8,128)(2,1)S(1)} collective-permute-done((bf16[3,64,256]{2,1,0:T(8,128)(2,1)S(1)}, bf16[3,64,256]{2,1,0:T(8,128)(2,1)S(1)}, u32[]{:S(2)}, u32[]{:S(2)}) %collective-permute-start.20) | collective-permute-done | bytes 98336 | tf_op jit(solution)/shard_map/ppermute | solution.py:30
  34.0 0.7 %collective-permute-start.21 = (bf16[64,256]{1,0:T(8,128)(2,1)S(1)}, bf16[64,256]{1,0:T(8,128)(2,1)S(1)}, u32[]{:S(2)}, u32[]{:S(2)}) collective-permute-start(bf16[64,256]{1,0:T(8,128)(2,1)S(1)} %get-tuple-element.36), channel_id=1, source_target_pairs={{0,2},{1,3},{2,4},{3,5},{4,6},{5,7},{6,0},{7,1},{8,10},{9,11},{10,... | collective-permute-start | bytes 98312 | tf_op jit(solution)/shard_map/ppermute | solution.py:30
  34.8 3.9 %collective-permute-start.22 = (bf16[64,256]{1,0:T(8,128)(2,1)S(1)}, bf16[64,256]{1,0:T(8,128)(2,1)S(1)}, u32[]{:S(2)}, u32[]{:S(2)}) collective-permute-start(bf16[64,256]{1,0:T(8,128)(2,1)S(1)} %get-tuple-element.37), channel_id=1, source_target_pairs={{0,4},{1,5},{2,6},{3,7},{4,0},{5,1},{6,2},{7,3},{8,12},{9,13},{10,... | collective-permute-start | bytes 98312 | tf_op jit(solution)/shard_map/ppermute | solution.py:30
  38.8 1.2 %collective-permute-done.21 = bf16[64,256]{1,0:T(8,128)(2,1)S(1)} collective-permute-done((bf16[64,256]{1,0:T(8,128)(2,1)S(1)}, bf16[64,256]{1,0:T(8,128)(2,1)S(1)}, u32[]{:S(2)}, u32[]{:S(2)}) %collective-permute-start.21) | collective-permute-done | bytes 32800 | tf_op jit(solution)/shard_map/ppermute | solution.py:30
  40.0 0.7 %collective-permute-done.22 = bf16[64,256]{1,0:T(8,128)(2,1)S(1)} collective-permute-done((bf16[64,256]{1,0:T(8,128)(2,1)S(1)}, bf16[64,256]{1,0:T(8,128)(2,1)S(1)}, u32[]{:S(2)}, u32[]{:S(2)}) %collective-permute-start.22) | collective-permute-done | bytes 32800 | tf_op jit(solution)/shard_map/ppermute | solution.py:30
  40.7 1.9 %collective-permute-done.23 = bf16[64,256]{1,0:T(8,128)(2,1)S(1)} collective-permute-done((bf16[64,256]{1,0:T(8,128)(2,1)S(1)}, bf16[64,256]{1,0:T(8,128)(2,1)S(1)}, u32[]{:S(2)}, u32[]{:S(2)}) %collective-permute-start.23) | collective-permute-done | bytes 32800 | tf_op jit(solution)/shard_map/ppermute | solution.py:30
  42.6 0.7 %fusion.5 = bf16[1,64,256]{2,1,0:T(8,128)(2,1)} fusion(bf16[64,256]{1,0:T(8,128)(2,1)S(1)} %collective-permute-done.23, bf16[64,256]{1,0:T(8,128)(2,1)S(1)} %collective-permute-done.22, f32[64,256]{1,0:T(8,128)S(1)} %shard_map.78, bf16[64,256]{1,0:T(8,128)(2,1)S(1)} %collective-permute-done.21, s32[]{:T(128)} %bitcast.9, pred[64]{0:T(512)(128)(4,1)S(1)} %add_compare_fusion.1), kind=kLoop, calls=%fused_computation.10 | loop fusion | flops 163840 | bytes 196676 | tf_op jit(solution)/shard_map/convert_element_type | solution.py:263
  (51 shorter events, 3.7 us)
Async XLA Ops:
  2.3 7.4 %collective-permute-start.3 = (bf16[1,128,256]{2,1,0:T(8,128)(2,1)S(1)}, bf16[1,128,256]{2,1,0:T(8,128)(2,1)S(1)}, u32[]{:S(2)}, u32[]{:S(2)}) collective-permute-start(bf16[1,128,256]{2,1,0:T(8,128)(2,1)S(1)} %fusion.3), channel_id=1, source_target_pairs={{0,4},{1,5},{2,6},{3,7},{4,0},{5,1},{6,2},{7,3},{8,12},{9,13},{10,... | collective-permute-start | bytes 196616 | tf_op jit(solution)/shard_map/ppermute | solution.py:55
  7.5 11.2 %collective-permute-start.1 = (bf16[1,256,256]{2,1,0:T(8,128)(2,1)S(1)}, bf16[1,256,256]{2,1,0:T(8,128)(2,1)S(1)}, u32[]{:S(2)}, u32[]{:S(2)}) collective-permute-start(bf16[1,256,256]{2,1,0:T(8,128)(2,1)S(1)} %fusion.1.refs_0_), channel_id=1, source_target_pairs={{0,2},{1,3},{2,0},{3,1},{4,6},{5,7},{6,4},{7,5},{8,10},{9,11},{10,... | collective-permute-start | bytes 393224 | tf_op jit(solution)/shard_map/ppermute | solution.py:30
  9.6 4.8 %collective-permute-start.9 = (bf16[1,128,256]{2,1,0:T(8,128)(2,1)S(1)}, bf16[1,128,256]{2,1,0:T(8,128)(2,1)S(1)}, u32[]{:S(2)}, u32[]{:S(2)}) collective-permute-start(bf16[1,128,256]{2,1,0:T(8,128)(2,1)S(1)} %collective-permute-done.3.refs_4_), channel_id=1, source_target_pairs={{0,24},{8,0},{16,8},{24,16},{1,25},{9,1},{17,9},{25,17},{2,26},{10... | collective-permute-start | bytes 196616 | tf_op jit(solution)/shard_map/ppermute | solution.py:30
  12.5 4.3 %collective-permute-start.7 = (bf16[1,128,256]{2,1,0:T(8,128)(2,1)S(1)}, bf16[1,128,256]{2,1,0:T(8,128)(2,1)S(1)}, u32[]{:S(2)}, u32[]{:S(2)}) collective-permute-start(bf16[1,128,256]{2,1,0:T(8,128)(2,1)S(1)} %collective-permute-done.3.refs_4_), channel_id=1, source_target_pairs={{0,16},{8,24},{16,0},{24,8},{1,17},{9,25},{17,1},{25,9},{2,18},{10... | collective-permute-start | bytes 196616 | tf_op jit(solution)/shard_map/ppermute | solution.py:30
  13.0 5.2 %collective-permute-start.5 = (bf16[1,128,256]{2,1,0:T(8,128)(2,1)S(1)}, bf16[1,128,256]{2,1,0:T(8,128)(2,1)S(1)}, u32[]{:S(2)}, u32[]{:S(2)}) collective-permute-start(bf16[1,128,256]{2,1,0:T(8,128)(2,1)S(1)} %collective-permute-done.3.refs_4_), channel_id=1, source_target_pairs={{0,8},{8,16},{16,24},{24,0},{1,9},{9,17},{17,25},{25,1},{2,10},{10... | collective-permute-start | bytes 196616 | tf_op jit(solution)/shard_map/ppermute | solution.py:30
  13.6 4.6 %collective-permute-start.4 = (bf16[1,128,256]{2,1,0:T(8,128)(2,1)S(1)}, bf16[1,128,256]{2,1,0:T(8,128)(2,1)S(1)}, u32[]{:S(2)}, u32[]{:S(2)}) collective-permute-start(bf16[1,128,256]{2,1,0:T(8,128)(2,1)S(1)} %collective-permute-done.3.refs_4_), channel_id=1, source_target_pairs={{0,1},{1,0},{2,3},{3,2},{4,5},{5,4},{6,7},{7,6},{8,9},{9,8},{10,11... | collective-permute-start | bytes 196616 | tf_op jit(solution)/shard_map/ppermute | solution.py:30
  14.4 4.4 %collective-permute-start = (bf16[1,256,256]{2,1,0:T(8,128)(2,1)S(1)}, bf16[1,256,256]{2,1,0:T(8,128)(2,1)S(1)}, u32[]{:S(2)}, u32[]{:S(2)}) collective-permute-start(bf16[1,256,256]{2,1,0:T(8,128)(2,1)S(1)} %fusion.1.refs_0_), channel_id=1, source_target_pairs={{0,1},{1,0},{2,3},{3,2},{4,5},{5,4},{6,7},{7,6},{8,9},{9,8},{10,11... | collective-permute-start | bytes 393224 | tf_op jit(solution)/shard_map/ppermute | solution.py:30
  16.8 2.0 %collective-permute-start.10 = (bf16[1,128,256]{2,1,0:T(8,128)(2,1)S(1)}, bf16[1,128,256]{2,1,0:T(8,128)(2,1)S(1)}, u32[]{:S(2)}, u32[]{:S(2)}) collective-permute-start(bf16[1,128,256]{2,1,0:T(8,128)(2,1)S(1)} %collective-permute-done.9.refs_10_), channel_id=1, source_target_pairs={{0,1},{1,0},{2,3},{3,2},{4,5},{5,4},{6,7},{7,6},{8,9},{9,8},{10,11... | collective-permute-start | bytes 196616 | tf_op jit(solution)/shard_map/ppermute | solution.py:30
  18.2 1.3 %collective-permute-start.8 = (bf16[1,128,256]{2,1,0:T(8,128)(2,1)S(1)}, bf16[1,128,256]{2,1,0:T(8,128)(2,1)S(1)}, u32[]{:S(2)}, u32[]{:S(2)}) collective-permute-start(bf16[1,128,256]{2,1,0:T(8,128)(2,1)S(1)} %collective-permute-done.7.refs_8_), channel_id=1, source_target_pairs={{0,1},{1,0},{2,3},{3,2},{4,5},{5,4},{6,7},{7,6},{8,9},{9,8},{10,11... | collective-permute-start | bytes 196616 | tf_op jit(solution)/shard_map/ppermute | solution.py:30
  18.2 1.4 %collective-permute-start.6 = (bf16[1,128,256]{2,1,0:T(8,128)(2,1)S(1)}, bf16[1,128,256]{2,1,0:T(8,128)(2,1)S(1)}, u32[]{:S(2)}, u32[]{:S(2)}) collective-permute-start(bf16[1,128,256]{2,1,0:T(8,128)(2,1)S(1)} %collective-permute-done.5.refs_6_), channel_id=1, source_target_pairs={{0,1},{1,0},{2,3},{3,2},{4,5},{5,4},{6,7},{7,6},{8,9},{9,8},{10,11... | collective-permute-start | bytes 196616 | tf_op jit(solution)/shard_map/ppermute | solution.py:30
  18.7 1.3 %collective-permute-start.2 = (bf16[1,256,256]{2,1,0:T(8,128)(2,1)S(1)}, bf16[1,256,256]{2,1,0:T(8,128)(2,1)S(1)}, u32[]{:S(2)}, u32[]{:S(2)}) collective-permute-start(bf16[1,256,256]{2,1,0:T(8,128)(2,1)S(1)} %collective-permute-done.1.refs_2_), channel_id=1, source_target_pairs={{0,1},{1,0},{2,3},{3,2},{4,5},{5,4},{6,7},{7,6},{8,9},{9,8},{10,11... | collective-permute-start | bytes 393224 | tf_op jit(solution)/shard_map/ppermute | solution.py:30
  23.8 1.4 %collective-permute-start.11 = (bf16[4,64,256]{2,1,0:T(8,128)(2,1)S(1)}, bf16[4,64,256]{2,1,0:T(8,128)(2,1)S(1)}, u32[]{:S(2)}, u32[]{:S(2)}) collective-permute-start(bf16[4,64,256]{2,1,0:T(8,128)(2,1)S(1)} %get-tuple-element.24), channel_id=1, source_target_pairs={{0,1},{1,0},{2,3},{3,2},{4,5},{5,4},{6,7},{7,6},{8,9},{9,8},{10,11... | collective-permute-start | bytes 393224 | tf_op jit(solution)/shard_map/ppermute | solution.py:30
  24.0 1.4 %collective-permute-start.13 = (bf16[4,64,256]{2,1,0:T(8,128)(2,1)S(1)}, bf16[4,64,256]{2,1,0:T(8,128)(2,1)S(1)}, u32[]{:S(2)}, u32[]{:S(2)}) collective-permute-start(bf16[4,64,256]{2,1,0:T(8,128)(2,1)S(1)} %get-tuple-element.27), channel_id=1, source_target_pairs={{0,1},{1,0},{2,3},{3,2},{4,5},{5,4},{6,7},{7,6},{8,9},{9,8},{10,11... | collective-permute-start | bytes 393224 | tf_op jit(solution)/shard_map/ppermute | solution.py:30
  24.4 2.7 %collective-permute-start.15 = (bf16[4,64,256]{2,1,0:T(8,128)(2,1)S(1)}, bf16[4,64,256]{2,1,0:T(8,128)(2,1)S(1)}, u32[]{:S(2)}, u32[]{:S(2)}) collective-permute-start(bf16[4,64,256]{2,1,0:T(8,128)(2,1)S(1)} %get-tuple-element.30), channel_id=1, source_target_pairs={{0,1},{1,0},{2,3},{3,2},{4,5},{5,4},{6,7},{7,6},{8,9},{9,8},{10,11... | collective-permute-start | bytes 393224 | tf_op jit(solution)/shard_map/ppermute | solution.py:30
  24.5 5.4 %collective-permute-start.17 = (bf16[4,64,256]{2,1,0:T(8,128)(2,1)S(1)}, bf16[4,64,256]{2,1,0:T(8,128)(2,1)S(1)}, u32[]{:S(2)}, u32[]{:S(2)}) collective-permute-start(bf16[4,64,256]{2,1,0:T(8,128)(2,1)S(1)} %get-tuple-element.32), channel_id=1, source_target_pairs={{0,1},{1,0},{2,3},{3,2},{4,5},{5,4},{6,7},{7,6},{8,9},{9,8},{10,11... | collective-permute-start | bytes 393224 | tf_op jit(solution)/shard_map/ppermute | solution.py:30
  25.2 6.6 %collective-permute-start.18 = (bf16[3,64,256]{2,1,0:T(8,128)(2,1)S(1)}, bf16[3,64,256]{2,1,0:T(8,128)(2,1)S(1)}, u32[]{:S(2)}, u32[]{:S(2)}) collective-permute-start(bf16[3,64,256]{2,1,0:T(8,128)(2,1)S(1)} %get-tuple-element.33), channel_id=1, source_target_pairs={{0,8},{8,16},{16,24},{24,0},{1,9},{9,17},{17,25},{25,1},{2,10},{10... | collective-permute-start | bytes 294920 | tf_op jit(solution)/shard_map/ppermute | solution.py:30
  25.4 7.9 %collective-permute-start.19 = (bf16[3,64,256]{2,1,0:T(8,128)(2,1)S(1)}, bf16[3,64,256]{2,1,0:T(8,128)(2,1)S(1)}, u32[]{:S(2)}, u32[]{:S(2)}) collective-permute-start(bf16[3,64,256]{2,1,0:T(8,128)(2,1)S(1)} %get-tuple-element.34), channel_id=1, source_target_pairs={{0,16},{8,24},{16,0},{24,8},{1,17},{9,25},{17,1},{25,9},{2,18},{10... | collective-permute-start | bytes 294920 | tf_op jit(solution)/shard_map/ppermute | solution.py:30
  27.1 6.9 %collective-permute-start.20 = (bf16[3,64,256]{2,1,0:T(8,128)(2,1)S(1)}, bf16[3,64,256]{2,1,0:T(8,128)(2,1)S(1)}, u32[]{:S(2)}, u32[]{:S(2)}) collective-permute-start(bf16[3,64,256]{2,1,0:T(8,128)(2,1)S(1)} %get-tuple-element.35), channel_id=1, source_target_pairs={{0,24},{8,0},{16,8},{24,16},{1,25},{9,1},{17,9},{25,17},{2,26},{10... | collective-permute-start | bytes 294920 | tf_op jit(solution)/shard_map/ppermute | solution.py:30
  29.9 8.7 %collective-permute-start.12 = (bf16[1,64,256]{2,1,0:T(8,128)(2,1)S(1)}, bf16[1,64,256]{2,1,0:T(8,128)(2,1)S(1)}, u32[]{:S(2)}, u32[]{:S(2)}) collective-permute-start(bf16[1,64,256]{2,1,0:T(8,128)(2,1)S(1)} %get-tuple-element.25), channel_id=1, source_target_pairs={{0,8},{8,16},{16,24},{24,0},{1,9},{9,17},{17,25},{25,1},{2,10},{10... | collective-permute-start | bytes 98312 | tf_op jit(solution)/shard_map/ppermute | solution.py:30
  29.9 8.8 %collective-permute-start.14 = (bf16[1,64,256]{2,1,0:T(8,128)(2,1)S(1)}, bf16[1,64,256]{2,1,0:T(8,128)(2,1)S(1)}, u32[]{:S(2)}, u32[]{:S(2)}) collective-permute-start(bf16[1,64,256]{2,1,0:T(8,128)(2,1)S(1)} %get-tuple-element.28), channel_id=1, source_target_pairs={{0,16},{8,24},{16,0},{24,8},{1,17},{9,25},{17,1},{25,9},{2,18},{10... | collective-permute-start | bytes 98312 | tf_op jit(solution)/shard_map/ppermute | solution.py:30
  31.8 7.0 %collective-permute-start.16 = (bf16[1,64,256]{2,1,0:T(8,128)(2,1)S(1)}, bf16[1,64,256]{2,1,0:T(8,128)(2,1)S(1)}, u32[]{:S(2)}, u32[]{:S(2)}) collective-permute-start(bf16[1,64,256]{2,1,0:T(8,128)(2,1)S(1)} %get-tuple-element.31), channel_id=1, source_target_pairs={{0,24},{8,0},{16,8},{24,16},{1,25},{9,1},{17,9},{25,17},{2,26},{10... | collective-permute-start | bytes 98312 | tf_op jit(solution)/shard_map/ppermute | solution.py:30
  34.0 5.9 %collective-permute-start.21 = (bf16[64,256]{1,0:T(8,128)(2,1)S(1)}, bf16[64,256]{1,0:T(8,128)(2,1)S(1)}, u32[]{:S(2)}, u32[]{:S(2)}) collective-permute-start(bf16[64,256]{1,0:T(8,128)(2,1)S(1)} %get-tuple-element.36), channel_id=1, source_target_pairs={{0,2},{1,3},{2,4},{3,5},{4,6},{5,7},{6,0},{7,1},{8,10},{9,11},{10,... | collective-permute-start | bytes 98312 | tf_op jit(solution)/shard_map/ppermute | solution.py:30
  34.8 5.9 %collective-permute-start.22 = (bf16[64,256]{1,0:T(8,128)(2,1)S(1)}, bf16[64,256]{1,0:T(8,128)(2,1)S(1)}, u32[]{:S(2)}, u32[]{:S(2)}) collective-permute-start(bf16[64,256]{1,0:T(8,128)(2,1)S(1)} %get-tuple-element.37), channel_id=1, source_target_pairs={{0,4},{1,5},{2,6},{3,7},{4,0},{5,1},{6,2},{7,3},{8,12},{9,13},{10,... | collective-permute-start | bytes 98312 | tf_op jit(solution)/shard_map/ppermute | solution.py:30
  38.6 3.9 %collective-permute-start.23 = (bf16[64,256]{1,0:T(8,128)(2,1)S(1)}, bf16[64,256]{1,0:T(8,128)(2,1)S(1)}, u32[]{:S(2)}, u32[]{:S(2)}) collective-permute-start(bf16[64,256]{1,0:T(8,128)(2,1)S(1)} %get-tuple-element.38), channel_id=1, source_target_pairs={{0,6},{1,7},{2,0},{3,1},{4,2},{5,3},{6,4},{7,5},{8,14},{9,15},{10,... | collective-permute-start | bytes 98312 | tf_op jit(solution)/shard_map/ppermute | solution.py:30
  (6 other events, 75.0 us)
